TPU v7x, 32 devices: a whole 2x2x4 slice. The times are simulated.
32 devices in a mesh: dp: 8 (over z, y), mp: 4 (over x, core).
Axes of the slice: x: 2, y: 2, z: 4, core: 2. Of those that a mesh axis runs over, the one named last changes fastest.
Arguments:
- hidden_in: bfloat16 [8, 1024, 1280], P('dp', 'mp'), may hold values from -6 to 6
- segment_ids: int32 [8, 1024], P('dp'), may hold values from 0 to 15, never falling along the last dimension, each value on 1 to 512 neighbouring positions
- attn_gain: float32 [1280], replicated, may hold values from 0.1 to 1.9
- query_weight: bfloat16 [1280, 1280], P(None, 'mp'), may hold values from -0.15625 to 0.15625
- key_weight: bfloat16 [1280, 1280], P(None, 'mp'), may hold values from -0.15625 to 0.15625
- value_weight: bfloat16 [1280, 1280], P(None, 'mp'), may hold values from -0.15625 to 0.15625
- out_weight: bfloat16 [1280, 1280], P('mp'), may hold values from -0.625 to 0.625
- mlp_gain: float32 [1280], replicated, may hold values from 0.1 to 1.9
- up_weight: bfloat16 [1280, 5120], P(None, 'mp'), may hold values from -0.15625 to 0.15625
- down_weight: bfloat16 [5120, 1280], P('mp'), may hold values from -0.078125 to 0.078125
- out_cotangent: bfloat16 [8, 1024, 1280], P('dp', 'mp'), may hold values from -6 to 6
Outputs:
- result: bfloat16 [8, 1024, 1280], P('dp', 'mp')
- input_grad: float32 [8, 1024, 1280], P('dp', 'mp')
- attn_gain_grad: float32 [1280], replicated
- query_grad: float32 [1280, 1280], P(None, 'mp')
- key_grad: float32 [1280, 1280], P(None, 'mp')
- value_grad: float32 [1280, 1280], P(None, 'mp')
- out_grad: float32 [1280, 1280], P('mp')
- mlp_gain_grad: float32 [1280], replicated
- up_grad: float32 [1280, 5120], P(None, 'mp')
- down_grad: float32 [5120, 1280], P('mp')
Inputs may be any that keep to these rules, and one draw needn't show every extreme that they name: `segment_ids`: within each row the ids never fall; each segment is a run of 1 to 512 tokens, and one segment has exactly 512.
All inputs are finite; a program needn't handle non-finite values.
Results may differ from a plain program's by a relative error of at most 0.012.
The roundings to bfloat16 on the way count: a program that leaves them out, or rounds other values in their place, can miss the bound.
Values may be sent and summed in bfloat16 or wider, within the bound.
A program may use at most 128 MiB of HBM per device.

v0:
```python
import math

import jax
import jax.numpy as jnp
from jax import lax
from jax.sharding import PartitionSpec as P

HEAD = 80


EPS = 1e-06
MASKED = -1e30
GELU_C = math.sqrt(2.0 / math.pi)
GELU_K = 0.044715


def normalize(values, gain):
    inverse = lax.rsqrt(jnp.mean(values * values, -1, keepdims=True) + EPS)
    normed = values * inverse
    return (normed * gain, normed, inverse)


def norm_back(upstream, normed, inverse, gain):
    scaled = upstream * gain
    inner = jnp.mean(scaled * normed, -1, keepdims=True)
    return (inverse * (scaled - normed * inner), jnp.sum(upstream * normed, axis=(0, 1)))


def gelu_slope(values):
    tangent = jnp.tanh(GELU_C * (values + GELU_K * values * values * values))
    return 0.5 * (1.0 + tangent) + 0.5 * values * (1.0 - tangent * tangent) * GELU_C * (
        1.0 + 3.0 * GELU_K * values * values
    )


def project(left, weight):
    return jnp.einsum("rsd,de->rse", left, weight, preferred_element_type=jnp.float32)


def project_back(left, weight):
    return jnp.einsum("rse,de->rsd", left, weight, preferred_element_type=jnp.float32)


def weight_grad(left, right):
    return jnp.einsum("rsd,rse->de", left, right, preferred_element_type=jnp.float32)


def rotary_tables(segments, head_size):
    seq_len = segments.shape[1]
    places = jnp.arange(seq_len, dtype=jnp.int32)
    starts_here = jnp.concatenate(
        [jnp.ones((segments.shape[0], 1), bool), segments[:, 1:] != segments[:, :-1]], axis=1
    )
    first = lax.cummax(jnp.where(starts_here, places[None, :], 0), axis=1)
    position = (places[None, :] - first).astype(jnp.float32)
    half = head_size // 2
    freqs = jnp.exp(jnp.arange(half, dtype=jnp.float32) * (-2.0 * math.log(10000.0) / head_size))
    angles = position[:, :, None] * freqs[None, None, :]
    return (jnp.cos(angles)[:, :, None, :], jnp.sin(angles)[:, :, None, :])


def rotate(values, cosine, sine):
    half = values.shape[-1] // 2
    first, second = (values[..., :half], values[..., half:])
    return jnp.concatenate([first * cosine - second * sine, second * cosine + first * sine], -1)


def rotate_back(grads, cosine, sine):
    half = grads.shape[-1] // 2
    first, second = (grads[..., :half], grads[..., half:])
    return jnp.concatenate([first * cosine + second * sine, second * cosine - first * sine], -1)


def allowed_block(segments_row, start, size):
    seq_len = segments_row.shape[0]
    query_pos = start + jnp.arange(size, dtype=jnp.int32)
    key_pos = jnp.arange(seq_len, dtype=jnp.int32)
    query_seg = segments_row[start : start + size]
    return (query_pos[:, None] >= key_pos[None, :]) & (query_seg[:, None] == segments_row[None, :])


def block_scores(query_block, keys, allowed, scale):
    scores = (
        jnp.einsum("qhd,khd->hqk", query_block, keys, preferred_element_type=jnp.float32) * scale
    )
    return jnp.where(allowed[None], scores, MASKED)


def attend_forward(queries, keys, values, segments_row, scale, block):
    outputs = []
    sums = []
    for start in range(0, queries.shape[0], block):
        allowed = allowed_block(segments_row, start, block)
        scores = block_scores(queries[start : start + block], keys, allowed, scale)
        top = jnp.max(scores, -1, keepdims=True)
        expo = jnp.exp(scores - top)
        total = jnp.sum(expo, -1, keepdims=True)
        probs = (expo / total).astype(jnp.bfloat16)
        outputs.append(
            jnp.einsum("hqk,khd->qhd", probs, values, preferred_element_type=jnp.float32)
        )
        sums.append(top + jnp.log(total))
    return (jnp.concatenate(outputs, 0), jnp.concatenate(sums, 1))


def attend_back(queries, keys, values, grad_mixed, log_sums, segments_row, scale, block):
    key_total = jnp.zeros(keys.shape, jnp.float32)
    value_total = jnp.zeros(values.shape, jnp.float32)
    query_parts = []
    for start in range(0, queries.shape[0], block):
        allowed = allowed_block(segments_row, start, block)
        query_block = queries[start : start + block]
        scores = block_scores(query_block, keys, allowed, scale)
        probs = jnp.exp(scores - log_sums[:, start : start + block])
        grad_block = grad_mixed[start : start + block]
        grad_probs = jnp.einsum(
            "qhd,khd->hqk", grad_block, values, preferred_element_type=jnp.float32
        )
        inner = jnp.sum(probs * grad_probs, -1, keepdims=True)
        grad_scores = (probs * (grad_probs - inner)).astype(jnp.bfloat16)
        query_parts.append(
            jnp.einsum("hqk,khd->qhd", grad_scores, keys, preferred_element_type=jnp.float32)
            * scale
        )
        key_total = (
            key_total
            + jnp.einsum(
                "hqk,qhd->khd", grad_scores, query_block, preferred_element_type=jnp.float32
            )
            * scale
        )
        value_total = value_total + jnp.einsum(
            "hqk,qhd->khd",
            probs.astype(jnp.bfloat16),
            grad_block,
            preferred_element_type=jnp.float32,
        )
    return (jnp.concatenate(query_parts, 0), key_total, value_total)


def on_device(
    hidden_in,
    segment_ids,
    attn_gain,
    query_weight,
    key_weight,
    value_weight,
    out_weight,
    mlp_gain,
    up_weight,
    down_weight,
    out_cotangent,
):
    row_count = segment_ids.shape[0]
    seq_len = segment_ids.shape[1]
    local_width = query_weight.shape[1]
    head_count = local_width // HEAD
    scale = 1.0 / math.sqrt(HEAD)
    block = min(512, seq_len)
    head_shape = (row_count, seq_len, head_count, HEAD)
    x_float = hidden_in.astype(jnp.float32)
    scaled_one, normed_one, inverse_one = normalize(x_float, attn_gain)
    rows_one = lax.all_gather(scaled_one.astype(jnp.bfloat16), "mp", axis=1, tiled=True)
    cosine, sine = rotary_tables(segment_ids, HEAD)
    queries = rotate(project(rows_one, query_weight).reshape(head_shape), cosine, sine).astype(
        jnp.bfloat16
    )
    keys = rotate(project(rows_one, key_weight).reshape(head_shape), cosine, sine).astype(
        jnp.bfloat16
    )
    values = project(rows_one, value_weight).reshape(head_shape).astype(jnp.bfloat16)
    row_index = 0
    mixed_one, log_one = attend_forward(
        queries[row_index], keys[row_index], values[row_index], segment_ids[row_index], scale, block
    )
    mixed_rows = [mixed_one]
    log_rows = [log_one]
    mixed = jnp.stack(mixed_rows, 0).reshape(row_count, seq_len, local_width).astype(jnp.bfloat16)
    attn_share = lax.psum_scatter(project(mixed, out_weight), "mp", scatter_dimension=1, tiled=True)
    resid = x_float + attn_share
    scaled_two, normed_two, inverse_two = normalize(resid, mlp_gain)
    rows_two = lax.all_gather(scaled_two.astype(jnp.bfloat16), "mp", axis=1, tiled=True)
    up_pre = project(rows_two, up_weight)
    hidden = jax.nn.gelu(up_pre, approximate=True).astype(jnp.bfloat16)
    mlp_share = lax.psum_scatter(
        project(hidden, down_weight).astype(jnp.bfloat16), "mp", scatter_dimension=1, tiled=True
    ).astype(jnp.float32)
    result = (resid + mlp_share).astype(jnp.bfloat16)
    grad_top = out_cotangent.astype(jnp.float32)
    grad_rows = lax.all_gather(out_cotangent, "mp", axis=1, tiled=True)
    down_total = weight_grad(hidden, grad_rows)
    grad_hidden = project_back(grad_rows, down_weight)
    grad_up_pre = (grad_hidden * gelu_slope(up_pre)).astype(jnp.bfloat16)
    up_total = weight_grad(rows_two, grad_up_pre)
    grad_two = lax.psum_scatter(
        project_back(grad_up_pre, up_weight), "mp", scatter_dimension=1, tiled=True
    )
    resid_part, mlp_gain_part = norm_back(grad_two, normed_two, inverse_two, mlp_gain)
    grad_resid = grad_top + resid_part
    branch_rows = lax.all_gather(grad_resid.astype(jnp.bfloat16), "mp", axis=1, tiled=True)
    out_total = weight_grad(mixed, branch_rows)
    grad_mixed = project_back(branch_rows, out_weight).astype(jnp.bfloat16).reshape(head_shape)
    row_index = 0
    grad_q, grad_k, grad_v = attend_back(
        queries[row_index],
        keys[row_index],
        values[row_index],
        grad_mixed[row_index],
        log_rows[row_index],
        segment_ids[row_index],
        scale,
        block,
    )
    query_rows = [grad_q]
    key_rows = [grad_k]
    value_rows = [grad_v]
    grad_query = (
        rotate_back(jnp.stack(query_rows, 0), cosine, sine)
        .astype(jnp.bfloat16)
        .reshape(row_count, seq_len, local_width)
    )
    grad_key = (
        rotate_back(jnp.stack(key_rows, 0), cosine, sine)
        .astype(jnp.bfloat16)
        .reshape(row_count, seq_len, local_width)
    )
    grad_value = (
        jnp.stack(value_rows, 0).astype(jnp.bfloat16).reshape(row_count, seq_len, local_width)
    )
    query_total = weight_grad(rows_one, grad_query)
    key_total = weight_grad(rows_one, grad_key)
    value_total = weight_grad(rows_one, grad_value)
    grad_terms = (
        project_back(grad_query, query_weight)
        + project_back(grad_key, key_weight)
        + project_back(grad_value, value_weight)
    )
    grad_one = lax.psum_scatter(grad_terms, "mp", scatter_dimension=1, tiled=True)
    input_part, attn_gain_part = norm_back(grad_one, normed_one, inverse_one, attn_gain)
    input_grad = grad_resid + input_part
    attn_gain_part, mlp_gain_part = lax.psum((attn_gain_part, mlp_gain_part), "mp")
    (
        query_total,
        key_total,
        value_total,
        out_total,
        attn_gain_part,
        mlp_gain_part,
        up_total,
        down_total,
    ) = lax.psum(
        (
            query_total,
            key_total,
            value_total,
            out_total,
            attn_gain_part,
            mlp_gain_part,
            up_total,
            down_total,
        ),
        "dp",
    )
    return (
        result,
        input_grad,
        attn_gain_part,
        query_total,
        key_total,
        value_total,
        out_total,
        mlp_gain_part,
        up_total,
        down_total,
    )


def solution(mesh):
    return jax.shard_map(
        on_device,
        mesh=mesh,
        in_specs=(
            P("dp", "mp", None),
            P("dp", None),
            P(),
            P(None, "mp"),
            P(None, "mp"),
            P(None, "mp"),
            P("mp", None),
            P(),
            P(None, "mp"),
            P("mp", None),
            P("dp", "mp", None),
        ),
        out_specs=(
            P("dp", "mp", None),
            P("dp", "mp", None),
            P(),
            P(None, "mp"),
            P(None, "mp"),
            P(None, "mp"),
            P("mp", None),
            P(),
            P(None, "mp"),
            P("mp", None),
        ),
        check_vma=False,
    )
```

profile of v0, /device:TPU:0, one launch (start us, length us, event | category | flops | bytes accessed | tf_op | source)
XLA Modules:
  0.0 1015.7 jit_solution(13953661050742696063)
XLA Ops:
  15.6 24.3 %all-gather.5.cloned.1.call-done = bf16[1,1024,1280]{2,1,0:T(8,128)(2,1)} async-done(((bf16[1,256,1280]{2,1,0:T(8,128)(2,1)}), bf16[1,1024,1280]{2,1,0:T(8,128)(2,1)}) %all-gather.5.cloned.1.call-update) | async-done | bytes 2621456 | tf_op jit(solution)/shard_map/all_gather | solution.py:163
  59.0 3.9 convolution_bitcast_fusion.1
  63.2 51.2 %reduce-scatter.5.cloned.1.call-done = f32[1,256,1280]{2,1,0:T(8,128)} async-done(((f32[1,1024,1280]{2,1,0:T(8,128)}), f32[1,256,1280]{2,1,0:T(8,128)}) %reduce-scatter.5.cloned.1.call-update) | async-done | bytes 1310736 | tf_op jit(solution)/shard_map/reduce_scatter | solution.py:179
  118.9 25.1 %all-gather.7.cloned.1.call-done = bf16[1,1024,1280]{2,1,0:T(8,128)(2,1)} async-done(((bf16[1,256,1280]{2,1,0:T(8,128)(2,1)}), bf16[1,1024,1280]{2,1,0:T(8,128)(2,1)}) %all-gather.7.cloned.1.call-update) | async-done | bytes 2621456 | tf_op jit(solution)/shard_map/all_gather | solution.py:182
  144.0 7.7 fusion.37
  151.6 19.3 %all-gather.9.cloned.1.call-done = bf16[1,1024,1280]{2,1,0:T(8,128)(2,1)} async-done(((bf16[1,256,1280]{2,1,0:T(8,128)(2,1)}), bf16[1,1024,1280]{2,1,0:T(8,128)(2,1)}) %all-gather.9.cloned.1.call-update) | async-done | bytes 2621456 | tf_op jit(solution)/shard_map/all_gather | solution.py:190
  170.9 9.3 fusion.18
  181.7 5.3 convolution_bitcast_fusion
  187.1 51.5 %reduce-scatter.9.cloned.1.call-done = f32[1,256,1280]{2,1,0:T(8,128)} async-done(((f32[1,1024,1280]{2,1,0:T(8,128)}), f32[1,256,1280]{2,1,0:T(8,128)}) %reduce-scatter.9.cloned.1.call-update) | async-done | bytes 1310736 | tf_op jit(solution)/shard_map/reduce_scatter | solution.py:195
  242.2 25.2 %all-gather.11.cloned.1.call-done = bf16[1,1024,1280]{2,1,0:T(8,128)(2,1)} async-done(((bf16[1,256,1280]{2,1,0:T(8,128)(2,1)}), bf16[1,1024,1280]{2,1,0:T(8,128)(2,1)}) %all-gather.11.cloned.1.call-update) | async-done | bytes 2621456 | tf_op jit(solution)/shard_map/all_gather | solution.py:200
  270.6 5.0 fusion.19
  275.6 4.3 multiply_reduce_fusion
  280.0 4.4 multiply_reduce_fusion.1
  284.4 4.4 multiply_convert_fusion.1
  304.8 3.9 add_bitcast_fusion
  308.8 9.9 fusion.27
  318.9 9.4 fusion.35
  328.4 9.9 fusion.32
  347.0 13.2 %reduce-scatter.11.cloned.1.call-done = f32[1,256,1280]{2,1,0:T(8,128)} async-done(((f32[1,1024,1280]{2,1,0:T(8,128)}), f32[1,256,1280]{2,1,0:T(8,128)}) %reduce-scatter.11.cloned.1.call-update) | async-done | bytes 1310736 | tf_op jit(solution)/shard_map/reduce_scatter | solution.py:238
  362.0 10.1 all-reduce.2
  372.2 37.7 %all-reduce = (f32[1280]{0:T(1024)}, f32[1280]{0:T(1024)}) all-reduce(f32[1280]{0:T(1024)S(1)} %get-tuple-element.22, f32[1280]{0:T(1024)S(1)} %get-tuple-element.23), channel_id=1, replica_groups=mesh['dp'=8,'mp'=4] {'dp'}, use_global_device_ids=true, to_apply=%region_18.19 | all-reduce | flops 2560 | bytes 20480 | tf_op jit(solution)/shard_map/psum | solution.py:251
  409.9 3.7 fusion.81
  413.7 579.4 %all-reduce.5.cloned.1.call-done = (f32[1280,320]{0,1:T(8,128)}, f32[1280,320]{0,1:T(8,128)}, f32[1280,320]{0,1:T(8,128)}, f32[320,1280]{1,0:T(8,128)}, f32[1280,1280]{1,0:T(8,128)}, /*index=5*/f32[1280,1280]{1,0:T(8,128)}) async-done(((f32[1280,320]{0,1:T(8,128)}, f32[1280,320]{0,1:T(8,128)}, f32[1280,320]{0,1:T(8,128)}, f32[320,1280]{1,0:T(8,128)}, f32[1280,1280]{1,0:T(8,128)}, ...) | async-done | bytes 19660816 | tf_op jit(solution)/shard_map/psum | solution.py:251
  1004.5 3.3 copy.32
  (207 shorter events, 79.2 us)
Async XLA Ops:
  7.2 136.8 %copy-start = (bf16[1280,1280]{1,0:T(8,128)(2,1)S(1)}, bf16[1280,1280]{1,0:T(8,128)(2,1)}, u32[]{:S(2)}) copy-start(bf16[1280,1280]{1,0:T(8,128)(2,1)} %param.19) | copy-start | bytes 9830404
  7.2 32.7 %all-gather.5.cloned.1.call-start = ((), (), s32[]{:S(2)}) async-start(), calls=%async_computation.4 | async-start | bytes 3276800 | tf_op jit(solution)/shard_map/all_gather | solution.py:163
  11.4 103.0 %reduce-scatter.5.cloned.1.call-start = ((), (), s32[]{:S(2)}) async-start(), calls=%async_computation.5 | async-start | bytes 6553600 | tf_op jit(solution)/shard_map/reduce_scatter | solution.py:179
  13.8 30.3 %copy-start.28 = (f32[1024,40]{0,1:T(8,128)}, f32[1024,40]{0,1:T(8,128)S(1)}, u32[]{:S(2)}) copy-start(f32[1024,40]{0,1:T(8,128)S(1)} %get-tuple-element.42) | copy-start | bytes 491524
  62.9 54.3 %copy-start.43 = (f32[1280]{0:T(1024)S(1)}, f32[1280]{0:T(1024)}, u32[]{:S(2)}) copy-start(f32[1280]{0:T(1024)} %param.18) | copy-start | bytes 15364
  62.9 81.0 %all-gather.7.cloned.1.call-start = ((), (), s32[]{:S(2)}) async-start(), calls=%async_computation.6 | async-start | bytes 3276800 | tf_op jit(solution)/shard_map/all_gather | solution.py:182
  118.3 52.7 %all-gather.9.cloned.1.call-start = ((), (), s32[]{:S(2)}) async-start(), calls=%async_computation.8 | async-start | bytes 3276800 | tf_op jit(solution)/shard_map/all_gather | solution.py:190
  118.9 119.7 %reduce-scatter.9.cloned.1.call-start = ((), (), s32[]{:S(2)}) async-start(), calls=%async_computation.9 | async-start | bytes 6553600 | tf_op jit(solution)/shard_map/reduce_scatter | solution.py:195
  187.0 51.5 %copy-start.5 = (f32[1,256,1280]{2,1,0:T(8,128)S(1)}, f32[1,256,1280]{2,1,0:T(8,128)}, u32[]{:S(2)}) copy-start(f32[1,256,1280]{2,1,0:T(8,128)} %copy-done.4) | copy-start | bytes 3932164
  187.0 53.4 %copy-start.10 = (bf16[1,256,1280]{2,1,0:T(8,128)(2,1)S(1)}, bf16[1,256,1280]{2,1,0:T(8,128)(2,1)}, u32[]{:S(2)}) copy-start(bf16[1,256,1280]{2,1,0:T(8,128)(2,1)} %param.21) | copy-start | bytes 1966084
  187.1 80.3 %all-gather.11.cloned.1.call-start = ((), (), s32[]{:S(2)}) async-start(), calls=%async_computation.10 | async-start | bytes 3276800 | tf_op jit(solution)/shard_map/all_gather | solution.py:200
  241.7 118.6 %reduce-scatter.11.cloned.1.call-start = ((), (), s32[]{:S(2)}) async-start(), calls=%async_computation.11 | async-start | bytes 6553600 | tf_op jit(solution)/shard_map/reduce_scatter | solution.py:238
  270.5 9.4 copy-start.19
  270.6 9.4 slice-start.2
  308.7 101.2 %reduce-scatter.7.cloned.1.call-start = ((), (), s32[]{:S(2)}) async-start(), calls=%async_computation.7 | async-start | bytes 3276800 | tf_op jit(solution)/shard_map/reduce_scatter | solution.py:185
  318.7 674.4 %all-reduce.5.cloned.1.call-start = ((), (), s32[]{:S(2)}) async-start(), calls=%async_computation.12 | async-start | bytes 39321600 | tf_op jit(solution)/shard_map/psum | solution.py:251
  318.9 9.4 copy-start.50
  328.4 9.9 copy-start.40
  328.4 9.9 copy-start.42
  328.4 9.9 copy-start.51
  347.0 13.3 %copy-start.6 = (bf16[1,256,1280]{2,1,0:T(8,128)(2,1)S(1)}, bf16[1,256,1280]{2,1,0:T(8,128)(2,1)}, u32[]{:S(2)}) copy-start(bf16[1,256,1280]{2,1,0:T(8,128)(2,1)} %param.11) | copy-start | bytes 1966084
  347.0 13.3 %copy-start.44 = (f32[1280]{0:T(1024)S(1)}, f32[1280]{0:T(1024)}, u32[]{:S(2)}) copy-start(f32[1280]{0:T(1024)} %param.13) | copy-start | bytes 15364
  347.0 13.3 %copy-start.47 = (f32[256]{0:T(256)S(1)}, f32[256]{0:T(256)}, u32[]{:S(2)}) copy-start(f32[256]{0:T(256)} %copy-done.46) | copy-start | bytes 3076
  347.0 62.9 %copy-start.8 = (f32[1,256,1280]{2,1,0:T(8,128)S(1)}, f32[1,256,1280]{2,1,0:T(8,128)}, u32[]{:S(2)}) copy-start(f32[1,256,1280]{2,1,0:T(8,128)} %reduce-scatter.9.cloned.1.call-done) | copy-start | bytes 3932164
  (47 other events, 140.0 us)
Sparse Core Ops, SparseCore 0:
  11.6 28.2 all-gather.4
  63.0 51.3 reduce-scatter.4
  118.4 25.5 all-gather.6
  145.4 25.5 all-gather.8
  187.2 51.3 reduce-scatter.8
  241.8 25.5 all-gather.10
  308.8 51.3 reduce-scatter.10
  362.8 34.4 reduce-scatter.6
  403.9 589.1 all-reduce.4
where the time goes:
time: 1030 us; the launch traced here: 1020 us
  waiting for transfers between devices  790 us (77%)
  matrix products  109 us (11%)
  blocking collectives  47.9 us (5%)
  other arithmetic  30 us (3%)
  local copies, waits for them, and re-layouts  22.6 us (2%)
  between operations  14.9 us (1%)
    psum x1, waiting for transfers between devices, on_device(): lax.psum((query_total, key_total, value_total, out_total, attn_gain_part,...  579 us
    reduce_scatter x1, waiting for transfers between devices, on_device(): lax.psum_scatter(project_back(grad_up_pre, up_weight), 'mp', scatter_dime...  51.5 us
    reduce_scatter x1, waiting for transfers between devices, on_device(): lax.psum_scatter(project(mixed, out_weight), 'mp', scatter_dimension=1, t...  51.2 us
    psum x1, blocking collectives, on_device(): lax.psum((query_total, key_total, value_total, out_total, attn_gain_part,...  37.7 us
    dot_general x6, matrix products, weight_grad(): jnp.einsum('rsd,rse->de', left, right, preferred_element_type=jnp.float32)  28 us
    dot_general x6, matrix products, project(): jnp.einsum('rsd,de->rse', left, weight, preferred_element_type=jnp.float32)  26.6 us
    all_gather x1, waiting for transfers between devices, on_device(): lax.all_gather(grad_resid.astype(jnp.bfloat16), 'mp', axis=1, tiled=True)  25.2 us
    all_gather x1, waiting for transfers between devices, on_device(): lax.all_gather(scaled_two.astype(jnp.bfloat16), 'mp', axis=1, tiled=True)  25.1 us
  transfers between devices with their start and end apart: 9, of which 8 were waited for; matrix products, arithmetic and copies ran while one was open for 5% of the time, Pallas kernels for 0%

commit v1 on v0

--- a/solution.py
+++ b/solution.py
@@ -3,6 +3,8 @@
 import jax
 import jax.numpy as jnp
 from jax import lax
+from jax.experimental import pallas as pl
+from jax.experimental.pallas import tpu as pltpu
 from jax.sharding import PartitionSpec as P
 
 HEAD = 80
@@ -136,6 +138,329 @@
             preferred_element_type=jnp.float32,
         )
     return (jnp.concatenate(query_parts, 0), key_total, value_total)
+
+
+MESH = pl.DeviceIdType.MESH
+CHUNK = 64
+SLOTS = 8
+STAGES = 6
+(R1Z, R2Z, R3Z, FZM, FZA, FZB, R1Y, R2Y, R3Y, FYI, FYY) = range(11)
+(S0Z, S0Y, S1Z, S1Y, S2Z, S2Y, S3ZM, S3ZE, S3YE, S3YY, S4Z, S4Y) = range(12)
+
+
+def add_rows(total_ref, row, count, *others):
+    value = total_ref[pl.ds(row, count), :].astype(jnp.float32)
+    for other in others:
+        value = value + other[...].astype(jnp.float32)
+    total_ref[pl.ds(row, count), :] = value.astype(jnp.bfloat16)
+
+
+class Reducer:
+    def __init__(self, rows, bufs, send_sem, recv_sem, pairs):
+        self.rows, self.bufs, self.send_sem, self.recv_sem, self.pairs = rows, bufs, send_sem, recv_sem, pairs
+        dp = lax.axis_index("dp")
+        self.place, self.side = lax.div(dp, 2), lax.rem(dp, 2)
+        self.inner = (self.place == 1) | (self.place == 2)
+        self.end = jnp.logical_not(self.inner)
+        self.mate = 2 * (self.place + 1 - 2 * lax.rem(self.place, 2)) + self.side
+        self.across = 2 * (3 - self.place) + self.side
+        self.twin = 2 * self.place + 1 - self.side
+        self.half_z = lax.div(self.place, 2)
+        self.half_y = self.side
+
+    def copy(self, source, target, send, recv, slot, device):
+        return pltpu.make_async_remote_copy(
+            src_ref=source,
+            dst_ref=target,
+            send_sem=self.send_sem.at[send, slot],
+            recv_sem=self.recv_sem.at[recv, slot],
+            device_id={"dp": device},
+            device_id_type=MESH,
+        )
+
+    def whole_z(self, pair):
+        return pl.multiple_of(pair * (2 * CHUNK), CHUNK)
+
+    def at_z(self, pair, half):
+        return pl.multiple_of(pair * (2 * CHUNK) + half * (CHUNK // 2), CHUNK // 2)
+
+    def at_y(self, pair, half):
+        return pl.multiple_of(pair * (2 * CHUNK) + CHUNK + half * (CHUNK // 2), CHUNK // 2)
+
+    def moves(self, pair):
+        slot = lax.rem(pair, SLOTS)
+        rows, (one_z, two_z, three_z, one_y, two_y, three_y) = self.rows, self.bufs
+        half = CHUNK // 2
+        mine_z, mine_y = self.half_z, self.half_y
+        own_z = rows.at[pl.ds(self.at_z(pair, mine_z), half), :]
+        rest_z = rows.at[pl.ds(self.at_z(pair, 1 - mine_z), half), :]
+        own_y = rows.at[pl.ds(self.at_y(pair, mine_y), half), :]
+        rest_y = rows.at[pl.ds(self.at_y(pair, 1 - mine_y), half), :]
+        all_z = rows.at[pl.ds(self.whole_z(pair), CHUNK), :]
+        return dict(
+            s0z=lambda: self.copy(all_z, one_z.at[slot], S0Z, R1Z, slot, self.mate),
+            s0y=lambda: self.copy(rest_y, one_y.at[slot], S0Y, R1Y, slot, self.twin),
+            s1z=lambda: self.copy(rest_z, two_z.at[slot], S1Z, R2Z, slot, self.across),
+            s1y=lambda: self.copy(two_y.at[slot], two_y.at[slot], S1Y, R2Y, slot, self.mate),
+            s2z=lambda: self.copy(own_z, three_z.at[slot], S2Z, R3Z, slot, self.twin),
+            s2y=lambda: self.copy(own_y, three_y.at[slot], S2Y, R3Y, slot, self.across),
+            s3zm=lambda: self.copy(own_z, own_z, S3ZM, FZM, slot, self.across),
+            s3ze=lambda: self.copy(own_z, own_z, S3ZE, FZA, slot, self.mate),
+            s3ye=lambda: self.copy(own_y, own_y, S3YE, FYI, slot, self.mate),
+            s3yy=lambda: self.copy(own_y, own_y, S3YY, FYY, slot, self.twin),
+            s4z=lambda: self.copy(rest_z, rest_z, S4Z, FZB, slot, self.mate),
+            s4y=lambda: self.copy(own_y, own_y, S4Y, FYY, slot, self.twin),
+        )
+
+    def when(self, slot_index, stage, role, body):
+        pair = slot_index - stage
+        live = (pair >= 0) & (pair < self.pairs)
+        if role is not None:
+            live = live & role
+
+        @pl.when(live)
+        def _():
+            body(pair)
+
+    def slot(self, index):
+        half = CHUNK // 2
+        one_z, two_z, three_z, one_y, two_y, three_y = self.bufs
+
+        def last(pair):
+            m = self.moves(pair)
+            @pl.when(self.end)
+            def _():
+                m["s3ze"]().wait_recv()
+                m["s4z"]().wait_recv()
+                m["s1y"]().wait_send()
+                m["s4y"]().wait_send()
+                m["s4y"]().wait_recv()
+
+            @pl.when(self.inner)
+            def _():
+                m["s3zm"]().wait_send()
+                m["s3ze"]().wait_send()
+                m["s3ye"]().wait_send()
+                m["s3yy"]().wait_send()
+                m["s4z"]().wait_send()
+                m["s3yy"]().wait_recv()
+
+        def fourth_inner(pair):
+            m = self.moves(pair)
+            m["s3zm"]().wait_recv()
+            m["s4z"]().start()
+
+        def fourth_end(pair):
+            m = self.moves(pair)
+            m["s3ye"]().wait_recv()
+            m["s4y"]().start()
+
+        def third(pair):
+            m = self.moves(pair)
+            slot = lax.rem(pair, SLOTS)
+            m["s2z"]().wait()
+            m["s2y"]().wait()
+            add_rows(self.rows, self.at_z(pair, self.half_z), half, three_z.at[slot])
+            add_rows(self.rows, self.at_y(pair, self.half_y), half, three_y.at[slot])
+            m["s3ze"]().start()
+            m["s3zm"]().start()
+            m["s3ye"]().start()
+            m["s3yy"]().start()
+
+        def second(pair):
+            m = self.moves(pair)
+            slot = lax.rem(pair, SLOTS)
+            m["s1z"]().wait()
+            m["s1y"]().wait_recv()
+            m["s0y"]().wait_send()
+            add_rows(
+                self.rows, self.at_z(pair, self.half_z), half,
+                one_z.at[slot, pl.ds(pl.multiple_of(self.half_z * half, half), half), :], two_z.at[slot],
+            )
+            add_rows(self.rows, self.at_y(pair, self.half_y), half, one_y.at[slot], two_y.at[slot])
+            m["s2z"]().start()
+            m["s2y"]().start()
+
+        def first_inner(pair):
+            m = self.moves(pair)
+            slot = lax.rem(pair, SLOTS)
+            m["s0z"]().wait_recv()
+            m["s0y"]().wait_recv()
+            other = 1 - self.half_z
+            add_rows(
+                self.rows, self.at_z(pair, other), half,
+                one_z.at[slot, pl.ds(pl.multiple_of(other * half, half), half), :],
+            )
+            m["s1z"]().start()
+
+        def first_end(pair):
+            m = self.moves(pair)
+            slot = lax.rem(pair, SLOTS)
+            m["s0y"]().wait()
+            m["s0z"]().wait_send()
+            mine = self.rows[pl.ds(self.at_y(pair, self.half_y), half), :].astype(jnp.float32)
+            two_y[slot] = (mine + one_y[slot].astype(jnp.float32)).astype(jnp.bfloat16)
+            m["s1y"]().start()
+
+        def start(pair):
+            m = self.moves(pair)
+            m["s0y"]().start()
+
+            @pl.when(self.end)
+            def _():
+                m["s0z"]().start()
+
+        self.when(index, 0, None, start)
+        self.when(index, 1, self.end, first_end)
+        self.when(index, 1, self.inner, first_inner)
+        self.when(index, 2, self.inner, second)
+        self.when(index, 3, self.inner, third)
+        self.when(index, 4, self.inner, fourth_inner)
+        self.when(index, 4, self.end, fourth_end)
+        self.when(index, 5, None, last)
+
+    def greet(self, barrier):
+        for device in (self.mate, self.across, self.twin):
+            pl.semaphore_signal(barrier, inc=1, device_id={"dp": device}, device_id_type=MESH)
+        return 3
+
+
+def reducer_scratch(width):
+    half = CHUNK // 2
+    return [
+        pltpu.VMEM((SLOTS, CHUNK, width), jnp.bfloat16),
+        pltpu.VMEM((SLOTS, half, width), jnp.bfloat16),
+        pltpu.VMEM((SLOTS, half, width), jnp.bfloat16),
+        pltpu.VMEM((SLOTS, half, width), jnp.bfloat16),
+        pltpu.VMEM((SLOTS, half, width), jnp.bfloat16),
+        pltpu.VMEM((SLOTS, half, width), jnp.bfloat16),
+        pltpu.SemaphoreType.DMA((12, SLOTS)),
+        pltpu.SemaphoreType.DMA((11, SLOTS)),
+    ]
+
+
+def reduce_kernel(
+    down, up, outg, qg, kg, vg, down_o, up_o, out_o, q_o, k_o, v_o,
+    rows, b0, b1, b2, b3, b4, b5, send_sem, recv_sem, stage, stage_sem, load_sem, tstage, tsem,
+):
+    width = rows.shape[1]
+    local = outg.shape[0]
+    hidden = down.shape[0]
+    pairs = rows.shape[0] // (2 * CHUNK)
+    red = Reducer(rows, (b0, b1, b2, b3, b4, b5), send_sem, recv_sem, pairs)
+    barrier = pltpu.get_barrier_semaphore()
+    count = red.greet(barrier)
+    loads, at = [], 0
+    for i, source in enumerate((down, up, outg, qg, kg, vg)):
+        loads.append(pltpu.make_async_copy(source, rows.at[pl.ds(at, source.shape[0]), :], load_sem.at[i]))
+        at += source.shape[0]
+    for load in loads:
+        load.start()
+    pl.semaphore_wait(barrier, count)
+    for load in loads:
+        load.wait()
+
+    def put(pair, target, base, count=2 * CHUNK):
+        slot = lax.rem(pair, 2)
+        return pltpu.make_async_copy(
+            stage.at[slot, pl.ds(0, count), :], target.at[pl.ds(pl.multiple_of(base, CHUNK), count), :], stage_sem.at[slot]
+        )
+
+    down_pairs = hidden // (2 * CHUNK)
+
+    def out_pair(pair, first):
+        slot = lax.rem(pair, 2)
+
+        @pl.when(pair >= 2)
+        def _():
+            put(pair, down_o, 0).wait()
+
+        stage[slot] = rows[pl.ds(pl.multiple_of(pair * 2 * CHUNK, 2 * CHUNK), 2 * CHUNK), :].astype(jnp.float32)
+
+        @pl.when(pair < down_pairs)
+        def _():
+            put(pair, down_o, pair * 2 * CHUNK).start()
+
+        @pl.when((pair >= down_pairs) & (pair < 2 * down_pairs))
+        def _():
+            put(pair, up_o, (pair - down_pairs) * 2 * CHUNK).start()
+
+        @pl.when(pair >= 2 * down_pairs)
+        def _():
+            put(pair, out_o, (pair - 2 * down_pairs) * 2 * CHUNK).start()
+
+    whole_out = local // (2 * CHUNK)
+    plain = 2 * down_pairs + whole_out
+
+    def step(index, carry):
+        red.slot(index)
+        pair = index - 5
+
+        @pl.when((pair >= 0) & (pair < plain))
+        def _():
+            out_pair(pair, 0)
+
+        return carry
+
+    lax.fori_loop(0, pairs + STAGES - 1, step, 0)
+    left = local - whole_out * 2 * CHUNK
+    base = 2 * hidden
+    for pair in (plain, plain + 1):
+        put(pair, down_o, 0).wait()
+    if left:
+        stage[0, pl.ds(0, left), :] = rows[pl.ds(base + whole_out * 2 * CHUNK, left), :].astype(jnp.float32)
+        put(0, out_o, whole_out * 2 * CHUNK, left).start()
+        put(0, out_o, whole_out * 2 * CHUNK, left).wait()
+    block = 256
+    eye = (lax.broadcasted_iota(jnp.int32, (block, block), 0) == lax.broadcasted_iota(jnp.int32, (block, block), 1)).astype(jnp.bfloat16)
+    copies = []
+    n = 0
+    for i, target in enumerate((q_o, k_o, v_o)):
+        row = base + local * (i + 1)
+        for b in range(width // block):
+            slot = n % 2
+            if n >= 2:
+                copies[n - 2].wait()
+            tstage[slot] = lax.dot_general(
+                eye, rows[pl.ds(row, local), pl.ds(b * block, block)], (((1,), (1,)), ((), ())), preferred_element_type=jnp.float32
+            )
+            c = pltpu.make_async_copy(tstage.at[slot], target.at[pl.ds(b * block, block), :], tsem.at[slot])
+            c.start()
+            copies.append(c)
+            n += 1
+    copies[-2].wait()
+    copies[-1].wait()
+
+
+def reduce_grads(down, up, outg, qg, kg, vg):
+    local, width = outg.shape
+    hidden = down.shape[0]
+    total = 2 * hidden + 4 * local
+    f32 = jnp.float32
+    shapes = [(hidden, width), (hidden, width), (local, width)] + [(width, local)] * 3
+    return pl.pallas_call(
+        reduce_kernel,
+        out_shape=[jax.ShapeDtypeStruct(s, f32) for s in shapes],
+        in_specs=[pl.BlockSpec(memory_space=pl.ANY)] * 6,
+        out_specs=[pl.BlockSpec(memory_space=pl.ANY)] * 6,
+        scratch_shapes=[pltpu.VMEM((total, width), jnp.bfloat16)]
+        + reducer_scratch(width)
+        + [
+            pltpu.VMEM((2, 2 * CHUNK, width), f32),
+            pltpu.SemaphoreType.DMA((2,)),
+            pltpu.SemaphoreType.DMA((6,)),
+            pltpu.VMEM((2, 256, local), f32),
+            pltpu.SemaphoreType.DMA((2,)),
+        ],
+        compiler_params=pltpu.CompilerParams(collective_id=0, has_side_effects=True, vmem_limit_bytes=40 * 2**20),
+    )(down, up, outg, qg, kg, vg)
+
+
+def reduce_all(parts):
+    if lax.axis_size("dp") == 8:
+        return reduce_grads(*parts)
+    sums = [part.astype(jnp.float32) for part in lax.psum(parts, "dp")]
+    return sums[:3] + [part.T for part in sums[3:]]
 
 
 def on_device(
@@ -188,17 +513,17 @@
     result = (resid + mlp_share).astype(jnp.bfloat16)
     grad_top = out_cotangent.astype(jnp.float32)
     grad_rows = lax.all_gather(out_cotangent, "mp", axis=1, tiled=True)
-    down_total = weight_grad(hidden, grad_rows)
+    down_total = weight_grad(hidden, grad_rows).astype(jnp.bfloat16)
     grad_hidden = project_back(grad_rows, down_weight)
     grad_up_pre = (grad_hidden * gelu_slope(up_pre)).astype(jnp.bfloat16)
-    up_total = weight_grad(rows_two, grad_up_pre)
+    up_total = weight_grad(rows_two, grad_up_pre).astype(jnp.bfloat16)
     grad_two = lax.psum_scatter(
         project_back(grad_up_pre, up_weight), "mp", scatter_dimension=1, tiled=True
     )
     resid_part, mlp_gain_part = norm_back(grad_two, normed_two, inverse_two, mlp_gain)
     grad_resid = grad_top + resid_part
     branch_rows = lax.all_gather(grad_resid.astype(jnp.bfloat16), "mp", axis=1, tiled=True)
-    out_total = weight_grad(mixed, branch_rows)
+    out_total = weight_grad(mixed, branch_rows).astype(jnp.bfloat16)
     grad_mixed = project_back(branch_rows, out_weight).astype(jnp.bfloat16).reshape(head_shape)
     row_index = 0
     grad_q, grad_k, grad_v = attend_back(
@@ -227,9 +552,10 @@
     grad_value = (
         jnp.stack(value_rows, 0).astype(jnp.bfloat16).reshape(row_count, seq_len, local_width)
     )
-    query_total = weight_grad(rows_one, grad_query)
-    key_total = weight_grad(rows_one, grad_key)
-    value_total = weight_grad(rows_one, grad_value)
+    bf = jnp.bfloat16
+    query_total = weight_grad(grad_query, rows_one).astype(bf)
+    key_total = weight_grad(grad_key, rows_one).astype(bf)
+    value_total = weight_grad(grad_value, rows_one).astype(bf)
     grad_terms = (
         project_back(grad_query, query_weight)
         + project_back(grad_key, key_weight)
@@ -238,28 +564,9 @@
     grad_one = lax.psum_scatter(grad_terms, "mp", scatter_dimension=1, tiled=True)
     input_part, attn_gain_part = norm_back(grad_one, normed_one, inverse_one, attn_gain)
     input_grad = grad_resid + input_part
-    attn_gain_part, mlp_gain_part = lax.psum((attn_gain_part, mlp_gain_part), "mp")
-    (
-        query_total,
-        key_total,
-        value_total,
-        out_total,
-        attn_gain_part,
-        mlp_gain_part,
-        up_total,
-        down_total,
-    ) = lax.psum(
-        (
-            query_total,
-            key_total,
-            value_total,
-            out_total,
-            attn_gain_part,
-            mlp_gain_part,
-            up_total,
-            down_total,
-        ),
-        "dp",
+    attn_gain_part, mlp_gain_part = lax.psum((attn_gain_part, mlp_gain_part), ("dp", "mp"))
+    down_total, up_total, out_total, query_total, key_total, value_total = reduce_all(
+        (down_total, up_total, out_total, query_total, key_total, value_total)
     )
     return (
         result,

time: 1030 us -> 611 us (0.59)
  waiting for transfers between devices: 790 us -> 197 us
  Pallas kernels: 0 us -> 191 us
  matrix products: 109 us -> 97.1 us
    psum x1 -> x0, waiting for transfers between devices: 579 us -> none  [on_device(): lax.psum((query_total, key_total, value_total, out_total, attn_gain_part,...]
    pallas_call x0 -> x1, Pallas kernels: none -> 191 us  [reduce_grads(): pl.pallas_call(reduce_kernel, out_shape=[jax.ShapeDtypeStruct(s, f32) for...]
    reduce_scatter x1, waiting for transfers between devices: 13.2 us -> 0.01 us  [on_device(): lax.psum_scatter(grad_terms, 'mp', scatter_dimension=1, tiled=True)]
    psum x2 -> x1, blocking collectives: 47.9 us -> 38.3 us  [on_device(): lax.psum((attn_gain_part, mlp_gain_part), ('dp', 'mp'))]
    unnamed x130 -> x124, local copies, waits for them, and re-layouts: 22.3 us -> 30 us
  transfers between devices with their start and end apart: 9 -> 8, of which waited for: 8 -> 6; matrix products, arithmetic and copies ran while one was open for 5% -> 8% of each run, Pallas kernels for 0% -> 32%
where the time goes in v1:
time: 611 us; the launch traced here: 601 us
  waiting for transfers between devices  197 us (32%)
  Pallas kernels  191 us (31%)
  matrix products  97.1 us (16%)
  blocking collectives  38.3 us (6%)
  local copies, waits for them, and re-layouts  31.1 us (5%)
  other arithmetic  29.6 us (5%)
  between operations  15.4 us (3%)
    pallas_call x1, Pallas kernels, reduce_grads(): pl.pallas_call(reduce_kernel, out_shape=[jax.ShapeDtypeStruct(s, f32) for...  191 us
    reduce_scatter x1, waiting for transfers between devices, on_device(): lax.psum_scatter(project_back(grad_up_pre, up_weight), 'mp', scatter_dime...  51.4 us
    reduce_scatter x1, waiting for transfers between devices, on_device(): lax.psum_scatter(project(mixed, out_weight), 'mp', scatter_dimension=1, t...  51 us
    psum x1, blocking collectives, on_device(): lax.psum((attn_gain_part, mlp_gain_part), ('dp', 'mp'))  38.3 us
    unnamed x124, local copies, waits for them, and re-layouts  30 us
    dot_general x6, matrix products, project(): jnp.einsum('rsd,de->rse', left, weight, preferred_element_type=jnp.float32)  26.5 us
    all_gather x1, waiting for transfers between devices, on_device(): lax.all_gather(grad_resid.astype(jnp.bfloat16), 'mp', axis=1, tiled=True)  25.4 us
    all_gather x1, waiting for transfers between devices, on_device(): lax.all_gather(scaled_two.astype(jnp.bfloat16), 'mp', axis=1, tiled=True)  25.1 us
  transfers between devices with their start and end apart: 8, of which 6 were waited for; matrix products, arithmetic and copies ran while one was open for 8% of the time, Pallas kernels for 32%

profile of v1, /device:TPU:0, one launch (start us, length us, event | category | flops | bytes accessed | tf_op | source)
XLA Modules:
  0.0 601.1 jit_solution(10167952360104575371)
XLA Ops:
  15.6 24.3 %all-gather.5.cloned.1.call-done = bf16[1,1024,1280]{2,1,0:T(8,128)(2,1)} async-done(((bf16[1,256,1280]{2,1,0:T(8,128)(2,1)}), bf16[1,1024,1280]{2,1,0:T(8,128)(2,1)}) %all-gather.5.cloned.1.call-update) | async-done | bytes 2621456 | tf_op jit(solution)/shard_map/all_gather | solution.py:488
  39.9 3.1 fusion.51
  59.0 3.9 convolution_bitcast_fusion.1
  63.4 51.0 %reduce-scatter.5.cloned.1.call-done = f32[1,256,1280]{2,1,0:T(8,128)} async-done(((f32[1,1024,1280]{2,1,0:T(8,128)}), f32[1,256,1280]{2,1,0:T(8,128)}) %reduce-scatter.5.cloned.1.call-update) | async-done | bytes 1310736 | tf_op jit(solution)/shard_map/reduce_scatter | solution.py:504
  118.9 25.1 %all-gather.7.cloned.1.call-done = bf16[1,1024,1280]{2,1,0:T(8,128)(2,1)} async-done(((bf16[1,256,1280]{2,1,0:T(8,128)(2,1)}), bf16[1,1024,1280]{2,1,0:T(8,128)(2,1)}) %all-gather.7.cloned.1.call-update) | async-done | bytes 2621456 | tf_op jit(solution)/shard_map/all_gather | solution.py:507
  144.0 7.6 %fusion.34 = f32[1024,1280]{1,0:T(8,128)} fusion(bf16[1280,1280]{1,0:T(8,128)(2,1)S(1)} %copy-done, bf16[1,1024,1280]{2,1,0:T(8,128)(2,1)} %all-gather.7.cloned.1.call-done), kind=kOutput, calls=%fused_computation.57 | convolution fusion | flops 3355443200 | bytes 11141120 | tf_op jit(solution)/shard_map/rsd,de->rse/dot_general | solution.py:39
  151.6 19.3 %all-gather.9.cloned.1.call-done = bf16[1,1024,1280]{2,1,0:T(8,128)(2,1)} async-done(((bf16[1,256,1280]{2,1,0:T(8,128)(2,1)}), bf16[1,1024,1280]{2,1,0:T(8,128)(2,1)}) %all-gather.9.cloned.1.call-update) | async-done | bytes 2621456 | tf_op jit(solution)/shard_map/all_gather | solution.py:515
  170.9 9.3 %fusion.18 = bf16[1024,1280]{1,0:T(8,128)(2,1)S(1)} fusion(f32[1024,1280]{1,0:T(8,128)} %fusion.34, bf16[1280,1280]{1,0:T(8,128)(2,1)} %param.20, bf16[1,1024,1280]{2,1,0:T(8,128)(2,1)} %all-gather.9.cloned.1.call-done), kind=kOutput, calls=%fused_computation.35 | convolution fusion | flops 3380346880 | bytes 13762560 | tf_op jit(solution)/shard_map/rse,de->rsd/dot_general | solution.py:43
  181.8 5.3 convolution_bitcast_fusion
  187.1 51.4 %reduce-scatter.9.cloned.1.call-done = f32[1,256,1280]{2,1,0:T(8,128)} async-done(((f32[1,1024,1280]{2,1,0:T(8,128)}), f32[1,256,1280]{2,1,0:T(8,128)}) %reduce-scatter.9.cloned.1.call-update) | async-done | bytes 1310736 | tf_op jit(solution)/shard_map/reduce_scatter | solution.py:520
  242.6 25.4 %all-gather.11.cloned.1.call-done = bf16[1,1024,1280]{2,1,0:T(8,128)(2,1)} async-done(((bf16[1,256,1280]{2,1,0:T(8,128)(2,1)}), bf16[1,1024,1280]{2,1,0:T(8,128)(2,1)}) %all-gather.11.cloned.1.call-update) | async-done | bytes 2621456 | tf_op jit(solution)/shard_map/all_gather | solution.py:525
  268.0 3.0 fusion.78
  271.7 6.1 %multiply_reduce_fusion.1 = (f32[4,512]{1,0:T(4,128)}, f32[4,512,1024]{2,1,0:T(8,128)S(1)}) fusion(f32[4,512,1024]{2,1,0:T(8,128)} %copy-done.7, f32[4,512]{1,0:T(4,128)S(1)} %log_add_fusion.1, bf16[512,4,80]{0,2,1:T(8,128)(2,1)S(1)} %bitcast.160, bf16[1024,4,80]{0,2,1:T(8,128)(2,1)S(1)} %copy-done.23), kind=kOutput, calls=%fused_computation.4 | convolution fusion | flops 341833728 | bytes 17776640 | tf_op jit(solution)/shard_map/qhd,khd->hqk/dot_general | solution.py:118
  299.6 4.0 add_bitcast_fusion
  303.8 9.8 %fusion.27 = bf16[1,1024,1280]{2,1,0:T(8,128)(2,1)} fusion(bf16[1280,1280]{1,0:T(8,128)(2,1)} %param.20, f32[1024,1280]{1,0:T(8,128)} %fusion.34), kind=kOutput, calls=%fused_computation.46 | convolution fusion | flops 3368550400 | bytes 11141120 | tf_op jit(solution)/shard_map/rsd,de->rse/dot_general | solution.py:39
  313.6 8.3 %convolution_convert_fusion.up = bf16[1280,1280]{1,0:T(8,128)(2,1)} fusion(bf16[1024,1280]{1,0:T(8,128)(2,1)} %copy-done.52, bf16[1,1024,1280]{2,1,0:T(8,128)(2,1)} %all-gather.7.cloned.1.call-done), kind=kOutput, calls=%fused_computation.15 | convolution fusion | flops 3357081600 | bytes 8519680 | tf_op jit(solution)/shard_map/rsd,rse->de/dot_general | solution.py:47
  322.0 7.6 %convolution_convert_fusion.1.down = bf16[1280,1280]{1,0:T(8,128)(2,1)S(1)} fusion(bf16[1,1024,1280]{2,1,0:T(8,128)(2,1)S(1)} %copy-done.49, f32[1024,1280]{1,0:T(8,128)} %fusion.34), kind=kOutput, calls=%fused_computation.16 | convolution fusion | flops 3368878080 | bytes 11141120 | tf_op jit(solution)/shard_map/rsd,rse->de/dot_general | solution.py:47
  334.7 191.1 %shard_map.189 = (f32[1280,1280]{1,0:T(8,128)}, f32[1280,1280]{1,0:T(8,128)}, f32[320,1280]{1,0:T(8,128)S(1)}, f32[1280,320]{1,0:T(8,128)S(1)}, f32[1280,320]{1,0:T(8,128)S(1)}, /*index=5*/f32[1280,320]{1,0:T(8,128)S(1)}) custom-call(bf16[1280,1280]{1,0:T(8,128)(2,1)S(1)} %convolution_convert_fusion.1.down, bf16[1280,1280]{1,0:T(8,128)(2,1)} %convolution_convert_fusion.up, ...), custom_call_target="tpu_custom_call" | custom-call | tf_op jit(solution)/shard_map/pallas_call | solution.py:441
  529.6 2.7 copy.24
  532.4 2.7 copy.25
  538.8 38.3 %all-reduce = (f32[1280]{0:T(1024)}, f32[1280]{0:T(1024)}) all-reduce(f32[1280]{0:T(1024)S(1)} %get-tuple-element.44, f32[1280]{0:T(1024)S(1)} %copy-done.42), channel_id=1, replica_groups=mesh['dp'=8,'mp'=4] {'dp','mp'}, use_global_device_ids=true, to_apply=%region_17.18 | all-reduce | flops 2560 | bytes 20480 | tf_op jit(solution)/shard_map/psum | solution.py:567
  577.2 4.3 fusion.75
  582.7 6.8 %copy.31 = f32[1280,1280]{1,0:T(8,128)} copy(f32[1280,1280]{1,0:T(8,128)} %get-tuple-element.100) | data formatting | bytes 13107200
  589.4 3.3 copy.32
  (197 shorter events, 71.8 us)
Async XLA Ops:
  7.2 136.8 %copy-start = (bf16[1280,1280]{1,0:T(8,128)(2,1)S(1)}, bf16[1280,1280]{1,0:T(8,128)(2,1)}, u32[]{:S(2)}) copy-start(bf16[1280,1280]{1,0:T(8,128)(2,1)} %param.19) | copy-start | bytes 9830404
  7.2 32.7 %all-gather.5.cloned.1.call-start = ((), (), s32[]{:S(2)}) async-start(), calls=%async_computation.4 | async-start | bytes 3276800 | tf_op jit(solution)/shard_map/all_gather | solution.py:488
  11.4 103.0 %reduce-scatter.5.cloned.1.call-start = ((), (), s32[]{:S(2)}) async-start(), calls=%async_computation.5 | async-start | bytes 6553600 | tf_op jit(solution)/shard_map/reduce_scatter | solution.py:504
  49.0 7.0 %copy-start.7 = (f32[4,512,1024]{2,1,0:T(8,128)}, f32[4,512,1024]{2,1,0:T(8,128)S(1)}, u32[]{:S(2)}) copy-start(f32[4,512,1024]{2,1,0:T(8,128)S(1)} %get-tuple-element.75) | copy-start | bytes 25165828
  62.9 54.3 %copy-start.39 = (f32[1280]{0:T(1024)S(1)}, f32[1280]{0:T(1024)}, u32[]{:S(2)}) copy-start(f32[1280]{0:T(1024)} %param.18) | copy-start | bytes 15364
  62.9 81.0 %all-gather.7.cloned.1.call-start = ((), (), s32[]{:S(2)}) async-start(), calls=%async_computation.6 | async-start | bytes 3276800 | tf_op jit(solution)/shard_map/all_gather | solution.py:507
  118.3 52.7 %all-gather.9.cloned.1.call-start = ((), (), s32[]{:S(2)}) async-start(), calls=%async_computation.8 | async-start | bytes 3276800 | tf_op jit(solution)/shard_map/all_gather | solution.py:515
  118.8 119.7 %reduce-scatter.9.cloned.1.call-start = ((), (), s32[]{:S(2)}) async-start(), calls=%async_computation.9 | async-start | bytes 6553600 | tf_op jit(solution)/shard_map/reduce_scatter | solution.py:520
  187.0 51.5 %copy-start.9 = (f32[1,256,1280]{2,1,0:T(8,128)S(1)}, f32[1,256,1280]{2,1,0:T(8,128)}, u32[]{:S(2)}) copy-start(f32[1,256,1280]{2,1,0:T(8,128)} %copy-done.8) | copy-start | bytes 3932164
  187.1 53.9 %copy-start.12 = (bf16[1,256,1280]{2,1,0:T(8,128)(2,1)S(1)}, bf16[1,256,1280]{2,1,0:T(8,128)(2,1)}, u32[]{:S(2)}) copy-start(bf16[1,256,1280]{2,1,0:T(8,128)(2,1)} %param.21) | copy-start | bytes 1966084
  187.1 80.9 %all-gather.11.cloned.1.call-start = ((), (), s32[]{:S(2)}) async-start(), calls=%async_computation.10 | async-start | bytes 3276800 | tf_op jit(solution)/shard_map/all_gather | solution.py:525
  242.3 294.5 %reduce-scatter.11.cloned.1.call-start = ((), (), s32[]{:S(2)}) async-start(), calls=%async_computation.11 | async-start | bytes 6553600 | tf_op jit(solution)/shard_map/reduce_scatter | solution.py:564
  242.6 29.2 %copy-start.23 = (bf16[1024,4,80]{0,2,1:T(8,128)(2,1)S(1)}, bf16[1024,4,80]{0,2,1:T(8,128)(2,1)}, u32[]{:S(2)}) copy-start(bf16[1024,4,80]{0,2,1:T(8,128)(2,1)} %copy-done.22) | copy-start | bytes 1966084
  271.7 6.1 %slice-start.2 = ((s8[8388608]{0:T(1024)(128)(4,1)}), s8[4194304]{0:T(1024)(128)(4,1)S(1)}, s32[]{:S(2)}) async-start(s8[8388608]{0:T(1024)(128)(4,1)} %bitcast.152), calls=%async_computation.14 | async-start | bytes 8388608
  271.7 6.1 %slice-start.3 = ((s8[8388608]{0:T(1024)(128)(4,1)}), s8[4194304]{0:T(1024)(128)(4,1)S(1)}, s32[]{:S(2)}) async-start(s8[8388608]{0:T(1024)(128)(4,1)} %bitcast.152), calls=%async_computation.15 | async-start | bytes 8388608
  303.5 273.6 %reduce-scatter.7.cloned.1.call-start = ((), (), s32[]{:S(2)}) async-start(), calls=%async_computation.7 | async-start | bytes 3276800 | tf_op jit(solution)/shard_map/reduce_scatter | solution.py:510
  313.6 8.3 %copy-start.49 = (bf16[1,1024,1280]{2,1,0:T(8,128)(2,1)S(1)}, bf16[1,1024,1280]{2,1,0:T(8,128)(2,1)}, u32[]{:S(2)}) copy-start(bf16[1,1024,1280]{2,1,0:T(8,128)(2,1)} %all-gather.9.cloned.1.call-done) | copy-start | bytes 7864324
  322.0 7.6 %copy-start.36 = (bf16[4,80,512]{2,1,0:T(8,128)(2,1)S(1)}, bf16[4,80,512]{2,1,0:T(8,128)(2,1)}, u32[]{:S(2)}) copy-start(bf16[4,80,512]{2,1,0:T(8,128)(2,1)} %copy-done.35) | copy-start | bytes 983044
  322.0 7.6 %copy-start.38 = (bf16[4,80,512]{2,1,0:T(8,128)(2,1)S(1)}, bf16[4,80,512]{2,1,0:T(8,128)(2,1)}, u32[]{:S(2)}) copy-start(bf16[4,80,512]{2,1,0:T(8,128)(2,1)} %copy-done.37) | copy-start | bytes 983044
  322.0 7.6 %copy-start.50 = (bf16[1,1024,1280]{2,1,0:T(8,128)(2,1)S(1)}, bf16[1,1024,1280]{2,1,0:T(8,128)(2,1)}, u32[]{:S(2)}) copy-start(bf16[1,1024,1280]{2,1,0:T(8,128)(2,1)} %all-gather.11.cloned.1.call-done) | copy-start | bytes 7864324
  535.1 42.0 %copy-start.10 = (f32[1,256,1280]{2,1,0:T(8,128)S(1)}, f32[1,256,1280]{2,1,0:T(8,128)}, u32[]{:S(2)}) copy-start(f32[1,256,1280]{2,1,0:T(8,128)} %copy-done.8) | copy-start | bytes 3932164
  535.1 42.0 %copy-start.46 = (f32[256]{0:T(256)S(1)}, f32[256]{0:T(256)}, u32[]{:S(2)}) copy-start(f32[256]{0:T(256)} %copy-done.45) | copy-start | bytes 3076
  581.5 7.9 %slice-start.4 = ((s8[6553600]{0:T(1024)(128)(4,1)}), s8[4194304]{0:T(1024)(128)(4,1)S(1)}, s32[]{:S(2)}) async-start(s8[6553600]{0:T(1024)(128)(4,1)} %bitcast.154), calls=%async_computation.16 | async-start | bytes 8388608
  582.7 6.8 %slice-start.5 = ((s8[6553600]{0:T(1024)(128)(4,1)}), s8[2359296]{0:T(1024)(128)(4,1)S(1)}, s32[]{:S(2)}) async-start(s8[6553600]{0:T(1024)(128)(4,1)} %bitcast.154), calls=%async_computation.17 | async-start | bytes 4718592
  (43 other events, 101.7 us)
Sparse Core Ops, SparseCore 0:
  11.5 28.2 all-gather.4
  63.0 51.3 reduce-scatter.4
  118.4 25.5 all-gather.6
  145.4 25.5 all-gather.8
  187.2 51.3 reduce-scatter.8
  242.4 25.5 all-gather.10
  303.7 51.3 reduce-scatter.10
  357.6 34.4 reduce-scatter.6

commit v2 on v1

--- a/solution.py
+++ b/solution.py
@@ -142,7 +142,7 @@
 
 MESH = pl.DeviceIdType.MESH
 CHUNK = 64
-SLOTS = 8
+SLOTS = 6
 STAGES = 6
 (R1Z, R2Z, R3Z, FZM, FZA, FZB, R1Y, R2Y, R3Y, FYI, FYY) = range(11)
 (S0Z, S0Y, S1Z, S1Y, S2Z, S2Y, S3ZM, S3ZE, S3YE, S3YY, S4Z, S4Y) = range(12)
@@ -339,43 +339,350 @@
     ]
 
 
-def reduce_kernel(
-    down, up, outg, qg, kg, vg, down_o, up_o, out_o, q_o, k_o, v_o,
-    rows, b0, b1, b2, b3, b4, b5, send_sem, recv_sem, stage, stage_sem, load_sem, tstage, tsem,
+HEAD_PAD = 128
+BLOCK_SEQ = 256
+SPAN = 512
+
+
+def pad_matrix(local, padded, transposed):
+    shape, feature_dim = ((padded, local), 1) if transposed else ((local, padded), 0)
+    feature = lax.broadcasted_iota(jnp.int32, shape, feature_dim)
+    lane = lax.broadcasted_iota(jnp.int32, shape, 1 - feature_dim)
+    head = jnp.zeros(shape, jnp.int32)
+    for h in range(1, local // HEAD):
+        head = head + (feature >= h * HEAD).astype(jnp.int32)
+    within = feature - head * HEAD
+    target = head * HEAD_PAD + within + jnp.where(within >= HEAD // 2, HEAD_PAD // 2 - HEAD // 2, 0)
+    return jnp.where(lane == target, 1.0, 0.0).astype(jnp.bfloat16)
+
+
+def dot(a, b):
+    return jnp.dot(a, b, preferred_element_type=jnp.float32)
+
+
+def dot_nt(a, b):
+    return lax.dot_general(a, b, (((1,), (1,)), ((), ())), preferred_element_type=jnp.float32)
+
+
+def dot_tn(a, b):
+    return lax.dot_general(a, b, (((0,), (0,)), ((), ())), preferred_element_type=jnp.float32)
+
+
+def segment_columns(seg):
+    lines = jnp.broadcast_to(seg.astype(jnp.float32), (16, seg.shape[1])).astype(jnp.bfloat16)
+    pick = (lax.broadcasted_iota(jnp.int32, (16, 128), 0) == 0).astype(jnp.float32).astype(jnp.bfloat16)
+    return dot_tn(lines, pick)
+
+
+def rotary_into(seg, cos_ref, sin_ref):
+    seq = seg.shape[1]
+    ids = segment_columns(seg)
+    first = jnp.zeros((seq, 128), jnp.float32)
+    row = seg.astype(jnp.float32)
+    for s in range(1, 16):
+        before = jnp.sum(jnp.where(row < s, 1.0, 0.0), axis=1, keepdims=True)
+        first = jnp.where(ids == s, before, first)
+    position = lax.broadcasted_iota(jnp.int32, (seq, 128), 0).astype(jnp.float32) - first
+    lane = lax.broadcasted_iota(jnp.int32, (1, 128), 1)
+    upper = lane >= HEAD_PAD // 2
+    index = jnp.where(upper, lane - HEAD_PAD // 2, lane)
+    freqs = jnp.exp(index.astype(jnp.float32) * (-2.0 * math.log(10000.0) / HEAD))
+    freqs = jnp.where(index < HEAD // 2, freqs, 0.0)
+    angles = position * freqs
+    cos_ref[...] = jnp.cos(angles)
+    sin_ref[...] = jnp.where(upper, jnp.sin(angles), -jnp.sin(angles))
+
+
+class Ring4:
+    def __init__(self):
+        mp = lax.axis_index("mp")
+        chip, core = lax.div(mp, 2), lax.rem(mp, 2)
+        self.me = mp
+        self.core = 2 * chip + 1 - core
+        self.chip = 2 * (1 - chip) + core
+        self.far = 2 * (1 - chip) + 1 - core
+
+
+def block_rows(index):
+    return pl.ds(pl.multiple_of(index * BLOCK_SEQ, BLOCK_SEQ), BLOCK_SEQ)
+
+
+class Gather:
+    def __init__(self, ring, rows, sems):
+        def copy(block, device, which):
+            return pltpu.make_async_remote_copy(
+                src_ref=rows.at[block_rows(block), :],
+                dst_ref=rows.at[block_rows(block), :],
+                send_sem=sems.at[0, which],
+                recv_sem=sems.at[1, which],
+                device_id={"mp": device},
+                device_id_type=MESH,
+            )
+
+        self.near = lambda: copy(ring.me, ring.core, 0)
+        self.across = lambda: copy(ring.me, ring.chip, 1)
+        self.onward = lambda: copy(ring.chip, ring.core, 2)
+
+    def forward(self):
+        self.across().wait_recv()
+        self.onward().start()
+
+    def finish(self):
+        self.onward().wait()
+
+
+class Scatter:
+    def __init__(self, ring, send_core, recv_core, send_chip, recv_chip, sems):
+        self.bufs = (send_core, recv_core, send_chip, recv_chip)
+
+        def copy(source, target, device, which):
+            return pltpu.make_async_remote_copy(
+                src_ref=source,
+                dst_ref=target,
+                send_sem=sems.at[0, which],
+                recv_sem=sems.at[1, which],
+                device_id={"mp": device},
+                device_id_type=MESH,
+            )
+
+        self.far = lambda: copy(send_core.at[0], recv_core.at[0], ring.core, 0)
+        self.core = lambda: copy(send_core.at[1], recv_core.at[1], ring.core, 1)
+        self.chip = lambda: copy(send_chip, recv_chip, ring.chip, 2)
+
+
+def greet_mp(ring, barrier):
+    for device in (ring.core, ring.chip):
+        pl.semaphore_signal(barrier, inc=1, device_id={"mp": device}, device_id_type=MESH)
+    return 2
+
+
+def norm_rows(values):
+    inverse = lax.rsqrt(jnp.mean(values * values, -1, keepdims=True) + EPS)
+    return values * inverse, inverse
+
+
+def qkv_block(rows, weights, cos_ref, sin_ref, out, block):
+    at = block_rows(block)
+    turned = 2 * (weights.shape[1] // 3) // 256
+    tiles = weights.shape[1] // 256
+
+    def one(n, turn):
+        cols = pl.ds(pl.multiple_of(n * 256, 256), 256)
+        value = dot(rows[at, :], weights[:, cols])
+        if turn:
+            cosine, sine = cos_ref[at, :], sin_ref[at, :]
+            halves = [value[:, j * 128 : j * 128 + 128] for j in range(2)]
+            value = jnp.concatenate([h * cosine + pltpu.roll(h, 64, 1) * sine for h in halves], axis=1)
+        out[at, cols] = value.astype(jnp.bfloat16)
+
+    @pl.loop(0, turned)
+    def _(n):
+        one(n, True)
+
+    @pl.loop(turned, tiles)
+    def _(n):
+        one(n, False)
+
+
+def masks_into(seg, ids_ref, bias_ref):
+    seq = seg.shape[1]
+    for i in range(seq // BLOCK_SEQ):
+        low = max(0, i * BLOCK_SEQ - SPAN)
+        high = (i + 1) * BLOCK_SEQ
+        shape = (BLOCK_SEQ, high - low)
+        query = i * BLOCK_SEQ + lax.broadcasted_iota(jnp.int32, shape, 0)
+        key = low + lax.broadcasted_iota(jnp.int32, shape, 1)
+        ids = ids_ref[pl.ds(i * BLOCK_SEQ, BLOCK_SEQ), :][:, :1]
+        same = ids == seg[:, low:high].astype(jnp.float32)
+        bias_ref[pl.ds(i * BLOCK_SEQ, BLOCK_SEQ), pl.ds(0, high - low)] = jnp.where((query >= key) & same, 0.0, MASKED).astype(bias_ref.dtype)
+
+
+def attend_all(qkv, out, bias_ref, heads, scale):
+    seq = qkv.shape[0]
+    width = heads * HEAD_PAD
+
+    @pl.loop(0, heads)
+    def _(h):
+        lanes = [pl.ds(pl.multiple_of(part * width + h * HEAD_PAD, HEAD_PAD), HEAD_PAD) for part in range(3)]
+        for i in range(seq // BLOCK_SEQ):
+            low, high = max(0, i * BLOCK_SEQ - SPAN), (i + 1) * BLOCK_SEQ
+            rows, keys = pl.ds(i * BLOCK_SEQ, BLOCK_SEQ), pl.ds(low, high - low)
+            scores = dot_nt(qkv[rows, lanes[0]], qkv[keys, lanes[1]]) + bias_ref[rows, pl.ds(0, high - low)]
+            top = jnp.max(scores, -1, keepdims=True)
+            expo = jnp.exp((scores - top) * scale)
+            probs = expo * (1.0 / jnp.sum(expo, -1, keepdims=True))
+            out[rows, lanes[0]] = dot(probs.astype(jnp.bfloat16), qkv[keys, lanes[2]]).astype(jnp.bfloat16)
+
+
+def front_kernel(
+    x, g, seg, gain, wq, wk, wv, wo,
+    resid_o, h1_o, grow_o, qkv_o, mix_o, wqkv_o, wout_o, cos_o, sin_o,
+    rows_one, rows_g, qkv, mixed, raw, raw_out, wqkv, wout, cos_ref, sin_ref, ids_ref, bias_ref,
+    send_core, recv_core, send_chip, recv_chip, load_sem, save_sem, one_sem, g_sem, rs_sem,
 ):
-    width = rows.shape[1]
-    local = outg.shape[0]
-    hidden = down.shape[0]
+    ring = Ring4()
+    local, width = wo.shape
+    padded = wout.shape[0]
+    heads = local // HEAD
+    barrier = pltpu.get_barrier_semaphore()
+    count = greet_mp(ring, barrier)
+    loads = [pltpu.make_async_copy(w, raw.at[i], load_sem.at[i]) for i, w in enumerate((wq, wk, wv))]
+    loads.append(pltpu.make_async_copy(wo, raw_out, load_sem.at[3]))
+    own_g = pltpu.make_async_copy(g, rows_g.at[block_rows(ring.me), :], load_sem.at[4])
+    for load in loads:
+        load.start()
+    own_g.start()
+    values, _ = norm_rows(x[...].astype(jnp.float32))
+    rows_one[block_rows(ring.me), :] = (values * gain[...]).astype(jnp.bfloat16)
+    pl.semaphore_wait(barrier, count)
+    one, all_g = Gather(ring, rows_one, one_sem), Gather(ring, rows_g, g_sem)
+    scatter = Scatter(ring, send_core, recv_core, send_chip, recv_chip, rs_sem)
+    one.across().start()
+    one.near().start()
+    spread = pad_matrix(local, padded, False)
+    for i, load in enumerate(loads[:3]):
+        load.wait()
+        wqkv[:, pl.ds(i * padded, padded)] = dot(raw[i], spread).astype(jnp.bfloat16)
+    loads[3].wait()
+    wout[...] = dot(pad_matrix(local, padded, True), raw_out[...]).astype(jnp.bfloat16)
+    own_g.wait()
+    ids_ref[...] = segment_columns(seg[...])
+    rotary_into(seg[...], cos_ref, sin_ref)
+    qkv_block(rows_one, wqkv, cos_ref, sin_ref, qkv, ring.me)
+    one.near().wait_recv()
+    qkv_block(rows_one, wqkv, cos_ref, sin_ref, qkv, ring.core)
+    masks_into(seg[...], ids_ref, bias_ref)
+    one.forward()
+    one.across().wait_send()
+    all_g.across().start()
+    all_g.near().start()
+    qkv_block(rows_one, wqkv, cos_ref, sin_ref, qkv, ring.chip)
+    one.onward().wait_recv()
+    qkv_block(rows_one, wqkv, cos_ref, sin_ref, qkv, ring.far)
+    attend_all(qkv, mixed, bias_ref, heads, 1.0 / math.sqrt(HEAD))
+    saves = [
+        pltpu.make_async_copy(source, target, save_sem.at[i])
+        for i, (source, target) in enumerate(
+            ((rows_one, h1_o), (qkv, qkv_o), (mixed, mix_o), (wqkv, wqkv_o), (wout, wout_o), (cos_ref, cos_o), (sin_ref, sin_o), (rows_g, grow_o))
+        )
+    ]
+    for save in saves[:7]:
+        save.start()
+
+    def term(block):
+        return dot(mixed[block_rows(block), :], wout[...])
+
+    send_core[0] = term(ring.far).astype(jnp.bfloat16)
+    scatter.far().start()
+    send_core[1] = term(ring.core).astype(jnp.bfloat16)
+    scatter.core().start()
+    chip_term = term(ring.chip)
+    scatter.far().wait_recv()
+    send_chip[...] = (chip_term + recv_core[0].astype(jnp.float32)).astype(jnp.bfloat16)
+    scatter.chip().start()
+    all_g.forward()
+    own = x[...].astype(jnp.float32) + term(ring.me)
+    scatter.core().wait_recv()
+    own = own + recv_core[1].astype(jnp.float32)
+    all_g.near().wait_recv()
+    all_g.onward().wait_recv()
+    saves[7].start()
+    scatter.chip().wait_recv()
+    resid_o[...] = own + recv_chip[...].astype(jnp.float32)
+    for gather in (one, all_g):
+        gather.near().wait_send()
+        gather.onward().wait_send()
+    all_g.across().wait_send()
+    one_done = (scatter.far(), scatter.core(), scatter.chip())
+    for copy in one_done:
+        copy.wait_send()
+    for save in saves:
+        save.wait()
+
+
+def front(x, g, seg, gain, wq, wk, wv, wo):
+    bf, f32 = jnp.bfloat16, jnp.float32
+    local, width = wo.shape
+    padded = local // HEAD * HEAD_PAD
+    seq, rows = seg.shape[1], x.shape[0]
+    shapes = [((rows, width), f32), ((seq, width), bf), ((seq, width), bf), ((seq, 3 * padded), bf), ((seq, padded), bf), ((width, 3 * padded), bf), ((padded, width), bf), ((seq, 128), f32), ((seq, 128), f32)]
+    vm, hbm = pl.BlockSpec(memory_space=pltpu.VMEM), pl.BlockSpec(memory_space=pl.ANY)
+    sem = pltpu.SemaphoreType.DMA
+    return pl.pallas_call(
+        front_kernel,
+        out_shape=[jax.ShapeDtypeStruct(s, d) for s, d in shapes],
+        in_specs=[vm, vm, vm, vm, hbm, hbm, hbm, hbm],
+        out_specs=[vm] + [hbm] * 8,
+        scratch_shapes=[
+            pltpu.VMEM((seq, width), bf), pltpu.VMEM((seq, width), bf), pltpu.VMEM((seq, 3 * padded), bf), pltpu.VMEM((seq, padded), bf),
+            pltpu.VMEM((3, width, local), bf), pltpu.VMEM((local, width), bf), pltpu.VMEM((width, 3 * padded), bf), pltpu.VMEM((padded, width), bf),
+            pltpu.VMEM((seq, 128), f32), pltpu.VMEM((seq, 128), f32), pltpu.VMEM((seq, 128), f32), pltpu.VMEM((seq, SPAN + BLOCK_SEQ), f32),
+            pltpu.VMEM((2, rows, width), bf), pltpu.VMEM((2, rows, width), bf), pltpu.VMEM((rows, width), bf), pltpu.VMEM((rows, width), bf),
+            sem((5,)), sem((8,)), sem((2, 3)), sem((2, 3)), sem((2, 3)),
+        ],
+        compiler_params=pltpu.CompilerParams(collective_id=1, has_side_effects=True, vmem_limit_bytes=60 * 2**20),
+    )(x, g, seg, gain.reshape(1, -1), wq, wk, wv, wo)
+
+
+def gelu_parts(u):
+    tangent = jnp.tanh(GELU_C * (u + GELU_K * u * u * u))
+    return tangent
+
+
+def tail_kernel(
+    x, resid, seg, gain_one, gain_two, wup, wdown, h1, grow, qkv_in, mix_in, wqkv_in, wout_in, cos_in, sin_in,
+    result_o, input_o, gains_o, down_o, up_o, out_o, q_o, k_o, v_o,
+    rows, b0, b1, b2, b3, b4, b5, send_sem, recv_sem, stage, stage_sem, tstage, tsem,
+    w_up, w_down, w_qkv, w_out, rows_one, rows_g, rows_two, hidden, grad_up, branch, qkv, mixed, grad_mixed,
+    cos_ref, sin_ref, bias_ref, term_ref, key_sum, value_sum,
+    send_core, recv_core, send_chip, recv_chip, gain_acc, gain_recv,
+    load_sem, two_sem, branch_sem, rs_sem, rs2_sem, rs3_sem, gain_sem, free_sem,
+):
+    bf, f32 = jnp.bfloat16, jnp.float32
+    ring = Ring4()
+    seq, width = rows_two.shape
+    units = w_up.shape[1]
+    padded = w_out.shape[0]
+    heads = padded // HEAD_PAD
+    local = heads * HEAD
     pairs = rows.shape[0] // (2 * CHUNK)
+    scale = 1.0 / math.sqrt(HEAD)
     red = Reducer(rows, (b0, b1, b2, b3, b4, b5), send_sem, recv_sem, pairs)
     barrier = pltpu.get_barrier_semaphore()
-    count = red.greet(barrier)
-    loads, at = [], 0
-    for i, source in enumerate((down, up, outg, qg, kg, vg)):
-        loads.append(pltpu.make_async_copy(source, rows.at[pl.ds(at, source.shape[0]), :], load_sem.at[i]))
-        at += source.shape[0]
-    for load in loads:
+    count = greet_mp(ring, barrier) + red.greet(barrier)
+    places = ((wup, w_up), (grow, rows_g), (wdown, w_down), (mix_in, mixed), (wout_in, w_out), (cos_in, cos_ref), (sin_in, sin_ref), (qkv_in, qkv), (wqkv_in, w_qkv), (h1, rows_one))
+    loads = [pltpu.make_async_copy(source, target, load_sem.at[i]) for i, (source, target) in enumerate(places)]
+    loads[0].start()
+    loads[1].start()
+    normed, _ = norm_rows(resid[...])
+    rows_two[block_rows(ring.me), :] = (normed * gain_two[...]).astype(bf)
+    pl.semaphore_wait(barrier, count)
+    two, all_branch = Gather(ring, rows_two, two_sem), Gather(ring, branch, branch_sem)
+    first = Scatter(ring, send_core, recv_core, send_chip, recv_chip, rs_sem)
+    second = Scatter(ring, send_core, recv_core, send_chip, recv_chip, rs2_sem)
+    third = Scatter(ring, send_core, recv_core, send_chip, recv_chip, rs3_sem)
+    two.across().start()
+    two.near().start()
+    for load in loads[2:]:
         load.start()
-    pl.semaphore_wait(barrier, count)
-    for load in loads:
-        load.wait()
-
-    def put(pair, target, base, count=2 * CHUNK):
+
+    base = 2 * units
+    down_pairs = units // (2 * CHUNK)
+    whole_out = local // (2 * CHUNK)
+    plain = 2 * down_pairs + whole_out
+
+    def put(pair, target, row, many=2 * CHUNK):
         slot = lax.rem(pair, 2)
         return pltpu.make_async_copy(
-            stage.at[slot, pl.ds(0, count), :], target.at[pl.ds(pl.multiple_of(base, CHUNK), count), :], stage_sem.at[slot]
+            stage.at[slot, pl.ds(0, many), :], target.at[pl.ds(pl.multiple_of(row, CHUNK), many), :], stage_sem.at[slot]
         )
 
-    down_pairs = hidden // (2 * CHUNK)
-
-    def out_pair(pair, first):
-        slot = lax.rem(pair, 2)
-
+    def out_pair(pair):
         @pl.when(pair >= 2)
         def _():
             put(pair, down_o, 0).wait()
 
-        stage[slot] = rows[pl.ds(pl.multiple_of(pair * 2 * CHUNK, 2 * CHUNK), 2 * CHUNK), :].astype(jnp.float32)
+        stage[lax.rem(pair, 2)] = rows[pl.ds(pl.multiple_of(pair * 2 * CHUNK, 2 * CHUNK), 2 * CHUNK), :].astype(f32)
 
         @pl.when(pair < down_pairs)
         def _():
@@ -389,78 +696,310 @@
         def _():
             put(pair, out_o, (pair - 2 * down_pairs) * 2 * CHUNK).start()
 
-    whole_out = local // (2 * CHUNK)
-    plain = 2 * down_pairs + whole_out
-
-    def step(index, carry):
+    def slot(index):
         red.slot(index)
-        pair = index - 5
+        pair = index - (STAGES - 1)
 
         @pl.when((pair >= 0) & (pair < plain))
         def _():
-            out_pair(pair, 0)
-
-        return carry
-
-    lax.fori_loop(0, pairs + STAGES - 1, step, 0)
-    left = local - whole_out * 2 * CHUNK
-    base = 2 * hidden
+            out_pair(pair)
+
+    def tile(n):
+        return pl.ds(pl.multiple_of(n * 256, 256), 256)
+
+    def up_block(block):
+        @pl.loop(0, units // 256)
+        def _(n):
+            u = dot(rows_two[block_rows(block), :], w_up[:, tile(n)])
+            tangent = jnp.tanh(GELU_C * (u + GELU_K * u * u * u))
+            hidden[block_rows(block), tile(n)] = (0.5 * u * (1.0 + tangent)).astype(bf)
+
+    loads[0].wait()
+    up_block(ring.me)
+    two.near().wait_recv()
+    up_block(ring.core)
+    key_sum[...] = segment_columns(seg[...])
+    masks_into(seg[...], key_sum, bias_ref)
+    two.forward()
+    up_block(ring.chip)
+    two.onward().wait_recv()
+    up_block(ring.far)
+    loads[1].wait()
+
+    @pl.loop(0, units // 256)
+    def _(i):
+        rows[tile(i), :] = dot_tn(hidden[:, tile(i)], rows_g[...]).astype(bf)
+        slot(i)
+
+    loads[2].wait()
+
+    def order(k):
+        there = k < 2
+        chip = lax.div(ring.me, 2)
+        core = lax.rem(ring.me, 2)
+        flip = 1 - lax.rem(k, 2)
+        to_chip = jnp.where(there, 1 - chip, chip)
+        to_core = jnp.where(flip == 1, 1 - core, core)
+        return 2 * to_chip + to_core
+
+    def hand_on(k, scatter, start):
+        @pl.when(k == 0)
+        def _():
+            send_core[0] = term_ref[...].astype(bf)
+            scatter.far().start()
+
+        @pl.when(k == 1)
+        def _():
+            scatter.far().wait_recv()
+            send_chip[...] = (term_ref[...] + recv_core[0].astype(f32)).astype(bf)
+            scatter.chip().start()
+
+        @pl.when(k == 2)
+        def _():
+            send_core[1] = term_ref[...].astype(bf)
+            scatter.core().start()
+
+        @pl.when(k == 3)
+        def _():
+            scatter.core().wait_recv()
+            term_ref[...] = term_ref[...] + recv_core[1].astype(f32)
+
+    def settle(scatter):
+        for copy in (scatter.far(), scatter.core()):
+            copy.wait_send()
+        scatter.chip().wait()
+        return term_ref[...] + recv_chip[...].astype(f32)
+
+    @pl.loop(0, 4)
+    def _(k):
+        at = block_rows(order(k))
+
+        @pl.loop(0, units // 256)
+        def _(n):
+            u = dot(rows_two[at, :], w_up[:, tile(n)])
+            upstream = dot_nt(rows_g[at, :], w_down[tile(n), :])
+            tangent = jnp.tanh(GELU_C * (u + GELU_K * u * u * u))
+            slope = 0.5 * (1.0 + tangent) + 0.5 * u * (1.0 - tangent * tangent) * GELU_C * (1.0 + 3.0 * GELU_K * u * u)
+            grad_up[at, tile(n)] = (upstream * slope).astype(bf)
+
+        @pl.loop(0, width // 256)
+        def _(n):
+            term_ref[:, tile(n)] = dot_nt(grad_up[at, :], w_up[tile(n), :])
+
+        hand_on(k, first, None)
+        slot(5 + k)
+
+    def up_rows(i):
+        rows[pl.ds(pl.multiple_of(units + i * 256, 256), 256), :] = dot_tn(rows_two[:, tile(i)], grad_up[...]).astype(bf)
+
+    @pl.loop(0, 2)
+    def _(i):
+        up_rows(i)
+        slot(9 + i)
+
+    grad_two = settle(first)
+    normed, inverse = norm_rows(resid[...])
+    scaled = grad_two * gain_two[...]
+    part = inverse * (scaled - normed * jnp.mean(scaled * normed, -1, keepdims=True))
+    mlp_part = jnp.sum(grad_two * normed, axis=0, keepdims=True)
+    gain_acc[0] = jnp.zeros(gain_acc.shape[1:], f32)
+    gain_acc[0, 1:2, :] = mlp_part
+    mine = rows_g[block_rows(ring.me), :].astype(f32) + part
+    input_o[...] = mine
+    branch[block_rows(ring.me), :] = mine.astype(bf)
+    all_branch.across().start()
+    all_branch.near().start()
+
+    @pl.loop(2, units // 256)
+    def _(i):
+        up_rows(i)
+        slot(9 + i)
+
+    for load in loads[3:]:
+        load.wait()
+    all_branch.near().wait_recv()
+    all_branch.forward()
+    all_branch.onward().wait_recv()
+
+    def head_rows(left, lane, right, row):
+        value = dot_tn(left[:, lane], right[...])
+        halves = [value[at : at + HEAD // 2, :] for at in (0, 64, 128, 192)]
+        rows[pl.ds(pl.multiple_of(row, 16), 2 * HEAD), :] = jnp.concatenate(halves, axis=0).astype(bf)
+
+    @pl.loop(0, heads // 2)
+    def _(j):
+        head_rows(mixed, tile(j), branch, base + j * 2 * HEAD)
+
+    @pl.loop(0, 4)
+    def _(b):
+        grad_mixed[block_rows(b), :] = dot_nt(branch[block_rows(b), :], w_out[...]).astype(bf)
+
+    @pl.loop(0, heads)
+    def _(h):
+        lanes = [pl.ds(pl.multiple_of(n * padded + h * HEAD_PAD, HEAD_PAD), HEAD_PAD) for n in range(3)]
+        key_sum[...] = jnp.zeros_like(key_sum)
+        value_sum[...] = jnp.zeros_like(value_sum)
+        for i in range(seq // BLOCK_SEQ):
+            low, high = max(0, i * BLOCK_SEQ - SPAN), (i + 1) * BLOCK_SEQ
+            at, keys = pl.ds(i * BLOCK_SEQ, BLOCK_SEQ), pl.ds(low, high - low)
+            query, upstream = qkv[at, lanes[0]], grad_mixed[at, lanes[0]]
+            scores = dot_nt(query, qkv[keys, lanes[1]]) + bias_ref[at, pl.ds(0, high - low)]
+            top = jnp.max(scores, -1, keepdims=True)
+            expo = jnp.exp((scores - top) * scale)
+            probs = expo * (1.0 / jnp.sum(expo, -1, keepdims=True))
+            grad_probs = dot_nt(upstream, qkv[keys, lanes[2]])
+            inner = jnp.sum(probs * grad_probs, -1, keepdims=True)
+            grad_scores = (probs * (grad_probs - inner)).astype(bf)
+            value_sum[keys, :] += dot_tn(probs.astype(bf), upstream)
+            key_sum[keys, :] += dot_tn(grad_scores, query)
+            turned = dot(grad_scores, qkv[keys, lanes[1]]) * scale
+            qkv[at, lanes[0]] = (turned * cos_ref[at, :] - pltpu.roll(turned, 64, 1) * sin_ref[at, :]).astype(bf)
+            if i == 1:
+                slot(14 + 2 * h)
+        turned = key_sum[...] * scale
+        qkv[:, lanes[1]] = (turned * cos_ref[...] - pltpu.roll(turned, 64, 1) * sin_ref[...]).astype(bf)
+        qkv[:, lanes[2]] = value_sum[...].astype(bf)
+        at = block_rows(order(h))
+
+        @pl.loop(0, width // 256)
+        def _(n):
+            term_ref[:, tile(n)] = dot(hidden[at, :], w_down[:, tile(n)])
+
+        hand_on(h, second, None)
+        slot(15 + 2 * h)
+
+    @pl.loop(0, 3)
+    def _(part):
+        for j in range(heads // 2):
+            lane = pl.ds(pl.multiple_of(part * padded + j * 256, 256), 256)
+            head_rows(qkv, lane, rows_one, base + (part + 1) * local + j * 2 * HEAD)
+        slot(22 + part)
+
+    result_o[...] = (resid[...] + settle(second)).astype(bf)
+    for device in (ring.core, ring.chip):
+        pl.semaphore_signal(free_sem, inc=1, device_id={"mp": device}, device_id_type=MESH)
+    pl.semaphore_wait(free_sem, 2)
+
+    @pl.loop(0, 4)
+    def _(k):
+        at = block_rows(order(k))
+
+        @pl.loop(0, width // 256)
+        def _(n):
+            term_ref[:, tile(n)] = dot_nt(qkv[at, :], w_qkv[tile(n), :])
+
+        hand_on(k, third, None)
+        slot(25 + k)
+
+    eye = jnp.where(
+        lax.broadcasted_iota(jnp.int32, (256, 256), 0) == lax.broadcasted_iota(jnp.int32, (256, 256), 1), 1.0, 0.0
+    ).astype(bf)
+
+    def tput(n, target):
+        return pltpu.make_async_copy(tstage.at[lax.rem(n, 2)], target.at[tile(n), :], tsem.at[lax.rem(n, 2)])
+
+    def turn_out(part, target):
+        row = base + local * (part + 1)
+
+        @pl.loop(0, width // 256)
+        def _(n):
+            @pl.when(n >= 2)
+            def _():
+                tput(n, target).wait()
+
+            tstage[lax.rem(n, 2)] = dot_nt(eye, rows[pl.ds(row, local), tile(n)])
+            tput(n, target).start()
+
+        for n in (width // 256 - 2, width // 256 - 1):
+            tput(n, target).wait()
+
+    slot(29)
+    grad_one = settle(third)
+    normed, inverse = norm_rows(x[...].astype(f32))
+    scaled = grad_one * gain_one[...]
+    input_o[...] = input_o[...] + inverse * (scaled - normed * jnp.mean(scaled * normed, -1, keepdims=True))
+    gain_acc[0, 0:1, :] = jnp.sum(grad_one * normed, axis=0, keepdims=True)
+
+    def exchange(step):
+        names = ({"mp": ring.core}, {"mp": ring.chip}, {"dp": red.twin}, {"dp": red.mate}, {"dp": red.across})
+        return pltpu.make_async_remote_copy(
+            src_ref=gain_acc.at[step], dst_ref=gain_recv.at[step], send_sem=gain_sem.at[0, step], recv_sem=gain_sem.at[1, step],
+            device_id=names[step], device_id_type=MESH,
+        )
+
+    last = pairs + STAGES - 1
+
+    @pl.loop(30, last)
+    def _(index):
+        for step in range(5):
+
+            @pl.when(index == 30 + step)
+            def _():
+                if step:
+                    exchange(step - 1).wait_recv()
+                    gain_acc[step] = gain_acc[step - 1] + gain_recv[step - 1]
+                exchange(step).start()
+
+        slot(index)
+
+        @pl.when(index == 30)
+        def _():
+            turn_out(0, q_o)
+
+        @pl.when(index == 33)
+        def _():
+            turn_out(1, k_o)
+
+    exchange(4).wait_recv()
+    gains_o[...] = gain_acc[4] + gain_recv[4]
+    turn_out(2, v_o)
     for pair in (plain, plain + 1):
         put(pair, down_o, 0).wait()
+    left = local - whole_out * 2 * CHUNK
     if left:
-        stage[0, pl.ds(0, left), :] = rows[pl.ds(base + whole_out * 2 * CHUNK, left), :].astype(jnp.float32)
+        stage[0, pl.ds(0, left), :] = rows[pl.ds(base + whole_out * 2 * CHUNK, left), :].astype(f32)
         put(0, out_o, whole_out * 2 * CHUNK, left).start()
         put(0, out_o, whole_out * 2 * CHUNK, left).wait()
-    block = 256
-    eye = (lax.broadcasted_iota(jnp.int32, (block, block), 0) == lax.broadcasted_iota(jnp.int32, (block, block), 1)).astype(jnp.bfloat16)
-    copies = []
-    n = 0
-    for i, target in enumerate((q_o, k_o, v_o)):
-        row = base + local * (i + 1)
-        for b in range(width // block):
-            slot = n % 2
-            if n >= 2:
-                copies[n - 2].wait()
-            tstage[slot] = lax.dot_general(
-                eye, rows[pl.ds(row, local), pl.ds(b * block, block)], (((1,), (1,)), ((), ())), preferred_element_type=jnp.float32
-            )
-            c = pltpu.make_async_copy(tstage.at[slot], target.at[pl.ds(b * block, block), :], tsem.at[slot])
-            c.start()
-            copies.append(c)
-            n += 1
-    copies[-2].wait()
-    copies[-1].wait()
-
-
-def reduce_grads(down, up, outg, qg, kg, vg):
-    local, width = outg.shape
-    hidden = down.shape[0]
-    total = 2 * hidden + 4 * local
-    f32 = jnp.float32
-    shapes = [(hidden, width), (hidden, width), (local, width)] + [(width, local)] * 3
+    for step in range(5):
+        exchange(step).wait_send()
+    for gather in (two, all_branch):
+        gather.near().wait_send()
+        gather.across().wait_send()
+        gather.onward().wait_send()
+
+
+def tail(x, resid, seg, gain_one, gain_two, wup, wdown, h1, grow, qkv, mixed, wqkv, wout, cos, sin):
+    bf, f32 = jnp.bfloat16, jnp.float32
+    own, width = x.shape
+    units = wup.shape[1]
+    seq = seg.shape[1]
+    padded = wout.shape[0]
+    local = padded // HEAD_PAD * HEAD
+    total = 2 * units + 4 * local
+    vm, hbm = pl.BlockSpec(memory_space=pltpu.VMEM), pl.BlockSpec(memory_space=pl.ANY)
+    sem = pltpu.SemaphoreType.DMA
+    shapes = [((own, width), bf), ((own, width), f32), ((8, width), f32), ((units, width), f32), ((width, units), f32), ((local, width), f32)] + [((width, local), f32)] * 3
+    tall = pltpu.VMEM((seq, width), bf)
     return pl.pallas_call(
-        reduce_kernel,
-        out_shape=[jax.ShapeDtypeStruct(s, f32) for s in shapes],
-        in_specs=[pl.BlockSpec(memory_space=pl.ANY)] * 6,
-        out_specs=[pl.BlockSpec(memory_space=pl.ANY)] * 6,
-        scratch_shapes=[pltpu.VMEM((total, width), jnp.bfloat16)]
+        tail_kernel,
+        out_shape=[jax.ShapeDtypeStruct(s, d) for s, d in shapes],
+        in_specs=[vm] * 5 + [hbm] * 10,
+        out_specs=[vm] * 3 + [hbm] * 6,
+        scratch_shapes=[pltpu.VMEM((total, width), bf)]
         + reducer_scratch(width)
         + [
-            pltpu.VMEM((2, 2 * CHUNK, width), f32),
-            pltpu.SemaphoreType.DMA((2,)),
-            pltpu.SemaphoreType.DMA((6,)),
-            pltpu.VMEM((2, 256, local), f32),
-            pltpu.SemaphoreType.DMA((2,)),
+            pltpu.VMEM((2, 2 * CHUNK, width), f32), sem((2,)), pltpu.VMEM((2, 256, local), f32), sem((2,)),
+            pltpu.VMEM((width, units), bf), pltpu.VMEM((units, width), bf), pltpu.VMEM((width, 3 * padded), bf), pltpu.VMEM((padded, width), bf),
+            tall, tall, tall, pltpu.VMEM((seq, units), bf), pltpu.VMEM((seq, units), bf), tall,
+            pltpu.VMEM((seq, 3 * padded), bf), pltpu.VMEM((seq, padded), bf), pltpu.VMEM((seq, padded), bf),
+            pltpu.VMEM((seq, 128), f32), pltpu.VMEM((seq, 128), f32), pltpu.VMEM((seq, SPAN + BLOCK_SEQ), bf),
+            pltpu.VMEM((own, width), f32), pltpu.VMEM((seq, HEAD_PAD), f32), pltpu.VMEM((seq, HEAD_PAD), f32),
+            pltpu.VMEM((2, own, width), bf), pltpu.VMEM((2, own, width), bf), pltpu.VMEM((own, width), bf), pltpu.VMEM((own, width), bf),
+            pltpu.VMEM((5, 8, width), f32), pltpu.VMEM((5, 8, width), f32),
+            sem((10,)), sem((2, 3)), sem((2, 3)), sem((2, 3)), sem((2, 3)), sem((2, 3)), sem((2, 5)), pltpu.SemaphoreType.REGULAR,
         ],
-        compiler_params=pltpu.CompilerParams(collective_id=0, has_side_effects=True, vmem_limit_bytes=40 * 2**20),
-    )(down, up, outg, qg, kg, vg)
-
-
-def reduce_all(parts):
-    if lax.axis_size("dp") == 8:
-        return reduce_grads(*parts)
-    sums = [part.astype(jnp.float32) for part in lax.psum(parts, "dp")]
-    return sums[:3] + [part.T for part in sums[3:]]
+        compiler_params=pltpu.CompilerParams(collective_id=2, has_side_effects=True, vmem_limit_bytes=67043328),
+    )(x, resid, seg, gain_one.reshape(1, -1), gain_two.reshape(1, -1), wup, wdown, h1, grow, qkv, mixed, wqkv, wout, cos, sin)
 
 
 def on_device(
@@ -513,17 +1052,17 @@
     result = (resid + mlp_share).astype(jnp.bfloat16)
     grad_top = out_cotangent.astype(jnp.float32)
     grad_rows = lax.all_gather(out_cotangent, "mp", axis=1, tiled=True)
-    down_total = weight_grad(hidden, grad_rows).astype(jnp.bfloat16)
+    down_total = weight_grad(hidden, grad_rows)
     grad_hidden = project_back(grad_rows, down_weight)
     grad_up_pre = (grad_hidden * gelu_slope(up_pre)).astype(jnp.bfloat16)
-    up_total = weight_grad(rows_two, grad_up_pre).astype(jnp.bfloat16)
+    up_total = weight_grad(rows_two, grad_up_pre)
     grad_two = lax.psum_scatter(
         project_back(grad_up_pre, up_weight), "mp", scatter_dimension=1, tiled=True
     )
     resid_part, mlp_gain_part = norm_back(grad_two, normed_two, inverse_two, mlp_gain)
     grad_resid = grad_top + resid_part
     branch_rows = lax.all_gather(grad_resid.astype(jnp.bfloat16), "mp", axis=1, tiled=True)
-    out_total = weight_grad(mixed, branch_rows).astype(jnp.bfloat16)
+    out_total = weight_grad(mixed, branch_rows)
     grad_mixed = project_back(branch_rows, out_weight).astype(jnp.bfloat16).reshape(head_shape)
     row_index = 0
     grad_q, grad_k, grad_v = attend_back(
@@ -552,10 +1091,9 @@
     grad_value = (
         jnp.stack(value_rows, 0).astype(jnp.bfloat16).reshape(row_count, seq_len, local_width)
     )
-    bf = jnp.bfloat16
-    query_total = weight_grad(grad_query, rows_one).astype(bf)
-    key_total = weight_grad(grad_key, rows_one).astype(bf)
-    value_total = weight_grad(grad_value, rows_one).astype(bf)
+    query_total = weight_grad(rows_one, grad_query)
+    key_total = weight_grad(rows_one, grad_key)
+    value_total = weight_grad(rows_one, grad_value)
     grad_terms = (
         project_back(grad_query, query_weight)
         + project_back(grad_key, key_weight)
@@ -564,9 +1102,28 @@
     grad_one = lax.psum_scatter(grad_terms, "mp", scatter_dimension=1, tiled=True)
     input_part, attn_gain_part = norm_back(grad_one, normed_one, inverse_one, attn_gain)
     input_grad = grad_resid + input_part
-    attn_gain_part, mlp_gain_part = lax.psum((attn_gain_part, mlp_gain_part), ("dp", "mp"))
-    down_total, up_total, out_total, query_total, key_total, value_total = reduce_all(
-        (down_total, up_total, out_total, query_total, key_total, value_total)
+    attn_gain_part, mlp_gain_part = lax.psum((attn_gain_part, mlp_gain_part), "mp")
+    (
+        query_total,
+        key_total,
+        value_total,
+        out_total,
+        attn_gain_part,
+        mlp_gain_part,
+        up_total,
+        down_total,
+    ) = lax.psum(
+        (
+            query_total,
+            key_total,
+            value_total,
+            out_total,
+            attn_gain_part,
+            mlp_gain_part,
+            up_total,
+            down_total,
+        ),
+        "dp",
     )
     return (
         result,
@@ -582,9 +1139,21 @@
     )
 
 
+def on_device_kernels(
+    hidden_in, segment_ids, attn_gain, query_weight, key_weight, value_weight, out_weight, mlp_gain, up_weight, down_weight, out_cotangent
+):
+    resid, h1, grow, qkv, mixed, wqkv, wout, cos, sin = front(
+        hidden_in[0], out_cotangent[0], segment_ids, attn_gain, query_weight, key_weight, value_weight, out_weight
+    )
+    result, input_grad, gains, down, up, out, query, key, value = tail(
+        hidden_in[0], resid, segment_ids, attn_gain, mlp_gain, up_weight, down_weight, h1, grow, qkv, mixed, wqkv, wout, cos, sin
+    )
+    return (result[None], input_grad[None], gains[0], query, key, value, out, gains[1], up, down)
+
+
 def solution(mesh):
     return jax.shard_map(
-        on_device,
+        on_device_kernels if mesh.shape["dp"] == 8 else on_device,
         mesh=mesh,
         in_specs=(
             P("dp", "mp", None),

time: 611 us -> 315 us (0.52); the launches traced: 601 us -> 314 us
  waiting for transfers between devices: 197 us -> 0 us
  matrix products: 97.1 us -> 0 us
  Pallas kernels: 191 us -> 285 us
  blocking collectives: 38.3 us -> 0 us
  other arithmetic: 29.6 us -> 0.01 us
  between operations: 15.4 us -> 0.69 us
    reduce_scatter x4 -> x0, waiting for transfers between devices: 102 us -> none  [the longest x1 51.4 us: on_device(): lax.psum_scatter(project_back(grad_up_pre, up_weight), 'mp', scatter_dime...]
    dot_general x30 -> x0, matrix products: 97.1 us -> none  [the longest x6 26.5 us: project(): jnp.einsum('rsd,de->rse', left, weight, preferred_element_type=jnp.float32)]
    pallas_call x1 -> x2, Pallas kernels: 191 us -> 285 us  [the longest x1 232 us: tail(): pl.pallas_call(tail_kernel, out_shape=[jax.ShapeDtypeStruct(s, d) for s,...]
    all_gather x4 -> x0, waiting for transfers between devices: 94.1 us -> none  [the longest x1 25.4 us: on_device(): lax.all_gather(grad_resid.astype(jnp.bfloat16), 'mp', axis=1, tiled=True)]
    psum x1 -> x0, blocking collectives: 38.3 us -> none  [on_device(): lax.psum((attn_gain_part, mlp_gain_part), ('dp', 'mp'))]
    reduce_sum x6 -> x0, other arithmetic: 11.3 us -> none  [the longest x2 4.38 us: norm_back(): jnp.sum(upstream * normed, axis=(0, 1))]
    convert_element_type x7 -> x0, other arithmetic: 9.13 us -> none  [the longest x2 4.58 us: attend_back(): grad_scores = (probs * (grad_probs - inner)).astype(jnp.bfloat16)]
    unnamed x124 -> x25, local copies, waits for them, and re-layouts: 30 us -> 24.3 us
  transfers between devices with their start and end apart: 8 -> 0, of which waited for: 6 -> 0; matrix products, arithmetic and copies ran while one was open for 8% -> 0% of each run, Pallas kernels for 32% -> 0%
where the time goes in v2:
time: 315 us; the launch traced here: 314 us
  Pallas kernels  285 us (90%)
  local copies, waits for them, and re-layouts  28.5 us (9%)
    pallas_call x1, Pallas kernels, tail(): pl.pallas_call(tail_kernel, out_shape=[jax.ShapeDtypeStruct(s, d) for s,...  232 us
    pallas_call x1, Pallas kernels, front(): pl.pallas_call(front_kernel, out_shape=[jax.ShapeDtypeStruct(s, d) for s,...  53.5 us
    unnamed x25, local copies, waits for them, and re-layouts  24.3 us

profile of v2, /device:TPU:0, one launch (start us, length us, event | category | flops | bytes accessed | tf_op | source)
XLA Modules:
  0.0 314.4 jit_solution(11494158300328848110)
XLA Ops:
  0.6 0.0 copy-start.4
  0.7 0.0 copy-start.3
  0.7 1.4 reshape.27.gain.gain_one
  2.1 1.3 reshape.28.gain_two
  3.4 2.2 copy.21.wq
  5.6 0.0 copy-done.3
  5.6 1.3 copy.22.wk
  6.9 0.0 copy-done.4
  6.9 1.3 copy.23.wv
  8.2 53.5 %shard_map.186 = (f32[256,1280]{1,0:T(8,128)}, bf16[1024,1280]{1,0:T(8,128)(2,1)}, bf16[1024,1280]{1,0:T(8,128)(2,1)}, bf16[1024,1536]{1,0:T(8,128)(2,1)}, bf16[...) custom-call(bf16[256,1280]{1,0:T(8,128)(2,1)} %bitcast.6, ...), custom_call_target="tpu_custom_call" | custom-call | tf_op jit(solution)/shard_map/pallas_call | solution.py:611
  61.7 231.8 %shard_map.187 = (bf16[256,1280]{1,0:T(8,128)(2,1)}, f32[256,1280]{1,0:T(8,128)}, f32[8,1280]{1,0:T(8,128)}, f32[1280,1280]{1,0:T(8,128)}, f32[1280,1280]{1,0:T(...) custom-call(bf16[256,1280]{1,0:T(8,128)(2,1)} %bitcast.7, ...), custom_call_target="tpu_custom_call" | custom-call | tf_op jit(solution)/shard_map/pallas_call | solution.py:983
  293.4 1.5 slice_reduce_fusion
  294.9 2.7 copy.24
  297.7 2.9 copy.25
  300.5 0.0 copy-done.1
  300.5 1.7 copy.26
  302.2 2.1 copy.32
  304.3 0.0 copy-done.2
  304.3 1.1 copy.33
  305.4 2.8 copy.34
  308.2 0.0 copy-done
  308.3 3.0 copy.35
  311.3 0.4 slice-done.1
  311.6 2.8 copy.36
  (7 shorter events, 0.0 us)
Async XLA Ops:
  0.6 6.2 %copy-start.4 = (bf16[1280,320]{0,1:T(8,128)(2,1)S(1)}, bf16[1280,320]{0,1:T(8,128)(2,1)}, u32[]{:S(2)}) copy-start(bf16[1280,320]{0,1:T(8,128)(2,1)} %param.16) | copy-start | bytes 2457604
  0.7 4.9 %copy-start.3 = (bf16[1280,320]{0,1:T(8,128)(2,1)S(1)}, bf16[1280,320]{0,1:T(8,128)(2,1)}, u32[]{:S(2)}) copy-start(bf16[1280,320]{0,1:T(8,128)(2,1)} %param.15) | copy-start | bytes 2457604
  297.7 2.9 copy-start.1
  300.5 3.8 %copy-start.2 = (f32[256,1280]{1,0:T(8,128)S(1)}, f32[256,1280]{1,0:T(8,128)}, u32[]{:S(2)}) copy-start(f32[256,1280]{1,0:T(8,128)} %get-tuple-element.38) | copy-start | bytes 3932164
  302.2 6.0 %copy-start = (f32[1280,1280]{1,0:T(8,128)S(1)}, f32[1280,1280]{1,0:T(8,128)}, u32[]{:S(2)}) copy-start(f32[1280,1280]{1,0:T(8,128)} %get-tuple-element.76) | copy-start | bytes 19660804
  305.4 5.9 %slice-start = ((s8[6553600]{0:T(1024)(128)(4,1)}), s8[4194304]{0:T(1024)(128)(4,1)S(1)}, s32[]{:S(2)}) async-start(s8[6553600]{0:T(1024)(128)(4,1)} %bitcast.4), calls=%async_computation | async-start | bytes 8388608
  308.3 3.4 %slice-start.1 = ((s8[6553600]{0:T(1024)(128)(4,1)}), s8[2359296]{0:T(1024)(128)(4,1)S(1)}, s32[]{:S(2)}) async-start(s8[6553600]{0:T(1024)(128)(4,1)} %bitcast.4), calls=%async_computation.1 | async-start | bytes 4718592

commit v3 on v2

--- a/solution.py
+++ b/solution.py
@@ -344,10 +344,10 @@
 SPAN = 512
 
 
-def pad_matrix(local, padded, transposed):
-    shape, feature_dim = ((padded, local), 1) if transposed else ((local, padded), 0)
-    feature = lax.broadcasted_iota(jnp.int32, shape, feature_dim)
-    lane = lax.broadcasted_iota(jnp.int32, shape, 1 - feature_dim)
+def pad_matrix(local, padded):
+    shape = (padded, local)
+    feature = lax.broadcasted_iota(jnp.int32, shape, 1)
+    lane = lax.broadcasted_iota(jnp.int32, shape, 0)
     head = jnp.zeros(shape, jnp.int32)
     for h in range(1, local // HEAD):
         head = head + (feature >= h * HEAD).astype(jnp.int32)
@@ -408,46 +408,68 @@
 
 
 class Gather:
-    def __init__(self, ring, rows, sems):
-        def copy(block, device, which):
+    def __init__(self, ring, rows, sems, parts=1):
+        self.parts = parts
+        size = BLOCK_SEQ // parts
+
+        def copy(block, device, which, part):
+            at = pl.ds(pl.multiple_of(block * BLOCK_SEQ + part * size, size), size)
             return pltpu.make_async_remote_copy(
-                src_ref=rows.at[block_rows(block), :],
-                dst_ref=rows.at[block_rows(block), :],
-                send_sem=sems.at[0, which],
-                recv_sem=sems.at[1, which],
+                src_ref=rows.at[at, :],
+                dst_ref=rows.at[at, :],
+                send_sem=sems.at[0, which * parts + part],
+                recv_sem=sems.at[1, which * parts + part],
                 device_id={"mp": device},
                 device_id_type=MESH,
             )
 
-        self.near = lambda: copy(ring.me, ring.core, 0)
-        self.across = lambda: copy(ring.me, ring.chip, 1)
-        self.onward = lambda: copy(ring.chip, ring.core, 2)
+        self.near = lambda part=0: copy(ring.me, ring.core, 0, part)
+        self.across = lambda part=0: copy(ring.me, ring.chip, 1, part)
+        self.onward = lambda part=0: copy(ring.chip, ring.core, 2, part)
+
+    def start(self, part=0):
+        self.across(part).start()
+        self.near(part).start()
 
     def forward(self):
-        self.across().wait_recv()
-        self.onward().start()
-
-    def finish(self):
-        self.onward().wait()
+        for part in range(self.parts):
+            self.across(part).wait_recv()
+            self.onward(part).start()
+
+    def near_in(self):
+        for part in range(self.parts):
+            self.near(part).wait_recv()
+
+    def onward_in(self):
+        for part in range(self.parts):
+            self.onward(part).wait_recv()
+
+    def sent(self):
+        for part in range(self.parts):
+            self.near(part).wait_send()
+            self.across(part).wait_send()
+            self.onward(part).wait_send()
 
 
 class Scatter:
-    def __init__(self, ring, send_core, recv_core, send_chip, recv_chip, sems):
-        self.bufs = (send_core, recv_core, send_chip, recv_chip)
-
-        def copy(source, target, device, which):
+    def __init__(self, ring, send_core, recv_core, send_chip, recv_chip, sems, parts=1):
+        self.parts = parts
+        size = BLOCK_SEQ // parts
+
+        def copy(source, target, device, which, part):
+            at = pl.ds(part * size, size)
             return pltpu.make_async_remote_copy(
-                src_ref=source,
-                dst_ref=target,
-                send_sem=sems.at[0, which],
-                recv_sem=sems.at[1, which],
+                src_ref=source.at[at, :],
+                dst_ref=target.at[at, :],
+                send_sem=sems.at[0, which * parts + part],
+                recv_sem=sems.at[1, which * parts + part],
                 device_id={"mp": device},
                 device_id_type=MESH,
             )
 
-        self.far = lambda: copy(send_core.at[0], recv_core.at[0], ring.core, 0)
-        self.core = lambda: copy(send_core.at[1], recv_core.at[1], ring.core, 1)
-        self.chip = lambda: copy(send_chip, recv_chip, ring.chip, 2)
+        self.far = lambda part=0: copy(send_core.at[0], recv_core.at[0], ring.core, 0, part)
+        self.core = lambda part=0: copy(send_core.at[1], recv_core.at[1], ring.core, 1, part)
+        self.chip = lambda part=0: copy(send_chip, recv_chip, ring.chip, 2, part)
 
 
 def greet_mp(ring, barrier):
@@ -463,12 +485,12 @@
 
 def qkv_block(rows, weights, cos_ref, sin_ref, out, block):
     at = block_rows(block)
-    turned = 2 * (weights.shape[1] // 3) // 256
-    tiles = weights.shape[1] // 256
+    turned = 2 * (weights.shape[0] // 3) // 256
+    tiles = weights.shape[0] // 256
 
     def one(n, turn):
         cols = pl.ds(pl.multiple_of(n * 256, 256), 256)
-        value = dot(rows[at, :], weights[:, cols])
+        value = dot_nt(rows[at, :], weights[cols, :])
         if turn:
             cosine, sine = cos_ref[at, :], sin_ref[at, :]
             halves = [value[:, j * 128 : j * 128 + 128] for j in range(2)]
@@ -497,14 +519,13 @@
         bias_ref[pl.ds(i * BLOCK_SEQ, BLOCK_SEQ), pl.ds(0, high - low)] = jnp.where((query >= key) & same, 0.0, MASKED).astype(bias_ref.dtype)
 
 
-def attend_all(qkv, out, bias_ref, heads, scale):
-    seq = qkv.shape[0]
+def attend(qkv, out, bias_ref, heads, scale, blocks):
     width = heads * HEAD_PAD
 
     @pl.loop(0, heads)
     def _(h):
         lanes = [pl.ds(pl.multiple_of(part * width + h * HEAD_PAD, HEAD_PAD), HEAD_PAD) for part in range(3)]
-        for i in range(seq // BLOCK_SEQ):
+        for i in blocks:
             low, high = max(0, i * BLOCK_SEQ - SPAN), (i + 1) * BLOCK_SEQ
             rows, keys = pl.ds(i * BLOCK_SEQ, BLOCK_SEQ), pl.ds(low, high - low)
             scores = dot_nt(qkv[rows, lanes[0]], qkv[keys, lanes[1]]) + bias_ref[rows, pl.ds(0, high - low)]
@@ -514,129 +535,14 @@
             out[rows, lanes[0]] = dot(probs.astype(jnp.bfloat16), qkv[keys, lanes[2]]).astype(jnp.bfloat16)
 
 
-def front_kernel(
-    x, g, seg, gain, wq, wk, wv, wo,
-    resid_o, h1_o, grow_o, qkv_o, mix_o, wqkv_o, wout_o, cos_o, sin_o,
-    rows_one, rows_g, qkv, mixed, raw, raw_out, wqkv, wout, cos_ref, sin_ref, ids_ref, bias_ref,
-    send_core, recv_core, send_chip, recv_chip, load_sem, save_sem, one_sem, g_sem, rs_sem,
-):
-    ring = Ring4()
-    local, width = wo.shape
-    padded = wout.shape[0]
-    heads = local // HEAD
-    barrier = pltpu.get_barrier_semaphore()
-    count = greet_mp(ring, barrier)
-    loads = [pltpu.make_async_copy(w, raw.at[i], load_sem.at[i]) for i, w in enumerate((wq, wk, wv))]
-    loads.append(pltpu.make_async_copy(wo, raw_out, load_sem.at[3]))
-    own_g = pltpu.make_async_copy(g, rows_g.at[block_rows(ring.me), :], load_sem.at[4])
-    for load in loads:
-        load.start()
-    own_g.start()
-    values, _ = norm_rows(x[...].astype(jnp.float32))
-    rows_one[block_rows(ring.me), :] = (values * gain[...]).astype(jnp.bfloat16)
-    pl.semaphore_wait(barrier, count)
-    one, all_g = Gather(ring, rows_one, one_sem), Gather(ring, rows_g, g_sem)
-    scatter = Scatter(ring, send_core, recv_core, send_chip, recv_chip, rs_sem)
-    one.across().start()
-    one.near().start()
-    spread = pad_matrix(local, padded, False)
-    for i, load in enumerate(loads[:3]):
-        load.wait()
-        wqkv[:, pl.ds(i * padded, padded)] = dot(raw[i], spread).astype(jnp.bfloat16)
-    loads[3].wait()
-    wout[...] = dot(pad_matrix(local, padded, True), raw_out[...]).astype(jnp.bfloat16)
-    own_g.wait()
-    ids_ref[...] = segment_columns(seg[...])
-    rotary_into(seg[...], cos_ref, sin_ref)
-    qkv_block(rows_one, wqkv, cos_ref, sin_ref, qkv, ring.me)
-    one.near().wait_recv()
-    qkv_block(rows_one, wqkv, cos_ref, sin_ref, qkv, ring.core)
-    masks_into(seg[...], ids_ref, bias_ref)
-    one.forward()
-    one.across().wait_send()
-    all_g.across().start()
-    all_g.near().start()
-    qkv_block(rows_one, wqkv, cos_ref, sin_ref, qkv, ring.chip)
-    one.onward().wait_recv()
-    qkv_block(rows_one, wqkv, cos_ref, sin_ref, qkv, ring.far)
-    attend_all(qkv, mixed, bias_ref, heads, 1.0 / math.sqrt(HEAD))
-    saves = [
-        pltpu.make_async_copy(source, target, save_sem.at[i])
-        for i, (source, target) in enumerate(
-            ((rows_one, h1_o), (qkv, qkv_o), (mixed, mix_o), (wqkv, wqkv_o), (wout, wout_o), (cos_ref, cos_o), (sin_ref, sin_o), (rows_g, grow_o))
-        )
-    ]
-    for save in saves[:7]:
-        save.start()
-
-    def term(block):
-        return dot(mixed[block_rows(block), :], wout[...])
-
-    send_core[0] = term(ring.far).astype(jnp.bfloat16)
-    scatter.far().start()
-    send_core[1] = term(ring.core).astype(jnp.bfloat16)
-    scatter.core().start()
-    chip_term = term(ring.chip)
-    scatter.far().wait_recv()
-    send_chip[...] = (chip_term + recv_core[0].astype(jnp.float32)).astype(jnp.bfloat16)
-    scatter.chip().start()
-    all_g.forward()
-    own = x[...].astype(jnp.float32) + term(ring.me)
-    scatter.core().wait_recv()
-    own = own + recv_core[1].astype(jnp.float32)
-    all_g.near().wait_recv()
-    all_g.onward().wait_recv()
-    saves[7].start()
-    scatter.chip().wait_recv()
-    resid_o[...] = own + recv_chip[...].astype(jnp.float32)
-    for gather in (one, all_g):
-        gather.near().wait_send()
-        gather.onward().wait_send()
-    all_g.across().wait_send()
-    one_done = (scatter.far(), scatter.core(), scatter.chip())
-    for copy in one_done:
-        copy.wait_send()
-    for save in saves:
-        save.wait()
-
-
-def front(x, g, seg, gain, wq, wk, wv, wo):
-    bf, f32 = jnp.bfloat16, jnp.float32
-    local, width = wo.shape
-    padded = local // HEAD * HEAD_PAD
-    seq, rows = seg.shape[1], x.shape[0]
-    shapes = [((rows, width), f32), ((seq, width), bf), ((seq, width), bf), ((seq, 3 * padded), bf), ((seq, padded), bf), ((width, 3 * padded), bf), ((padded, width), bf), ((seq, 128), f32), ((seq, 128), f32)]
-    vm, hbm = pl.BlockSpec(memory_space=pltpu.VMEM), pl.BlockSpec(memory_space=pl.ANY)
-    sem = pltpu.SemaphoreType.DMA
-    return pl.pallas_call(
-        front_kernel,
-        out_shape=[jax.ShapeDtypeStruct(s, d) for s, d in shapes],
-        in_specs=[vm, vm, vm, vm, hbm, hbm, hbm, hbm],
-        out_specs=[vm] + [hbm] * 8,
-        scratch_shapes=[
-            pltpu.VMEM((seq, width), bf), pltpu.VMEM((seq, width), bf), pltpu.VMEM((seq, 3 * padded), bf), pltpu.VMEM((seq, padded), bf),
-            pltpu.VMEM((3, width, local), bf), pltpu.VMEM((local, width), bf), pltpu.VMEM((width, 3 * padded), bf), pltpu.VMEM((padded, width), bf),
-            pltpu.VMEM((seq, 128), f32), pltpu.VMEM((seq, 128), f32), pltpu.VMEM((seq, 128), f32), pltpu.VMEM((seq, SPAN + BLOCK_SEQ), f32),
-            pltpu.VMEM((2, rows, width), bf), pltpu.VMEM((2, rows, width), bf), pltpu.VMEM((rows, width), bf), pltpu.VMEM((rows, width), bf),
-            sem((5,)), sem((8,)), sem((2, 3)), sem((2, 3)), sem((2, 3)),
-        ],
-        compiler_params=pltpu.CompilerParams(collective_id=1, has_side_effects=True, vmem_limit_bytes=60 * 2**20),
-    )(x, g, seg, gain.reshape(1, -1), wq, wk, wv, wo)
-
-
-def gelu_parts(u):
-    tangent = jnp.tanh(GELU_C * (u + GELU_K * u * u * u))
-    return tangent
-
-
-def tail_kernel(
-    x, resid, seg, gain_one, gain_two, wup, wdown, h1, grow, qkv_in, mix_in, wqkv_in, wout_in, cos_in, sin_in,
-    result_o, input_o, gains_o, down_o, up_o, out_o, q_o, k_o, v_o,
-    rows, b0, b1, b2, b3, b4, b5, send_sem, recv_sem, stage, stage_sem, tstage, tsem,
+def layer_kernel(
+    x, g, seg, gain_one, gain_two, wq, wk, wv, wo, wup, wdown,
+    result_o, input_o, gains_o, sums_o,
+    rows, b0, b1, b2, b3, b4, b5, send_sem, recv_sem, save_sem,
     w_up, w_down, w_qkv, w_out, rows_one, rows_g, rows_two, hidden, grad_up, branch, qkv, mixed, grad_mixed,
-    cos_ref, sin_ref, bias_ref, term_ref, key_sum, value_sum,
+    cos_ref, sin_ref, bias_ref, resid, term_ref, key_sum, value_sum,
     send_core, recv_core, send_chip, recv_chip, gain_acc, gain_recv,
-    load_sem, two_sem, branch_sem, rs_sem, rs2_sem, rs3_sem, gain_sem, free_sem,
+    load_sem, one_sem, g_sem, two_sem, branch_sem, rs0_sem, rs_sem, rs2_sem, rs3_sem, gain_sem, free_sem,
 ):
     bf, f32 = jnp.bfloat16, jnp.float32
     ring = Ring4()
@@ -647,95 +553,154 @@
     local = heads * HEAD
     pairs = rows.shape[0] // (2 * CHUNK)
     scale = 1.0 / math.sqrt(HEAD)
+    half = BLOCK_SEQ // 2
+    chip = lax.div(ring.me, 2)
     red = Reducer(rows, (b0, b1, b2, b3, b4, b5), send_sem, recv_sem, pairs)
     barrier = pltpu.get_barrier_semaphore()
     count = greet_mp(ring, barrier) + red.greet(barrier)
-    places = ((wup, w_up), (grow, rows_g), (wdown, w_down), (mix_in, mixed), (wout_in, w_out), (cos_in, cos_ref), (sin_in, sin_ref), (qkv_in, qkv), (wqkv_in, w_qkv), (h1, rows_one))
+    places = [(w, rows.at[pl.ds(i * local, local), :]) for i, w in enumerate((wq, wk, wv, wo))]
+    places += [(g, rows_g.at[block_rows(ring.me), :]), (wup, w_up), (wdown, w_down)]
     loads = [pltpu.make_async_copy(source, target, load_sem.at[i]) for i, (source, target) in enumerate(places)]
-    loads[0].start()
-    loads[1].start()
-    normed, _ = norm_rows(resid[...])
-    rows_two[block_rows(ring.me), :] = (normed * gain_two[...]).astype(bf)
-    pl.semaphore_wait(barrier, count)
-    two, all_branch = Gather(ring, rows_two, two_sem), Gather(ring, branch, branch_sem)
+    for load in loads[:5]:
+        load.start()
+    normed, _ = norm_rows(x[...].astype(f32))
+    rows_one[block_rows(ring.me), :] = (normed * gain_one[...]).astype(bf)
+    one, all_g = Gather(ring, rows_one, one_sem, 2), Gather(ring, rows_g, g_sem)
+    two, all_branch = Gather(ring, rows_two, two_sem, 2), Gather(ring, branch, branch_sem)
+    ahead = Scatter(ring, send_core, recv_core, send_chip, recv_chip, rs0_sem, 2)
     first = Scatter(ring, send_core, recv_core, send_chip, recv_chip, rs_sem)
     second = Scatter(ring, send_core, recv_core, send_chip, recv_chip, rs2_sem)
     third = Scatter(ring, send_core, recv_core, send_chip, recv_chip, rs3_sem)
-    two.across().start()
-    two.near().start()
-    for load in loads[2:]:
+    pl.semaphore_wait(barrier, count)
+    one.start(0)
+    one.start(1)
+    for load in loads[5:]:
         load.start()
 
+    spread = pad_matrix(local, padded)
+    for i in range(3):
+        loads[i].wait()
+        w_qkv[pl.ds(i * padded, padded), :] = dot(spread, rows[pl.ds(i * local, local), :]).astype(bf)
+    loads[3].wait()
+    w_out[...] = dot(spread, rows[pl.ds(3 * local, local), :]).astype(bf)
+    rotary_into(seg[...], cos_ref, sin_ref)
+    qkv_block(rows_one, w_qkv, cos_ref, sin_ref, qkv, ring.me)
+    one.near_in()
+    qkv_block(rows_one, w_qkv, cos_ref, sin_ref, qkv, ring.core)
+    key_sum[...] = segment_columns(seg[...])
+    masks_into(seg[...], key_sum, bias_ref)
+    loads[4].wait()
+    one.forward()
+    one.across(0).wait_send()
+    one.across(1).wait_send()
+    all_g.start()
+    qkv_block(rows_one, w_qkv, cos_ref, sin_ref, qkv, ring.chip)
+    one.onward_in()
+    qkv_block(rows_one, w_qkv, cos_ref, sin_ref, qkv, ring.far)
+
+    early, late = (0, 1), (2, 3)
+
+    @pl.when(chip == 0)
+    def _():
+        attend(qkv, mixed, bias_ref, heads, scale, late)
+
+    @pl.when(chip == 1)
+    def _():
+        attend(qkv, mixed, bias_ref, heads, scale, early)
+
+    def term(block, part):
+        at = pl.ds(pl.multiple_of(block * BLOCK_SEQ + part * half, half), half)
+        return dot(mixed[at, :], w_out[...])
+
+    parts = [pl.ds(p * half, half) for p in range(2)]
+    for p in range(2):
+        send_core[0, parts[p], :] = term(ring.far, p).astype(bf)
+        ahead.far(p).start()
+    for p in range(2):
+        value = term(ring.chip, p)
+        ahead.far(p).wait_recv()
+        send_chip[parts[p], :] = (value + recv_core[0, parts[p], :].astype(f32)).astype(bf)
+        ahead.chip(p).start()
+
+    @pl.when(chip == 0)
+    def _():
+        attend(qkv, mixed, bias_ref, heads, scale, early)
+
+    @pl.when(chip == 1)
+    def _():
+        attend(qkv, mixed, bias_ref, heads, scale, late)
+
+    for p in range(2):
+        send_core[1, parts[p], :] = term(ring.core, p).astype(bf)
+        ahead.core(p).start()
+    all_g.forward()
+    for p in range(2):
+        resid[parts[p], :] = x[parts[p], :].astype(f32) + term(ring.me, p)
+    for p in range(2):
+        ahead.core(p).wait_recv()
+        ahead.chip(p).wait_recv()
+        value = resid[parts[p], :] + recv_core[1, parts[p], :].astype(f32) + recv_chip[parts[p], :].astype(f32)
+        resid[parts[p], :] = value
+        normed, _ = norm_rows(value)
+        at = pl.ds(pl.multiple_of(ring.me * BLOCK_SEQ + p * half, half), half)
+        rows_two[at, :] = (normed * gain_two[...]).astype(bf)
+        two.start(p)
+    for p in range(2):
+        ahead.far(p).wait_send()
+        ahead.core(p).wait_send()
+        ahead.chip(p).wait_send()
+
     base = 2 * units
-    down_pairs = units // (2 * CHUNK)
-    whole_out = local // (2 * CHUNK)
-    plain = 2 * down_pairs + whole_out
-
-    def put(pair, target, row, many=2 * CHUNK):
-        slot = lax.rem(pair, 2)
-        return pltpu.make_async_copy(
-            stage.at[slot, pl.ds(0, many), :], target.at[pl.ds(pl.multiple_of(row, CHUNK), many), :], stage_sem.at[slot]
-        )
-
-    def out_pair(pair):
-        @pl.when(pair >= 2)
-        def _():
-            put(pair, down_o, 0).wait()
-
-        stage[lax.rem(pair, 2)] = rows[pl.ds(pl.multiple_of(pair * 2 * CHUNK, 2 * CHUNK), 2 * CHUNK), :].astype(f32)
-
-        @pl.when(pair < down_pairs)
-        def _():
-            put(pair, down_o, pair * 2 * CHUNK).start()
-
-        @pl.when((pair >= down_pairs) & (pair < 2 * down_pairs))
-        def _():
-            put(pair, up_o, (pair - down_pairs) * 2 * CHUNK).start()
-
-        @pl.when(pair >= 2 * down_pairs)
-        def _():
-            put(pair, out_o, (pair - 2 * down_pairs) * 2 * CHUNK).start()
+
+    def put(pair):
+        at = pl.ds(pl.multiple_of(pair * 2 * CHUNK, 2 * CHUNK), 2 * CHUNK)
+        return pltpu.make_async_copy(rows.at[at, :], sums_o.at[at, :], save_sem.at[lax.rem(pair, 4)])
 
     def slot(index):
         red.slot(index)
         pair = index - (STAGES - 1)
 
-        @pl.when((pair >= 0) & (pair < plain))
+        @pl.when(pair >= 4)
         def _():
-            out_pair(pair)
+            put(pair - 4).wait()
+
+        @pl.when(pair >= 0)
+        def _():
+            put(pair).start()
 
     def tile(n):
         return pl.ds(pl.multiple_of(n * 256, 256), 256)
+
+    def up_tile(block, n):
+        u = dot(rows_two[block_rows(block), :], w_up[:, tile(n)])
+        tangent = jnp.tanh(GELU_C * (u + GELU_K * u * u * u))
+        hidden[block_rows(block), tile(n)] = (0.5 * u * (1.0 + tangent)).astype(bf)
 
     def up_block(block):
         @pl.loop(0, units // 256)
         def _(n):
-            u = dot(rows_two[block_rows(block), :], w_up[:, tile(n)])
-            tangent = jnp.tanh(GELU_C * (u + GELU_K * u * u * u))
-            hidden[block_rows(block), tile(n)] = (0.5 * u * (1.0 + tangent)).astype(bf)
-
-    loads[0].wait()
+            up_tile(block, n)
+
+    loads[5].wait()
     up_block(ring.me)
-    two.near().wait_recv()
+    two.near_in()
     up_block(ring.core)
-    key_sum[...] = segment_columns(seg[...])
-    masks_into(seg[...], key_sum, bias_ref)
+    all_g.near_in()
+    all_g.onward_in()
     two.forward()
-    up_block(ring.chip)
-    two.onward().wait_recv()
-    up_block(ring.far)
-    loads[1].wait()
+    two.onward_in()
 
     @pl.loop(0, units // 256)
-    def _(i):
-        rows[tile(i), :] = dot_tn(hidden[:, tile(i)], rows_g[...]).astype(bf)
-        slot(i)
-
-    loads[2].wait()
+    def _(n):
+        for block in (ring.chip, ring.far):
+            up_tile(block, n)
+        rows[tile(n), :] = dot_tn(hidden[:, tile(n)], rows_g[...]).astype(bf)
+        slot(n)
+
+    loads[6].wait()
 
     def order(k):
         there = k < 2
-        chip = lax.div(ring.me, 2)
         core = lax.rem(ring.me, 2)
         flip = 1 - lax.rem(k, 2)
         to_chip = jnp.where(there, 1 - chip, chip)
@@ -815,8 +780,6 @@
         up_rows(i)
         slot(9 + i)
 
-    for load in loads[3:]:
-        load.wait()
     all_branch.near().wait_recv()
     all_branch.forward()
     all_branch.onward().wait_recv()
@@ -886,32 +849,10 @@
 
         @pl.loop(0, width // 256)
         def _(n):
-            term_ref[:, tile(n)] = dot_nt(qkv[at, :], w_qkv[tile(n), :])
+            term_ref[:, tile(n)] = dot(qkv[at, :], w_qkv[:, tile(n)])
 
         hand_on(k, third, None)
         slot(25 + k)
-
-    eye = jnp.where(
-        lax.broadcasted_iota(jnp.int32, (256, 256), 0) == lax.broadcasted_iota(jnp.int32, (256, 256), 1), 1.0, 0.0
-    ).astype(bf)
-
-    def tput(n, target):
-        return pltpu.make_async_copy(tstage.at[lax.rem(n, 2)], target.at[tile(n), :], tsem.at[lax.rem(n, 2)])
-
-    def turn_out(part, target):
-        row = base + local * (part + 1)
-
-        @pl.loop(0, width // 256)
-        def _(n):
-            @pl.when(n >= 2)
-            def _():
-                tput(n, target).wait()
-
-            tstage[lax.rem(n, 2)] = dot_nt(eye, rows[pl.ds(row, local), tile(n)])
-            tput(n, target).start()
-
-        for n in (width // 256 - 2, width // 256 - 1):
-            tput(n, target).wait()
 
     slot(29)
     grad_one = settle(third)
@@ -942,64 +883,107 @@
 
         slot(index)
 
-        @pl.when(index == 30)
-        def _():
-            turn_out(0, q_o)
-
-        @pl.when(index == 33)
-        def _():
-            turn_out(1, k_o)
-
     exchange(4).wait_recv()
     gains_o[...] = gain_acc[4] + gain_recv[4]
-    turn_out(2, v_o)
-    for pair in (plain, plain + 1):
-        put(pair, down_o, 0).wait()
-    left = local - whole_out * 2 * CHUNK
-    if left:
-        stage[0, pl.ds(0, left), :] = rows[pl.ds(base + whole_out * 2 * CHUNK, left), :].astype(f32)
-        put(0, out_o, whole_out * 2 * CHUNK, left).start()
-        put(0, out_o, whole_out * 2 * CHUNK, left).wait()
+    for pair in range(pairs - 4, pairs):
+        put(pair).wait()
     for step in range(5):
         exchange(step).wait_send()
-    for gather in (two, all_branch):
-        gather.near().wait_send()
-        gather.across().wait_send()
-        gather.onward().wait_send()
-
-
-def tail(x, resid, seg, gain_one, gain_two, wup, wdown, h1, grow, qkv, mixed, wqkv, wout, cos, sin):
+    for part in range(2):
+        one.near(part).wait_send()
+        one.onward(part).wait_send()
+    for gather in (all_g, two, all_branch):
+        gather.sent()
+
+
+def layer(x, g, seg, gain_one, gain_two, wq, wk, wv, wo, wup, wdown):
     bf, f32 = jnp.bfloat16, jnp.float32
     own, width = x.shape
     units = wup.shape[1]
     seq = seg.shape[1]
-    padded = wout.shape[0]
-    local = padded // HEAD_PAD * HEAD
+    local = wo.shape[0]
+    padded = local // HEAD * HEAD_PAD
     total = 2 * units + 4 * local
     vm, hbm = pl.BlockSpec(memory_space=pltpu.VMEM), pl.BlockSpec(memory_space=pl.ANY)
     sem = pltpu.SemaphoreType.DMA
-    shapes = [((own, width), bf), ((own, width), f32), ((8, width), f32), ((units, width), f32), ((width, units), f32), ((local, width), f32)] + [((width, local), f32)] * 3
+    shapes = [((own, width), bf), ((own, width), f32), ((8, width), f32), ((total, width), bf)]
     tall = pltpu.VMEM((seq, width), bf)
     return pl.pallas_call(
-        tail_kernel,
+        layer_kernel,
         out_shape=[jax.ShapeDtypeStruct(s, d) for s, d in shapes],
-        in_specs=[vm] * 5 + [hbm] * 10,
-        out_specs=[vm] * 3 + [hbm] * 6,
+        in_specs=[vm, hbm, vm, vm, vm] + [hbm] * 6,
+        out_specs=[vm] * 3 + [hbm],
         scratch_shapes=[pltpu.VMEM((total, width), bf)]
         + reducer_scratch(width)
         + [
-            pltpu.VMEM((2, 2 * CHUNK, width), f32), sem((2,)), pltpu.VMEM((2, 256, local), f32), sem((2,)),
-            pltpu.VMEM((width, units), bf), pltpu.VMEM((units, width), bf), pltpu.VMEM((width, 3 * padded), bf), pltpu.VMEM((padded, width), bf),
+            sem((4,)),
+            pltpu.VMEM((width, units), bf), pltpu.VMEM((units, width), bf), pltpu.VMEM((3 * padded, width), bf), pltpu.VMEM((padded, width), bf),
             tall, tall, tall, pltpu.VMEM((seq, units), bf), pltpu.VMEM((seq, units), bf), tall,
             pltpu.VMEM((seq, 3 * padded), bf), pltpu.VMEM((seq, padded), bf), pltpu.VMEM((seq, padded), bf),
             pltpu.VMEM((seq, 128), f32), pltpu.VMEM((seq, 128), f32), pltpu.VMEM((seq, SPAN + BLOCK_SEQ), bf),
-            pltpu.VMEM((own, width), f32), pltpu.VMEM((seq, HEAD_PAD), f32), pltpu.VMEM((seq, HEAD_PAD), f32),
+            pltpu.VMEM((own, width), f32), pltpu.VMEM((own, width), f32), pltpu.VMEM((seq, HEAD_PAD), f32), pltpu.VMEM((seq, HEAD_PAD), f32),
             pltpu.VMEM((2, own, width), bf), pltpu.VMEM((2, own, width), bf), pltpu.VMEM((own, width), bf), pltpu.VMEM((own, width), bf),
             pltpu.VMEM((5, 8, width), f32), pltpu.VMEM((5, 8, width), f32),
-            sem((10,)), sem((2, 3)), sem((2, 3)), sem((2, 3)), sem((2, 3)), sem((2, 3)), sem((2, 5)), pltpu.SemaphoreType.REGULAR,
+            sem((7,)), sem((2, 6)), sem((2, 3)), sem((2, 6)), sem((2, 3)), sem((2, 6)), sem((2, 3)), sem((2, 3)), sem((2, 3)), sem((2, 5)),
+            pltpu.SemaphoreType.REGULAR,
         ],
-        compiler_params=pltpu.CompilerParams(collective_id=2, has_side_effects=True, vmem_limit_bytes=67043328),
-    )(x, resid, seg, gain_one.reshape(1, -1), gain_two.reshape(1, -1), wup, wdown, h1, grow, qkv, mixed, wqkv, wout, cos, sin)
+        compiler_params=pltpu.CompilerParams(collective_id=0, has_side_effects=True, vmem_limit_bytes=67043328),
+    )(x, g, seg, gain_one, gain_two, wq, wk, wv, wo, wup, wdown)
+
+
+def finish_kernel(result, input_grad, gains, sums, result_o, input_o, one_o, two_o, down_o, up_o, out_o, q_o, k_o, v_o, inbox, outbox, side_one, side_two, in_sem, out_sem, side_sem):
+    step = out_o.shape[0]
+    targets = [(down_o, i * step) for i in range(down_o.shape[0] // step)] + [(up_o, i * step) for i in range(up_o.shape[0] // step)]
+    targets += [(t, 0) for t in (out_o, q_o, k_o, v_o)]
+    count, depth = len(targets), inbox.shape[0]
+    bring = [pltpu.make_async_copy(result, side_one, side_sem.at[0]), pltpu.make_async_copy(input_grad, side_two, side_sem.at[1])]
+    take = [pltpu.make_async_copy(side_one, result_o, side_sem.at[2]), pltpu.make_async_copy(side_two, input_o, side_sem.at[3])]
+
+    def read(i):
+        return pltpu.make_async_copy(sums.at[pl.ds(i * step, step), :], inbox.at[i % depth], in_sem.at[i % depth])
+
+    def write(i):
+        target, at = targets[i]
+        return pltpu.make_async_copy(outbox.at[i % depth], target.at[pl.ds(at, step), :], out_sem.at[i % depth])
+
+    for i in range(depth):
+        read(i).start()
+    for side in bring:
+        side.start()
+    one_o[...] = gains[0, :]
+    two_o[...] = gains[1, :]
+    for i in range(count):
+        read(i).wait()
+        if i >= depth:
+            write(i - depth).wait()
+        outbox[i % depth] = inbox[i % depth].astype(jnp.float32)
+        write(i).start()
+        if i + depth < count:
+            read(i + depth).start()
+        if i == depth:
+            for come, go in zip(bring, take):
+                come.wait()
+                go.start()
+    for i in range(count - depth, count):
+        write(i).wait()
+    for side in take:
+        side.wait()
+
+
+def finish(result, input_grad, gains, sums, units, local):
+    bf, f32 = jnp.bfloat16, jnp.float32
+    own, width = result.shape
+    vm, hbm = pl.BlockSpec(memory_space=pltpu.VMEM), pl.BlockSpec(memory_space=pl.ANY)
+    sem = pltpu.SemaphoreType.DMA
+    shapes = [((own, width), bf), ((own, width), f32), ((width,), f32), ((width,), f32), ((units, width), f32), ((width, units), f32)] + [((local, width), f32)] * 4
+    return pl.pallas_call(
+        finish_kernel,
+        out_shape=[jax.ShapeDtypeStruct(s, d) for s, d in shapes],
+        in_specs=[hbm, hbm, vm, hbm],
+        out_specs=[hbm, hbm, vm, vm] + [hbm] * 6,
+        scratch_shapes=[pltpu.VMEM((3, local, width), bf), pltpu.VMEM((3, local, width), f32), pltpu.VMEM((own, width), bf), pltpu.VMEM((own, width), f32), sem((3,)), sem((3,)), sem((4,))],
+        compiler_params=pltpu.CompilerParams(vmem_limit_bytes=67043328),
+    )(result, input_grad, gains, sums)
 
 
 def on_device(
@@ -1142,13 +1126,12 @@
 def on_device_kernels(
     hidden_in, segment_ids, attn_gain, query_weight, key_weight, value_weight, out_weight, mlp_gain, up_weight, down_weight, out_cotangent
 ):
-    resid, h1, grow, qkv, mixed, wqkv, wout, cos, sin = front(
-        hidden_in[0], out_cotangent[0], segment_ids, attn_gain, query_weight, key_weight, value_weight, out_weight
-    )
-    result, input_grad, gains, down, up, out, query, key, value = tail(
-        hidden_in[0], resid, segment_ids, attn_gain, mlp_gain, up_weight, down_weight, h1, grow, qkv, mixed, wqkv, wout, cos, sin
-    )
-    return (result[None], input_grad[None], gains[0], query, key, value, out, gains[1], up, down)
+    sums = layer(
+        hidden_in[0], out_cotangent[0], segment_ids, attn_gain, mlp_gain,
+        query_weight.T, key_weight.T, value_weight.T, out_weight, up_weight, down_weight,
+    )
+    result, input_grad, one, two, down, up, out, query, key, value = finish(*sums, up_weight.shape[1], out_weight.shape[0])
+    return (result[None], input_grad[None], one, query.T, key.T, value.T, out, two, up, down)
 
 
 def solution(mesh):

time: 315 us -> 282 us (0.90)
  local copies, waits for them, and re-layouts: 28.5 us -> 0 us
  Pallas kernels: 285 us -> 281 us
    unnamed x25 -> x0, local copies, waits for them, and re-layouts: 24.3 us -> none
    pallas_call x2, Pallas kernels: 285 us -> 281 us  [the longest x1 268 us: layer(): pl.pallas_call(layer_kernel, out_shape=[jax.ShapeDtypeStruct(s, d) for s,...]
where the time goes in v3:
time: 282 us
  Pallas kernels  281 us (100%)
    pallas_call x1, Pallas kernels, layer(): pl.pallas_call(layer_kernel, out_shape=[jax.ShapeDtypeStruct(s, d) for s,...  268 us
    pallas_call x1, Pallas kernels, finish(): pl.pallas_call(finish_kernel, out_shape=[jax.ShapeDtypeStruct(s, d) for s...  12.7 us

profile of v3, /device:TPU:0, one launch (start us, length us, event | category | flops | bytes accessed | tf_op | source)
XLA Modules:
  0.0 281.7 jit_solution(17443609142818913763)
XLA Ops:
  0.6 268.2 %shard_map.186 = (bf16[256,1280]{1,0:T(8,128)(2,1)}, f32[256,1280]{1,0:T(8,128)}, f32[8,1280]{1,0:T(8,128)}, bf16[3840,1280]{1,0:T(8,128)(2,1)}) custom-call(bf16[256,1280]{1,0:T(8,128)(2,1)} %bitcast.13, bf16[256,1280]{1,0:T(8,128)(2,1)} %bitcast.14, s32[1,1024]{1,0:T(1,128)} %seg.1, f32[1280]{0:T(1024)} %gain_one.1, f32[1280]{0:T(1024)} %gain_two.1, ...), custom_call_target="tpu_custom_call" | custom-call | tf_op jit(solution)/shard_map/pallas_call | solution.py:911
  268.8 12.7 %shard_map.187 = (bf16[256,1280]{1,0:T(8,128)(2,1)}, f32[256,1280]{1,0:T(8,128)}, f32[1280]{0:T(1024)}, f32[1280]{0:T(1024)}, f32[1280,1280]{1,0:T(8,128)}, /*in...) custom-call(bf16[256,1280]{1,0:T(8,128)(2,1)} %get-tuple-element.24., ...), custom_call_target="tpu_custom_call" | custom-call | tf_op jit(solution)/shard_map/pallas_call | solution.py:979

commit v4 on v3

--- a/solution.py
+++ b/solution.py
@@ -542,7 +542,7 @@
     w_up, w_down, w_qkv, w_out, rows_one, rows_g, rows_two, hidden, grad_up, branch, qkv, mixed, grad_mixed,
     cos_ref, sin_ref, bias_ref, resid, term_ref, key_sum, value_sum,
     send_core, recv_core, send_chip, recv_chip, gain_acc, gain_recv,
-    load_sem, one_sem, g_sem, two_sem, branch_sem, rs0_sem, rs_sem, rs2_sem, rs3_sem, gain_sem, free_sem,
+    load_sem, one_sem, g_sem, two_sem, branch_sem, rs0_sem, rs_sem, rs2_sem, rs3_sem, gain_sem, free_sem, ready_sem,
 ):
     bf, f32 = jnp.bfloat16, jnp.float32
     ring = Ring4()
@@ -690,13 +690,6 @@
     two.forward()
     two.onward_in()
 
-    @pl.loop(0, units // 256)
-    def _(n):
-        for block in (ring.chip, ring.far):
-            up_tile(block, n)
-        rows[tile(n), :] = dot_tn(hidden[:, tile(n)], rows_g[...]).astype(bf)
-        slot(n)
-
     loads[6].wait()
 
     def order(k):
@@ -735,17 +728,33 @@
         scatter.chip().wait()
         return term_ref[...] + recv_chip[...].astype(f32)
 
+    def grad_tile(at, n):
+        u = dot(rows_two[at, :], w_up[:, tile(n)])
+        upstream = dot_nt(rows_g[at, :], w_down[tile(n), :])
+        tangent = jnp.tanh(GELU_C * (u + GELU_K * u * u * u))
+        slope = 0.5 * (1.0 + tangent) + 0.5 * u * (1.0 - tangent * tangent) * GELU_C * (1.0 + 3.0 * GELU_K * u * u)
+        grad_up[at, tile(n)] = (upstream * slope).astype(bf)
+
+    @pl.loop(0, units // 256)
+    def _(n):
+        for block in (ring.chip, ring.far):
+            up_tile(block, n)
+        rows[tile(n), :] = dot_tn(hidden[:, tile(n)], rows_g[...]).astype(bf)
+        slot(n)
+
+        @pl.loop(0, 3)
+        def _(k):
+            grad_tile(block_rows(order(k)), n)
+
     @pl.loop(0, 4)
     def _(k):
+        @pl.loop(0, 2)
+        def _(j):
+            @pl.when(2 * k + j < units // 256)
+            def _():
+                grad_tile(block_rows(order(3)), 2 * k + j)
+
         at = block_rows(order(k))
-
-        @pl.loop(0, units // 256)
-        def _(n):
-            u = dot(rows_two[at, :], w_up[:, tile(n)])
-            upstream = dot_nt(rows_g[at, :], w_down[tile(n), :])
-            tangent = jnp.tanh(GELU_C * (u + GELU_K * u * u * u))
-            slope = 0.5 * (1.0 + tangent) + 0.5 * u * (1.0 - tangent * tangent) * GELU_C * (1.0 + 3.0 * GELU_K * u * u)
-            grad_up[at, tile(n)] = (upstream * slope).astype(bf)
 
         @pl.loop(0, width // 256)
         def _(n):
@@ -757,11 +766,8 @@
     def up_rows(i):
         rows[pl.ds(pl.multiple_of(units + i * 256, 256), 256), :] = dot_tn(rows_two[:, tile(i)], grad_up[...]).astype(bf)
 
-    @pl.loop(0, 2)
-    def _(i):
-        up_rows(i)
-        slot(9 + i)
-
+    up_rows(0)
+    slot(9)
     grad_two = settle(first)
     normed, inverse = norm_rows(resid[...])
     scaled = grad_two * gain_two[...]
@@ -774,24 +780,41 @@
     branch[block_rows(ring.me), :] = mine.astype(bf)
     all_branch.across().start()
     all_branch.near().start()
-
-    @pl.loop(2, units // 256)
-    def _(i):
-        up_rows(i)
-        slot(9 + i)
-
-    all_branch.near().wait_recv()
-    all_branch.forward()
-    all_branch.onward().wait_recv()
+    for device in (ring.core, ring.chip):
+        pl.semaphore_signal(ready_sem, inc=1, device_id={"mp": device}, device_id_type=MESH)
 
     def head_rows(left, lane, right, row):
         value = dot_tn(left[:, lane], right[...])
         halves = [value[at : at + HEAD // 2, :] for at in (0, 64, 128, 192)]
         rows[pl.ds(pl.multiple_of(row, 16), 2 * HEAD), :] = jnp.concatenate(halves, axis=0).astype(bf)
 
-    @pl.loop(0, heads // 2)
-    def _(j):
-        head_rows(mixed, tile(j), branch, base + j * 2 * HEAD)
+    @pl.loop(1, units // 256)
+    def _(i):
+        up_rows(i)
+
+        @pl.when(i == 1)
+        def _():
+            pl.semaphore_wait(ready_sem, 2)
+
+        at = block_rows(order(i - 1))
+
+        @pl.loop(0, width // 256)
+        def _(n):
+            term_ref[:, tile(n)] = dot(hidden[at, :], w_down[:, tile(n)])
+
+        hand_on(i - 1, second, None)
+
+        @pl.when(i == 4)
+        def _():
+            all_branch.near().wait_recv()
+            all_branch.forward()
+            all_branch.onward().wait_recv()
+
+            @pl.loop(0, heads // 2)
+            def _(j):
+                head_rows(mixed, tile(j), branch, base + j * 2 * HEAD)
+
+        slot(9 + i)
 
     @pl.loop(0, 4)
     def _(b):
@@ -822,13 +845,6 @@
         turned = key_sum[...] * scale
         qkv[:, lanes[1]] = (turned * cos_ref[...] - pltpu.roll(turned, 64, 1) * sin_ref[...]).astype(bf)
         qkv[:, lanes[2]] = value_sum[...].astype(bf)
-        at = block_rows(order(h))
-
-        @pl.loop(0, width // 256)
-        def _(n):
-            term_ref[:, tile(n)] = dot(hidden[at, :], w_down[:, tile(n)])
-
-        hand_on(h, second, None)
         slot(15 + 2 * h)
 
     @pl.loop(0, 3)
@@ -925,7 +941,7 @@
             pltpu.VMEM((2, own, width), bf), pltpu.VMEM((2, own, width), bf), pltpu.VMEM((own, width), bf), pltpu.VMEM((own, width), bf),
             pltpu.VMEM((5, 8, width), f32), pltpu.VMEM((5, 8, width), f32),
             sem((7,)), sem((2, 6)), sem((2, 3)), sem((2, 6)), sem((2, 3)), sem((2, 6)), sem((2, 3)), sem((2, 3)), sem((2, 3)), sem((2, 5)),
-            pltpu.SemaphoreType.REGULAR,
+            pltpu.SemaphoreType.REGULAR, pltpu.SemaphoreType.REGULAR,
         ],
         compiler_params=pltpu.CompilerParams(collective_id=0, has_side_effects=True, vmem_limit_bytes=67043328),
     )(x, g, seg, gain_one, gain_two, wq, wk, wv, wo, wup, wdown)

time: 282 us -> 276 us (0.979)
  Pallas kernels: 281 us -> 274 us
    pallas_call x1, Pallas kernels: 268 us -> 262 us  [layer(): pl.pallas_call(layer_kernel, out_shape=[jax.ShapeDtypeStruct(s, d) for s,...]
where the time goes in v4:
time: 276 us; the launch traced here: 275 us
  Pallas kernels  274 us (99%)
    pallas_call x1, Pallas kernels, layer(): pl.pallas_call(layer_kernel, out_shape=[jax.ShapeDtypeStruct(s, d) for s,...  262 us
    pallas_call x1, Pallas kernels, finish(): pl.pallas_call(finish_kernel, out_shape=[jax.ShapeDtypeStruct(s, d) for s...  12.7 us

profile of v4, /device:TPU:0, one launch (start us, length us, event | category | flops | bytes accessed | tf_op | source)
XLA Modules:
  0.0 275.2 jit_solution(16722515927406278231)
XLA Ops:
  0.6 261.7 %shard_map.186 = (bf16[256,1280]{1,0:T(8,128)(2,1)}, f32[256,1280]{1,0:T(8,128)}, f32[8,1280]{1,0:T(8,128)}, bf16[3840,1280]{1,0:T(8,128)(2,1)}) custom-call(bf16[256,1280]{1,0:T(8,128)(2,1)} %bitcast.13, bf16[256,1280]{1,0:T(8,128)(2,1)} %bitcast.14, s32[1,1024]{1,0:T(1,128)} %seg.1, f32[1280]{0:T(1024)} %gain_one.1, f32[1280]{0:T(1024)} %gain_two.1, ...), custom_call_target="tpu_custom_call" | custom-call | tf_op jit(solution)/shard_map/pallas_call | solution.py:927
  262.3 12.7 %shard_map.187 = (bf16[256,1280]{1,0:T(8,128)(2,1)}, f32[256,1280]{1,0:T(8,128)}, f32[1280]{0:T(1024)}, f32[1280]{0:T(1024)}, f32[1280,1280]{1,0:T(8,128)}, /*in...) custom-call(bf16[256,1280]{1,0:T(8,128)(2,1)} %get-tuple-element.24., ...), custom_call_target="tpu_custom_call" | custom-call | tf_op jit(solution)/shard_map/pallas_call | solution.py:995

commit v5 on v4

--- a/solution.py
+++ b/solution.py
@@ -451,6 +451,37 @@
             self.onward(part).wait_send()
 
 
+class GatherColumns:
+    def __init__(self, ring, rows, sems):
+        parts = rows.shape[1] // 256
+
+        def copy(block, device, which, part):
+            view = rows.at[block_rows(block), pl.ds(pl.multiple_of(part * 256, 256), 256)]
+            return pltpu.make_async_remote_copy(
+                src_ref=view,
+                dst_ref=view,
+                send_sem=sems.at[0, which * parts + part],
+                recv_sem=sems.at[1, which * parts + part],
+                device_id={"mp": device},
+                device_id_type=MESH,
+            )
+
+        self.parts = parts
+        self.near = lambda part: copy(ring.me, ring.core, 0, part)
+        self.across = lambda part: copy(ring.me, ring.chip, 1, part)
+        self.onward = lambda part: copy(ring.chip, ring.core, 2, part)
+
+    def forward(self, part):
+        self.across(part).wait_recv()
+        self.onward(part).start()
+
+    def sent(self):
+        for part in range(self.parts):
+            self.near(part).wait_send()
+            self.across(part).wait_send()
+            self.onward(part).wait_send()
+
+
 class Scatter:
     def __init__(self, ring, send_core, recv_core, send_chip, recv_chip, sems, parts=1):
         self.parts = parts
@@ -483,8 +514,7 @@
     return values * inverse, inverse
 
 
-def qkv_block(rows, weights, cos_ref, sin_ref, out, block):
-    at = block_rows(block)
+def qkv_block(rows, weights, cos_ref, sin_ref, out, at):
     turned = 2 * (weights.shape[0] // 3) // 256
     tiles = weights.shape[0] // 256
 
@@ -542,7 +572,7 @@
     w_up, w_down, w_qkv, w_out, rows_one, rows_g, rows_two, hidden, grad_up, branch, qkv, mixed, grad_mixed,
     cos_ref, sin_ref, bias_ref, resid, term_ref, key_sum, value_sum,
     send_core, recv_core, send_chip, recv_chip, gain_acc, gain_recv,
-    load_sem, one_sem, g_sem, two_sem, branch_sem, rs0_sem, rs_sem, rs2_sem, rs3_sem, gain_sem, free_sem, ready_sem,
+    load_sem, one_sem, g_sem, two_sem, branch_sem, rs0_sem, rs_sem, rs2_sem, rs3_sem, gain_sem, free_sem, ready_sem, down_sem,
 ):
     bf, f32 = jnp.bfloat16, jnp.float32
     ring = Ring4()
@@ -565,7 +595,7 @@
         load.start()
     normed, _ = norm_rows(x[...].astype(f32))
     rows_one[block_rows(ring.me), :] = (normed * gain_one[...]).astype(bf)
-    one, all_g = Gather(ring, rows_one, one_sem, 2), Gather(ring, rows_g, g_sem)
+    one, all_g = Gather(ring, rows_one, one_sem, 2), GatherColumns(ring, rows_g, g_sem)
     two, all_branch = Gather(ring, rows_two, two_sem, 2), Gather(ring, branch, branch_sem)
     ahead = Scatter(ring, send_core, recv_core, send_chip, recv_chip, rs0_sem, 2)
     first = Scatter(ring, send_core, recv_core, send_chip, recv_chip, rs_sem)
@@ -584,19 +614,33 @@
     loads[3].wait()
     w_out[...] = dot(spread, rows[pl.ds(3 * local, local), :]).astype(bf)
     rotary_into(seg[...], cos_ref, sin_ref)
-    qkv_block(rows_one, w_qkv, cos_ref, sin_ref, qkv, ring.me)
+    qkv_block(rows_one, w_qkv, cos_ref, sin_ref, qkv, block_rows(ring.me))
     one.near_in()
-    qkv_block(rows_one, w_qkv, cos_ref, sin_ref, qkv, ring.core)
+    qkv_block(rows_one, w_qkv, cos_ref, sin_ref, qkv, block_rows(ring.core))
     key_sum[...] = segment_columns(seg[...])
     masks_into(seg[...], key_sum, bias_ref)
     loads[4].wait()
-    one.forward()
-    one.across(0).wait_send()
-    one.across(1).wait_send()
-    all_g.start()
-    qkv_block(rows_one, w_qkv, cos_ref, sin_ref, qkv, ring.chip)
-    one.onward_in()
-    qkv_block(rows_one, w_qkv, cos_ref, sin_ref, qkv, ring.far)
+    for part in range(all_g.parts):
+        all_g.near(part).start()
+
+    def half_rows(block, part):
+        return pl.ds(pl.multiple_of(block * BLOCK_SEQ + part * half, half), half)
+
+    @pl.loop(0, 2)
+    def _(p):
+        one.across(p).wait_recv()
+        one.onward(p).start()
+
+        @pl.when(p == 1)
+        def _():
+            one.across(0).wait_send()
+            one.across(1).wait_send()
+            all_g.across(0).start()
+            all_g.across(1).start()
+
+        qkv_block(rows_one, w_qkv, cos_ref, sin_ref, qkv, half_rows(ring.chip, p))
+        one.onward(p).wait_recv()
+        qkv_block(rows_one, w_qkv, cos_ref, sin_ref, qkv, half_rows(ring.far, p))
 
     early, late = (0, 1), (2, 3)
 
@@ -609,8 +653,7 @@
         attend(qkv, mixed, bias_ref, heads, scale, early)
 
     def term(block, part):
-        at = pl.ds(pl.multiple_of(block * BLOCK_SEQ + part * half, half), half)
-        return dot(mixed[at, :], w_out[...])
+        return dot(mixed[half_rows(block, part), :], w_out[...])
 
     parts = [pl.ds(p * half, half) for p in range(2)]
     for p in range(2):
@@ -633,7 +676,8 @@
     for p in range(2):
         send_core[1, parts[p], :] = term(ring.core, p).astype(bf)
         ahead.core(p).start()
-    all_g.forward()
+    for part in range(2):
+        all_g.forward(part)
     for p in range(2):
         resid[parts[p], :] = x[parts[p], :].astype(f32) + term(ring.me, p)
     for p in range(2):
@@ -651,6 +695,7 @@
         ahead.chip(p).wait_send()
 
     base = 2 * units
+    turned_pairs = width // (2 * CHUNK)
 
     def put(pair):
         at = pl.ds(pl.multiple_of(pair * 2 * CHUNK, 2 * CHUNK), 2 * CHUNK)
@@ -660,35 +705,48 @@
         red.slot(index)
         pair = index - (STAGES - 1)
 
-        @pl.when(pair >= 4)
+        @pl.when(pair >= turned_pairs + 4)
         def _():
             put(pair - 4).wait()
 
-        @pl.when(pair >= 0)
+        @pl.when(pair >= turned_pairs)
         def _():
             put(pair).start()
 
     def tile(n):
         return pl.ds(pl.multiple_of(n * 256, 256), 256)
 
-    def up_tile(block, n):
-        u = dot(rows_two[block_rows(block), :], w_up[:, tile(n)])
-        tangent = jnp.tanh(GELU_C * (u + GELU_K * u * u * u))
-        hidden[block_rows(block), tile(n)] = (0.5 * u * (1.0 + tangent)).astype(bf)
-
-    def up_block(block):
+    def up_rows_of(at):
         @pl.loop(0, units // 256)
         def _(n):
-            up_tile(block, n)
+            u = dot(rows_two[at, :], w_up[:, tile(n)])
+            tangent = jnp.tanh(GELU_C * (u + GELU_K * u * u * u))
+            hidden[at, tile(n)] = (0.5 * u * (1.0 + tangent)).astype(bf)
 
     loads[5].wait()
-    up_block(ring.me)
+    up_rows_of(block_rows(ring.me))
     two.near_in()
-    up_block(ring.core)
-    all_g.near_in()
-    all_g.onward_in()
-    two.forward()
-    two.onward_in()
+    up_rows_of(block_rows(ring.core))
+    for part in range(all_g.parts):
+        all_g.near(part).wait_recv()
+    for part in range(2):
+        all_g.onward(part).wait_recv()
+
+    @pl.loop(0, 2)
+    def _(p):
+        two.across(p).wait_recv()
+        two.onward(p).start()
+
+        @pl.when(p == 1)
+        def _():
+            two.across(0).wait_send()
+            two.across(1).wait_send()
+            for part in range(2, all_g.parts):
+                all_g.across(part).start()
+
+        up_rows_of(half_rows(ring.chip, p))
+        two.onward(p).wait_recv()
+        up_rows_of(half_rows(ring.far, p))
 
     loads[6].wait()
 
@@ -735,25 +793,38 @@
         slope = 0.5 * (1.0 + tangent) + 0.5 * u * (1.0 - tangent * tangent) * GELU_C * (1.0 + 3.0 * GELU_K * u * u)
         grad_up[at, tile(n)] = (upstream * slope).astype(bf)
 
-    @pl.loop(0, units // 256)
+    @pl.loop(0, width // 256)
     def _(n):
-        for block in (ring.chip, ring.far):
-            up_tile(block, n)
-        rows[tile(n), :] = dot_tn(hidden[:, tile(n)], rows_g[...]).astype(bf)
+        @pl.when(n == 2)
+        def _():
+            all_g.onward(2).wait_recv()
+
+        @pl.when(n == 3)
+        def _():
+            all_g.onward(3).wait_recv()
+            all_g.onward(4).wait_recv()
+
+        rows[tile(n), :] = dot_tn(rows_g[:, tile(n)], hidden[...]).astype(bf)
         slot(n)
 
-        @pl.loop(0, 3)
+        @pl.when(n < 3)
+        def _():
+            all_g.forward(n + 2)
+
+        @pl.loop(0, 2)
         def _(k):
-            grad_tile(block_rows(order(k)), n)
+            grad_tile(block_rows(order(2 + k)), n)
+
+        @pl.when(n >= 3)
+        def _():
+            at = block_rows(order(n - 3))
+
+            @pl.loop(0, units // 256)
+            def _(m):
+                grad_tile(at, m)
 
     @pl.loop(0, 4)
     def _(k):
-        @pl.loop(0, 2)
-        def _(j):
-            @pl.when(2 * k + j < units // 256)
-            def _():
-                grad_tile(block_rows(order(3)), 2 * k + j)
-
         at = block_rows(order(k))
 
         @pl.loop(0, width // 256)
@@ -819,6 +890,13 @@
     @pl.loop(0, 4)
     def _(b):
         grad_mixed[block_rows(b), :] = dot_nt(branch[block_rows(b), :], w_out[...]).astype(bf)
+
+    def turn_down(n, target, at):
+        eye = jnp.where(
+            lax.broadcasted_iota(jnp.int32, (256, 256), 0) == lax.broadcasted_iota(jnp.int32, (256, 256), 1), 1.0, 0.0
+        ).astype(bf)
+        for m in range(width // 256):
+            target[at, pl.ds(m * 256, 256)] = dot_tn(rows[pl.ds(m * 256, 256), tile(n)], eye).astype(bf)
 
     @pl.loop(0, heads)
     def _(h):
@@ -846,6 +924,7 @@
         qkv[:, lanes[1]] = (turned * cos_ref[...] - pltpu.roll(turned, 64, 1) * sin_ref[...]).astype(bf)
         qkv[:, lanes[2]] = value_sum[...].astype(bf)
         slot(15 + 2 * h)
+        turn_down(h, grad_up, tile(h))
 
     @pl.loop(0, 3)
     def _(part):
@@ -854,6 +933,7 @@
             head_rows(qkv, lane, rows_one, base + (part + 1) * local + j * 2 * HEAD)
         slot(22 + part)
 
+    turn_down(4, hidden, pl.ds(0, 256))
     result_o[...] = (resid[...] + settle(second)).astype(bf)
     for device in (ring.core, ring.chip):
         pl.semaphore_signal(free_sem, inc=1, device_id={"mp": device}, device_id_type=MESH)
@@ -870,6 +950,12 @@
         hand_on(k, third, None)
         slot(25 + k)
 
+    downs = [
+        pltpu.make_async_copy(grad_up, sums_o.at[pl.ds(0, seq), :], down_sem.at[0]),
+        pltpu.make_async_copy(hidden.at[pl.ds(0, units - seq), :], sums_o.at[pl.ds(seq, units - seq), :], down_sem.at[1]),
+    ]
+    for copy in downs:
+        copy.start()
     slot(29)
     grad_one = settle(third)
     normed, inverse = norm_rows(x[...].astype(f32))
@@ -903,13 +989,16 @@
     gains_o[...] = gain_acc[4] + gain_recv[4]
     for pair in range(pairs - 4, pairs):
         put(pair).wait()
+    for copy in downs:
+        copy.wait()
     for step in range(5):
         exchange(step).wait_send()
-    for part in range(2):
-        one.near(part).wait_send()
-        one.onward(part).wait_send()
-    for gather in (all_g, two, all_branch):
-        gather.sent()
+    for gather in (one, two):
+        for part in range(2):
+            gather.near(part).wait_send()
+            gather.onward(part).wait_send()
+    all_g.sent()
+    all_branch.sent()
 
 
 def layer(x, g, seg, gain_one, gain_two, wq, wk, wv, wo, wup, wdown):
@@ -940,8 +1029,8 @@
             pltpu.VMEM((own, width), f32), pltpu.VMEM((own, width), f32), pltpu.VMEM((seq, HEAD_PAD), f32), pltpu.VMEM((seq, HEAD_PAD), f32),
             pltpu.VMEM((2, own, width), bf), pltpu.VMEM((2, own, width), bf), pltpu.VMEM((own, width), bf), pltpu.VMEM((own, width), bf),
             pltpu.VMEM((5, 8, width), f32), pltpu.VMEM((5, 8, width), f32),
-            sem((7,)), sem((2, 6)), sem((2, 3)), sem((2, 6)), sem((2, 3)), sem((2, 6)), sem((2, 3)), sem((2, 3)), sem((2, 3)), sem((2, 5)),
-            pltpu.SemaphoreType.REGULAR, pltpu.SemaphoreType.REGULAR,
+            sem((7,)), sem((2, 6)), sem((2, 3 * (width // 256))), sem((2, 6)), sem((2, 3)), sem((2, 6)), sem((2, 3)), sem((2, 3)), sem((2, 3)), sem((2, 5)),
+            pltpu.SemaphoreType.REGULAR, pltpu.SemaphoreType.REGULAR, sem((2,)),
         ],
         compiler_params=pltpu.CompilerParams(collective_id=0, has_side_effects=True, vmem_limit_bytes=67043328),
     )(x, g, seg, gain_one, gain_two, wq, wk, wv, wo, wup, wdown)

time: 276 us -> 280 us (1.014)
  Pallas kernels: 274 us -> 279 us
    pallas_call x1, Pallas kernels: 262 us -> 266 us  [layer(): pl.pallas_call(layer_kernel, out_shape=[jax.ShapeDtypeStruct(s, d) for s,...]
where the time goes in v5:
time: 280 us
  Pallas kernels  279 us (100%)
    pallas_call x1, Pallas kernels, layer(): pl.pallas_call(layer_kernel, out_shape=[jax.ShapeDtypeStruct(s, d) for s,...  266 us
    pallas_call x1, Pallas kernels, finish(): pl.pallas_call(finish_kernel, out_shape=[jax.ShapeDtypeStruct(s, d) for s...  12.7 us

profile of v5, /device:TPU:0, one launch (start us, length us, event | category | flops | bytes accessed | tf_op | source)
XLA Modules:
  0.0 279.7 jit_solution(15755981838362082635)
XLA Ops:
  0.6 266.2 %shard_map.186 = (bf16[256,1280]{1,0:T(8,128)(2,1)}, f32[256,1280]{1,0:T(8,128)}, f32[8,1280]{1,0:T(8,128)}, bf16[3840,1280]{1,0:T(8,128)(2,1)}) custom-call(bf16[256,1280]{1,0:T(8,128)(2,1)} %bitcast.13, bf16[256,1280]{1,0:T(8,128)(2,1)} %bitcast.14, s32[1,1024]{1,0:T(1,128)} %seg.1, f32[1280]{0:T(1024)} %gain_one.1, f32[1280]{0:T(1024)} %gain_two.1, ...), custom_call_target="tpu_custom_call" | custom-call | tf_op jit(solution)/shard_map/pallas_call | solution.py:1016
  266.9 12.7 %shard_map.187 = (bf16[256,1280]{1,0:T(8,128)(2,1)}, f32[256,1280]{1,0:T(8,128)}, f32[1280]{0:T(1024)}, f32[1280]{0:T(1024)}, f32[1280,1280]{1,0:T(8,128)}, /*in...) custom-call(bf16[256,1280]{1,0:T(8,128)(2,1)} %get-tuple-element.24., ...), custom_call_target="tpu_custom_call" | custom-call | tf_op jit(solution)/shard_map/pallas_call | solution.py:1084

commit v6 on v4

--- a/solution.py
+++ b/solution.py
@@ -538,7 +538,7 @@
 def layer_kernel(
     x, g, seg, gain_one, gain_two, wq, wk, wv, wo, wup, wdown,
     result_o, input_o, gains_o, sums_o,
-    rows, b0, b1, b2, b3, b4, b5, send_sem, recv_sem, save_sem,
+    result, input_grad, out_sem, rows, b0, b1, b2, b3, b4, b5, send_sem, recv_sem, save_sem,
     w_up, w_down, w_qkv, w_out, rows_one, rows_g, rows_two, hidden, grad_up, branch, qkv, mixed, grad_mixed,
     cos_ref, sin_ref, bias_ref, resid, term_ref, key_sum, value_sum,
     send_core, recv_core, send_chip, recv_chip, gain_acc, gain_recv,
@@ -742,17 +742,19 @@
         rows[tile(n), :] = dot_tn(hidden[:, tile(n)], rows_g[...]).astype(bf)
         slot(n)
 
-        @pl.loop(0, 3)
+        @pl.loop(0, 2)
         def _(k):
             grad_tile(block_rows(order(k)), n)
 
     @pl.loop(0, 4)
     def _(k):
-        @pl.loop(0, 2)
+        late = lax.rem(k, 2)
+
+        @pl.loop(0, 3)
         def _(j):
-            @pl.when(2 * k + j < units // 256)
+            @pl.when(3 * late + j < units // 256)
             def _():
-                grad_tile(block_rows(order(3)), 2 * k + j)
+                grad_tile(block_rows(order(2 + lax.div(k, 2))), 3 * late + j)
 
         at = block_rows(order(k))
 
@@ -776,7 +778,7 @@
     gain_acc[0] = jnp.zeros(gain_acc.shape[1:], f32)
     gain_acc[0, 1:2, :] = mlp_part
     mine = rows_g[block_rows(ring.me), :].astype(f32) + part
-    input_o[...] = mine
+    input_grad[...] = mine
     branch[block_rows(ring.me), :] = mine.astype(bf)
     all_branch.across().start()
     all_branch.near().start()
@@ -854,7 +856,7 @@
             head_rows(qkv, lane, rows_one, base + (part + 1) * local + j * 2 * HEAD)
         slot(22 + part)
 
-    result_o[...] = (resid[...] + settle(second)).astype(bf)
+    result[...] = (resid[...] + settle(second)).astype(bf)
     for device in (ring.core, ring.chip):
         pl.semaphore_signal(free_sem, inc=1, device_id={"mp": device}, device_id_type=MESH)
     pl.semaphore_wait(free_sem, 2)
@@ -874,7 +876,7 @@
     grad_one = settle(third)
     normed, inverse = norm_rows(x[...].astype(f32))
     scaled = grad_one * gain_one[...]
-    input_o[...] = input_o[...] + inverse * (scaled - normed * jnp.mean(scaled * normed, -1, keepdims=True))
+    input_grad[...] = input_grad[...] + inverse * (scaled - normed * jnp.mean(scaled * normed, -1, keepdims=True))
     gain_acc[0, 0:1, :] = jnp.sum(grad_one * normed, axis=0, keepdims=True)
 
     def exchange(step):
@@ -884,10 +886,16 @@
             device_id=names[step], device_id_type=MESH,
         )
 
+    leave = [pltpu.make_async_copy(result, result_o, out_sem.at[0]), pltpu.make_async_copy(input_grad, input_o, out_sem.at[1])]
     last = pairs + STAGES - 1
 
     @pl.loop(30, last)
     def _(index):
+        @pl.when(index == 31)
+        def _():
+            for copy in leave:
+                copy.start()
+
         for step in range(5):
 
             @pl.when(index == 30 + step)
@@ -903,6 +911,8 @@
     gains_o[...] = gain_acc[4] + gain_recv[4]
     for pair in range(pairs - 4, pairs):
         put(pair).wait()
+    for copy in leave:
+        copy.wait()
     for step in range(5):
         exchange(step).wait_send()
     for part in range(2):
@@ -928,8 +938,8 @@
         layer_kernel,
         out_shape=[jax.ShapeDtypeStruct(s, d) for s, d in shapes],
         in_specs=[vm, hbm, vm, vm, vm] + [hbm] * 6,
-        out_specs=[vm] * 3 + [hbm],
-        scratch_shapes=[pltpu.VMEM((total, width), bf)]
+        out_specs=[hbm, hbm, vm, hbm],
+        scratch_shapes=[pltpu.VMEM((own, width), bf), pltpu.VMEM((own, width), f32), sem((2,)), pltpu.VMEM((total, width), bf)]
         + reducer_scratch(width)
         + [
             sem((4,)),
@@ -948,9 +958,8 @@
 
 
 def finish_kernel(result, input_grad, gains, sums, result_o, input_o, one_o, two_o, down_o, up_o, out_o, q_o, k_o, v_o, inbox, outbox, side_one, side_two, in_sem, out_sem, side_sem):
-    step = out_o.shape[0]
-    targets = [(down_o, i * step) for i in range(down_o.shape[0] // step)] + [(up_o, i * step) for i in range(up_o.shape[0] // step)]
-    targets += [(t, 0) for t in (out_o, q_o, k_o, v_o)]
+    step = inbox.shape[1]
+    targets = [(t, i * step) for t in (down_o, up_o, out_o, q_o, k_o, v_o) for i in range(t.shape[0] // step)]
     count, depth = len(targets), inbox.shape[0]
     bring = [pltpu.make_async_copy(result, side_one, side_sem.at[0]), pltpu.make_async_copy(input_grad, side_two, side_sem.at[1])]
     take = [pltpu.make_async_copy(side_one, result_o, side_sem.at[2]), pltpu.make_async_copy(side_two, input_o, side_sem.at[3])]
@@ -997,7 +1006,7 @@
         out_shape=[jax.ShapeDtypeStruct(s, d) for s, d in shapes],
         in_specs=[hbm, hbm, vm, hbm],
         out_specs=[hbm, hbm, vm, vm] + [hbm] * 6,
-        scratch_shapes=[pltpu.VMEM((3, local, width), bf), pltpu.VMEM((3, local, width), f32), pltpu.VMEM((own, width), bf), pltpu.VMEM((own, width), f32), sem((3,)), sem((3,)), sem((4,))],
+        scratch_shapes=[pltpu.VMEM((6, local // 2, width), bf), pltpu.VMEM((6, local // 2, width), f32), pltpu.VMEM((own, width), bf), pltpu.VMEM((own, width), f32), sem((6,)), sem((6,)), sem((4,))],
         compiler_params=pltpu.CompilerParams(vmem_limit_bytes=67043328),
     )(result, input_grad, gains, sums)
 

time: 276 us -> 277 us (level)
  no operation moved by 1% of the time
where the time goes in v6:
time: 277 us
  Pallas kernels  276 us (100%)
    pallas_call x1, Pallas kernels, layer(): pl.pallas_call(layer_kernel, out_shape=[jax.ShapeDtypeStruct(s, d) for s,...  263 us
    pallas_call x1, Pallas kernels, finish(): pl.pallas_call(finish_kernel, out_shape=[jax.ShapeDtypeStruct(s, d) for s...  12.9 us

profile of v6, /device:TPU:0, one launch (start us, length us, event | category | flops | bytes accessed | tf_op | source)
XLA Modules:
  0.0 276.5 jit_solution(16967709494727918135)
XLA Ops:
  0.6 262.8 %shard_map.186 = (bf16[256,1280]{1,0:T(8,128)(2,1)}, f32[256,1280]{1,0:T(8,128)}, f32[8,1280]{1,0:T(8,128)}, bf16[3840,1280]{1,0:T(8,128)(2,1)}) custom-call(bf16[256,1280]{1,0:T(8,128)(2,1)} %bitcast.13, bf16[256,1280]{1,0:T(8,128)(2,1)} %bitcast.14, s32[1,1024]{1,0:T(1,128)} %seg.1, f32[1280]{0:T(1024)} %gain_one.1, f32[1280]{0:T(1024)} %gain_two.1, ...), custom_call_target="tpu_custom_call" | custom-call | tf_op jit(solution)/shard_map/pallas_call | solution.py:937
  263.4 12.9 %shard_map.187 = (bf16[256,1280]{1,0:T(8,128)(2,1)}, f32[256,1280]{1,0:T(8,128)}, f32[1280]{0:T(1024)}, f32[1280]{0:T(1024)}, f32[1280,1280]{1,0:T(8,128)}, /*in...) custom-call(bf16[256,1280]{1,0:T(8,128)(2,1)} %get-tuple-element.24., ...), custom_call_target="tpu_custom_call" | custom-call | tf_op jit(solution)/shard_map/pallas_call | solution.py:1004

commit v7 on v4

--- a/solution.py
+++ b/solution.py
@@ -746,6 +746,9 @@
         def _(k):
             grad_tile(block_rows(order(k)), n)
 
+    def up_rows(i):
+        rows[pl.ds(pl.multiple_of(units + i * 256, 256), 256), :] = dot_tn(rows_two[:, tile(i)], grad_up[...]).astype(bf)
+
     @pl.loop(0, 4)
     def _(k):
         @pl.loop(0, 2)
@@ -761,12 +764,17 @@
             term_ref[:, tile(n)] = dot_nt(grad_up[at, :], w_up[tile(n), :])
 
         hand_on(k, first, None)
+
+        @pl.when(k == 3)
+        def _():
+            up_rows(0)
+
         slot(5 + k)
 
-    def up_rows(i):
-        rows[pl.ds(pl.multiple_of(units + i * 256, 256), 256), :] = dot_tn(rows_two[:, tile(i)], grad_up[...]).astype(bf)
-
-    up_rows(0)
+    @pl.loop(1, 3)
+    def _(i):
+        up_rows(i)
+
     slot(9)
     grad_two = settle(first)
     normed, inverse = norm_rows(resid[...])
@@ -788,21 +796,27 @@
         halves = [value[at : at + HEAD // 2, :] for at in (0, 64, 128, 192)]
         rows[pl.ds(pl.multiple_of(row, 16), 2 * HEAD), :] = jnp.concatenate(halves, axis=0).astype(bf)
 
-    @pl.loop(1, units // 256)
+    @pl.loop(1, 5)
     def _(i):
-        up_rows(i)
+        @pl.when(i <= 2)
+        def _():
+            up_rows(2 + i)
 
         @pl.when(i == 1)
         def _():
             pl.semaphore_wait(ready_sem, 2)
 
-        at = block_rows(order(i - 1))
-
-        @pl.loop(0, width // 256)
-        def _(n):
-            term_ref[:, tile(n)] = dot(hidden[at, :], w_down[:, tile(n)])
-
-        hand_on(i - 1, second, None)
+        @pl.loop(0, 2)
+        def _(j):
+            @pl.when(((j == 0) & (i <= 3)) | (i == 3))
+            def _():
+                at = block_rows(order(i - 1 + j))
+
+                @pl.loop(0, width // 256)
+                def _(n):
+                    term_ref[:, tile(n)] = dot(hidden[at, :], w_down[:, tile(n)])
+
+                hand_on(i - 1 + j, second, None)
 
         @pl.when(i == 4)
         def _():
@@ -814,18 +828,18 @@
             def _(j):
                 head_rows(mixed, tile(j), branch, base + j * 2 * HEAD)
 
+            @pl.loop(0, 4)
+            def _(b):
+                grad_mixed[block_rows(b), :] = dot_nt(branch[block_rows(b), :], w_out[...]).astype(bf)
+
         slot(9 + i)
-
-    @pl.loop(0, 4)
-    def _(b):
-        grad_mixed[block_rows(b), :] = dot_nt(branch[block_rows(b), :], w_out[...]).astype(bf)
 
     @pl.loop(0, heads)
     def _(h):
         lanes = [pl.ds(pl.multiple_of(n * padded + h * HEAD_PAD, HEAD_PAD), HEAD_PAD) for n in range(3)]
         key_sum[...] = jnp.zeros_like(key_sum)
         value_sum[...] = jnp.zeros_like(value_sum)
-        for i in range(seq // BLOCK_SEQ):
+        for step, i in enumerate((1, 2, 0, 3)):
             low, high = max(0, i * BLOCK_SEQ - SPAN), (i + 1) * BLOCK_SEQ
             at, keys = pl.ds(i * BLOCK_SEQ, BLOCK_SEQ), pl.ds(low, high - low)
             query, upstream = qkv[at, lanes[0]], grad_mixed[at, lanes[0]]
@@ -840,7 +854,7 @@
             key_sum[keys, :] += dot_tn(grad_scores, query)
             turned = dot(grad_scores, qkv[keys, lanes[1]]) * scale
             qkv[at, lanes[0]] = (turned * cos_ref[at, :] - pltpu.roll(turned, 64, 1) * sin_ref[at, :]).astype(bf)
-            if i == 1:
+            if step == 1:
                 slot(14 + 2 * h)
         turned = key_sum[...] * scale
         qkv[:, lanes[1]] = (turned * cos_ref[...] - pltpu.roll(turned, 64, 1) * sin_ref[...]).astype(bf)

time: 276 us -> 277 us (level)
  no operation moved by 1% of the time
where the time goes in v7:
time: 277 us
  Pallas kernels  276 us (100%)
    pallas_call x1, Pallas kernels, layer(): pl.pallas_call(layer_kernel, out_shape=[jax.ShapeDtypeStruct(s, d) for s,...  263 us
    pallas_call x1, Pallas kernels, finish(): pl.pallas_call(finish_kernel, out_shape=[jax.ShapeDtypeStruct(s, d) for s...  12.7 us

profile of v7, /device:TPU:0, one launch (start us, length us, event | category | flops | bytes accessed | tf_op | source)
XLA Modules:
  0.0 276.7 jit_solution(6500027905958535006)
XLA Ops:
  0.6 263.2 %shard_map.186 = (bf16[256,1280]{1,0:T(8,128)(2,1)}, f32[256,1280]{1,0:T(8,128)}, f32[8,1280]{1,0:T(8,128)}, bf16[3840,1280]{1,0:T(8,128)(2,1)}) custom-call(bf16[256,1280]{1,0:T(8,128)(2,1)} %bitcast.13, bf16[256,1280]{1,0:T(8,128)(2,1)} %bitcast.14, s32[1,1024]{1,0:T(1,128)} %seg.1, f32[1280]{0:T(1024)} %gain_one.1, f32[1280]{0:T(1024)} %gain_two.1, ...), custom_call_target="tpu_custom_call" | custom-call | tf_op jit(solution)/shard_map/pallas_call | solution.py:941
  263.9 12.7 %shard_map.187 = (bf16[256,1280]{1,0:T(8,128)(2,1)}, f32[256,1280]{1,0:T(8,128)}, f32[1280]{0:T(1024)}, f32[1280]{0:T(1024)}, f32[1280,1280]{1,0:T(8,128)}, /*in...) custom-call(bf16[256,1280]{1,0:T(8,128)(2,1)} %get-tuple-element.24., ...), custom_call_target="tpu_custom_call" | custom-call | tf_op jit(solution)/shard_map/pallas_call | solution.py:1009

commit v8 on v4

--- a/solution.py
+++ b/solution.py
@@ -519,8 +519,9 @@
         bias_ref[pl.ds(i * BLOCK_SEQ, BLOCK_SEQ), pl.ds(0, high - low)] = jnp.where((query >= key) & same, 0.0, MASKED).astype(bias_ref.dtype)
 
 
-def attend(qkv, out, bias_ref, heads, scale, blocks):
+def attend(qkv, out, bias_ref, stats, heads, scale, blocks):
     width = heads * HEAD_PAD
+    lane = lax.broadcasted_iota(jnp.int32, (BLOCK_SEQ, 128), 1)
 
     @pl.loop(0, heads)
     def _(h):
@@ -531,7 +532,9 @@
             scores = dot_nt(qkv[rows, lanes[0]], qkv[keys, lanes[1]]) + bias_ref[rows, pl.ds(0, high - low)]
             top = jnp.max(scores, -1, keepdims=True)
             expo = jnp.exp((scores - top) * scale)
-            probs = expo * (1.0 / jnp.sum(expo, -1, keepdims=True))
+            total = jnp.sum(expo, -1, keepdims=True)
+            probs = expo * (1.0 / total)
+            stats[rows, :] = jnp.where(lane == h, top * scale + jnp.log(total), stats[rows, :])
             out[rows, lanes[0]] = dot(probs.astype(jnp.bfloat16), qkv[keys, lanes[2]]).astype(jnp.bfloat16)
 
 
@@ -542,7 +545,7 @@
     w_up, w_down, w_qkv, w_out, rows_one, rows_g, rows_two, hidden, grad_up, branch, qkv, mixed, grad_mixed,
     cos_ref, sin_ref, bias_ref, resid, term_ref, key_sum, value_sum,
     send_core, recv_core, send_chip, recv_chip, gain_acc, gain_recv,
-    load_sem, one_sem, g_sem, two_sem, branch_sem, rs0_sem, rs_sem, rs2_sem, rs3_sem, gain_sem, free_sem, ready_sem,
+    load_sem, one_sem, g_sem, two_sem, branch_sem, rs0_sem, rs_sem, rs2_sem, rs3_sem, gain_sem, free_sem, ready_sem, stats,
 ):
     bf, f32 = jnp.bfloat16, jnp.float32
     ring = Ring4()
@@ -598,15 +601,16 @@
     one.onward_in()
     qkv_block(rows_one, w_qkv, cos_ref, sin_ref, qkv, ring.far)
 
+    stats[...] = jnp.zeros_like(stats)
     early, late = (0, 1), (2, 3)
 
     @pl.when(chip == 0)
     def _():
-        attend(qkv, mixed, bias_ref, heads, scale, late)
+        attend(qkv, mixed, bias_ref, stats, heads, scale, late)
 
     @pl.when(chip == 1)
     def _():
-        attend(qkv, mixed, bias_ref, heads, scale, early)
+        attend(qkv, mixed, bias_ref, stats, heads, scale, early)
 
     def term(block, part):
         at = pl.ds(pl.multiple_of(block * BLOCK_SEQ + part * half, half), half)
@@ -624,11 +628,11 @@
 
     @pl.when(chip == 0)
     def _():
-        attend(qkv, mixed, bias_ref, heads, scale, early)
+        attend(qkv, mixed, bias_ref, stats, heads, scale, early)
 
     @pl.when(chip == 1)
     def _():
-        attend(qkv, mixed, bias_ref, heads, scale, late)
+        attend(qkv, mixed, bias_ref, stats, heads, scale, late)
 
     for p in range(2):
         send_core[1, parts[p], :] = term(ring.core, p).astype(bf)
@@ -671,24 +675,32 @@
     def tile(n):
         return pl.ds(pl.multiple_of(n * 256, 256), 256)
 
-    def up_tile(block, n):
-        u = dot(rows_two[block_rows(block), :], w_up[:, tile(n)])
+    def half_rows(block, part):
+        return pl.ds(pl.multiple_of(block * BLOCK_SEQ + part * half, half), half)
+
+    def up_tile(at, n):
+        u = dot(rows_two[at, :], w_up[:, tile(n)])
         tangent = jnp.tanh(GELU_C * (u + GELU_K * u * u * u))
-        hidden[block_rows(block), tile(n)] = (0.5 * u * (1.0 + tangent)).astype(bf)
-
-    def up_block(block):
+        hidden[at, tile(n)] = (0.5 * u * (1.0 + tangent)).astype(bf)
+
+    def up_rows_of(at):
         @pl.loop(0, units // 256)
         def _(n):
-            up_tile(block, n)
+            up_tile(at, n)
 
     loads[5].wait()
-    up_block(ring.me)
+    up_rows_of(block_rows(ring.me))
     two.near_in()
-    up_block(ring.core)
+    up_rows_of(block_rows(ring.core))
     all_g.near_in()
     all_g.onward_in()
-    two.forward()
-    two.onward_in()
+    two.across(0).wait_recv()
+    two.onward(0).start()
+    up_rows_of(half_rows(ring.chip, 0))
+    two.onward(0).wait_recv()
+    up_rows_of(half_rows(ring.far, 0))
+    two.across(1).wait_recv()
+    two.onward(1).start()
 
     loads[6].wait()
 
@@ -737,8 +749,13 @@
 
     @pl.loop(0, units // 256)
     def _(n):
-        for block in (ring.chip, ring.far):
-            up_tile(block, n)
+        up_tile(half_rows(ring.chip, 1), n)
+
+        @pl.when(n == 0)
+        def _():
+            two.onward(1).wait_recv()
+
+        up_tile(half_rows(ring.far, 1), n)
         rows[tile(n), :] = dot_tn(hidden[:, tile(n)], rows_g[...]).astype(bf)
         slot(n)
 
@@ -820,6 +837,8 @@
     def _(b):
         grad_mixed[block_rows(b), :] = dot_nt(branch[block_rows(b), :], w_out[...]).astype(bf)
 
+    lane = lax.broadcasted_iota(jnp.int32, (BLOCK_SEQ, 128), 1)
+
     @pl.loop(0, heads)
     def _(h):
         lanes = [pl.ds(pl.multiple_of(n * padded + h * HEAD_PAD, HEAD_PAD), HEAD_PAD) for n in range(3)]
@@ -830,9 +849,8 @@
             at, keys = pl.ds(i * BLOCK_SEQ, BLOCK_SEQ), pl.ds(low, high - low)
             query, upstream = qkv[at, lanes[0]], grad_mixed[at, lanes[0]]
             scores = dot_nt(query, qkv[keys, lanes[1]]) + bias_ref[at, pl.ds(0, high - low)]
-            top = jnp.max(scores, -1, keepdims=True)
-            expo = jnp.exp((scores - top) * scale)
-            probs = expo * (1.0 / jnp.sum(expo, -1, keepdims=True))
+            level = jnp.sum(jnp.where(lane == h, stats[at, :], 0.0), -1, keepdims=True)
+            probs = jnp.exp(scores * scale - level)
             grad_probs = dot_nt(upstream, qkv[keys, lanes[2]])
             inner = jnp.sum(probs * grad_probs, -1, keepdims=True)
             grad_scores = (probs * (grad_probs - inner)).astype(bf)
@@ -941,7 +959,7 @@
             pltpu.VMEM((2, own, width), bf), pltpu.VMEM((2, own, width), bf), pltpu.VMEM((own, width), bf), pltpu.VMEM((own, width), bf),
             pltpu.VMEM((5, 8, width), f32), pltpu.VMEM((5, 8, width), f32),
             sem((7,)), sem((2, 6)), sem((2, 3)), sem((2, 6)), sem((2, 3)), sem((2, 6)), sem((2, 3)), sem((2, 3)), sem((2, 3)), sem((2, 5)),
-            pltpu.SemaphoreType.REGULAR, pltpu.SemaphoreType.REGULAR,
+            pltpu.SemaphoreType.REGULAR, pltpu.SemaphoreType.REGULAR, pltpu.VMEM((seq, 128), f32),
         ],
         compiler_params=pltpu.CompilerParams(collective_id=0, has_side_effects=True, vmem_limit_bytes=67043328),
     )(x, g, seg, gain_one, gain_two, wq, wk, wv, wo, wup, wdown)

time: 276 us -> 274 us (level)
  no operation moved by 1% of the time
where the time goes in v8:
time: 274 us
  Pallas kernels  273 us (100%)
    pallas_call x1, Pallas kernels, layer(): pl.pallas_call(layer_kernel, out_shape=[jax.ShapeDtypeStruct(s, d) for s,...  260 us
    pallas_call x1, Pallas kernels, finish(): pl.pallas_call(finish_kernel, out_shape=[jax.ShapeDtypeStruct(s, d) for s...  12.7 us

profile of v8, /device:TPU:0, one launch (start us, length us, event | category | flops | bytes accessed | tf_op | source)
XLA Modules:
  0.0 274.0 jit_solution(18445577110488431779)
XLA Ops:
  0.6 260.5 %shard_map.186 = (bf16[256,1280]{1,0:T(8,128)(2,1)}, f32[256,1280]{1,0:T(8,128)}, f32[8,1280]{1,0:T(8,128)}, bf16[3840,1280]{1,0:T(8,128)(2,1)}) custom-call(bf16[256,1280]{1,0:T(8,128)(2,1)} %bitcast.13, bf16[256,1280]{1,0:T(8,128)(2,1)} %bitcast.14, s32[1,1024]{1,0:T(1,128)} %seg.1, f32[1280]{0:T(1024)} %gain_one.1, f32[1280]{0:T(1024)} %gain_two.1, ...), custom_call_target="tpu_custom_call" | custom-call | tf_op jit(solution)/shard_map/pallas_call | solution.py:945
  261.1 12.7 %shard_map.187 = (bf16[256,1280]{1,0:T(8,128)(2,1)}, f32[256,1280]{1,0:T(8,128)}, f32[1280]{0:T(1024)}, f32[1280]{0:T(1024)}, f32[1280,1280]{1,0:T(8,128)}, /*in...) custom-call(bf16[256,1280]{1,0:T(8,128)(2,1)} %get-tuple-element.24., ...), custom_call_target="tpu_custom_call" | custom-call | tf_op jit(solution)/shard_map/pallas_call | solution.py:1013

commit v9 on v8

--- a/solution.py
+++ b/solution.py
@@ -533,9 +533,8 @@
             top = jnp.max(scores, -1, keepdims=True)
             expo = jnp.exp((scores - top) * scale)
             total = jnp.sum(expo, -1, keepdims=True)
-            probs = expo * (1.0 / total)
             stats[rows, :] = jnp.where(lane == h, top * scale + jnp.log(total), stats[rows, :])
-            out[rows, lanes[0]] = dot(probs.astype(jnp.bfloat16), qkv[keys, lanes[2]]).astype(jnp.bfloat16)
+            out[rows, lanes[0]] = (dot(expo.astype(jnp.bfloat16), qkv[keys, lanes[2]]) * (1.0 / total)).astype(jnp.bfloat16)
 
 
 def layer_kernel(
@@ -586,17 +585,17 @@
         w_qkv[pl.ds(i * padded, padded), :] = dot(spread, rows[pl.ds(i * local, local), :]).astype(bf)
     loads[3].wait()
     w_out[...] = dot(spread, rows[pl.ds(3 * local, local), :]).astype(bf)
+    loads[4].wait()
+    all_g.start()
     rotary_into(seg[...], cos_ref, sin_ref)
     qkv_block(rows_one, w_qkv, cos_ref, sin_ref, qkv, ring.me)
     one.near_in()
     qkv_block(rows_one, w_qkv, cos_ref, sin_ref, qkv, ring.core)
     key_sum[...] = segment_columns(seg[...])
     masks_into(seg[...], key_sum, bias_ref)
-    loads[4].wait()
     one.forward()
     one.across(0).wait_send()
     one.across(1).wait_send()
-    all_g.start()
     qkv_block(rows_one, w_qkv, cos_ref, sin_ref, qkv, ring.chip)
     one.onward_in()
     qkv_block(rows_one, w_qkv, cos_ref, sin_ref, qkv, ring.far)
@@ -902,17 +901,17 @@
             device_id=names[step], device_id_type=MESH,
         )
 
+    exchange(0).start()
     last = pairs + STAGES - 1
 
     @pl.loop(30, last)
     def _(index):
-        for step in range(5):
-
-            @pl.when(index == 30 + step)
+        for step in range(1, 5):
+
+            @pl.when(index == 29 + step)
             def _():
-                if step:
-                    exchange(step - 1).wait_recv()
-                    gain_acc[step] = gain_acc[step - 1] + gain_recv[step - 1]
+                exchange(step - 1).wait_recv()
+                gain_acc[step] = gain_acc[step - 1] + gain_recv[step - 1]
                 exchange(step).start()
 
         slot(index)

time: 274 us -> 274 us (level)
  no operation moved by 1% of the time
where the time goes in v9:
time: 274 us
  Pallas kernels  273 us (100%)
    pallas_call x1, Pallas kernels, layer(): pl.pallas_call(layer_kernel, out_shape=[jax.ShapeDtypeStruct(s, d) for s,...  260 us
    pallas_call x1, Pallas kernels, finish(): pl.pallas_call(finish_kernel, out_shape=[jax.ShapeDtypeStruct(s, d) for s...  12.7 us

profile of v9, /device:TPU:0, one launch (start us, length us, event | category | flops | bytes accessed | tf_op | source)
XLA Modules:
  0.0 273.9 jit_solution(13961544287697439350)
XLA Ops:
  0.6 260.4 %shard_map.186 = (bf16[256,1280]{1,0:T(8,128)(2,1)}, f32[256,1280]{1,0:T(8,128)}, f32[8,1280]{1,0:T(8,128)}, bf16[3840,1280]{1,0:T(8,128)(2,1)}) custom-call(bf16[256,1280]{1,0:T(8,128)(2,1)} %bitcast.13, bf16[256,1280]{1,0:T(8,128)(2,1)} %bitcast.14, s32[1,1024]{1,0:T(1,128)} %seg.1, f32[1280]{0:T(1024)} %gain_one.1, f32[1280]{0:T(1024)} %gain_two.1, ...), custom_call_target="tpu_custom_call" | custom-call | tf_op jit(solution)/shard_map/pallas_call | solution.py:944
  261.0 12.7 %shard_map.187 = (bf16[256,1280]{1,0:T(8,128)(2,1)}, f32[256,1280]{1,0:T(8,128)}, f32[1280]{0:T(1024)}, f32[1280]{0:T(1024)}, f32[1280,1280]{1,0:T(8,128)}, /*in...) custom-call(bf16[256,1280]{1,0:T(8,128)(2,1)} %get-tuple-element.24., ...), custom_call_target="tpu_custom_call" | custom-call | tf_op jit(solution)/shard_map/pallas_call | solution.py:1012

commit v10 on v9

--- a/solution.py
+++ b/solution.py
@@ -483,8 +483,7 @@
     return values * inverse, inverse
 
 
-def qkv_block(rows, weights, cos_ref, sin_ref, out, block):
-    at = block_rows(block)
+def qkv_block(rows, weights, cos_ref, sin_ref, out, at):
     turned = 2 * (weights.shape[0] // 3) // 256
     tiles = weights.shape[0] // 256
 
@@ -588,17 +587,24 @@
     loads[4].wait()
     all_g.start()
     rotary_into(seg[...], cos_ref, sin_ref)
-    qkv_block(rows_one, w_qkv, cos_ref, sin_ref, qkv, ring.me)
+    qkv_block(rows_one, w_qkv, cos_ref, sin_ref, qkv, block_rows(ring.me))
     one.near_in()
-    qkv_block(rows_one, w_qkv, cos_ref, sin_ref, qkv, ring.core)
+    qkv_block(rows_one, w_qkv, cos_ref, sin_ref, qkv, block_rows(ring.core))
     key_sum[...] = segment_columns(seg[...])
     masks_into(seg[...], key_sum, bias_ref)
-    one.forward()
+    def half_rows(block, part):
+        return pl.ds(pl.multiple_of(block * BLOCK_SEQ + part * half, half), half)
+
+    @pl.loop(0, 2)
+    def _(p):
+        one.across(p).wait_recv()
+        one.onward(p).start()
+        qkv_block(rows_one, w_qkv, cos_ref, sin_ref, qkv, half_rows(ring.chip, p))
+        one.onward(p).wait_recv()
+        qkv_block(rows_one, w_qkv, cos_ref, sin_ref, qkv, half_rows(ring.far, p))
+
     one.across(0).wait_send()
     one.across(1).wait_send()
-    qkv_block(rows_one, w_qkv, cos_ref, sin_ref, qkv, ring.chip)
-    one.onward_in()
-    qkv_block(rows_one, w_qkv, cos_ref, sin_ref, qkv, ring.far)
 
     stats[...] = jnp.zeros_like(stats)
     early, late = (0, 1), (2, 3)
@@ -673,9 +679,6 @@
 
     def tile(n):
         return pl.ds(pl.multiple_of(n * 256, 256), 256)
-
-    def half_rows(block, part):
-        return pl.ds(pl.multiple_of(block * BLOCK_SEQ + part * half, half), half)
 
     def up_tile(at, n):
         u = dot(rows_two[at, :], w_up[:, tile(n)])

time: 274 us -> 274 us (level)
  no operation moved by 1% of the time
where the time goes in v10:
time: 274 us
  Pallas kernels  273 us (100%)
    pallas_call x1, Pallas kernels, layer(): pl.pallas_call(layer_kernel, out_shape=[jax.ShapeDtypeStruct(s, d) for s,...  260 us
    pallas_call x1, Pallas kernels, finish(): pl.pallas_call(finish_kernel, out_shape=[jax.ShapeDtypeStruct(s, d) for s...  12.7 us

profile of v10, /device:TPU:0, one launch (start us, length us, event | category | flops | bytes accessed | tf_op | source)
XLA Modules:
  0.0 273.6 jit_solution(5732285866524120079)
XLA Ops:
  0.6 260.1 %shard_map.186 = (bf16[256,1280]{1,0:T(8,128)(2,1)}, f32[256,1280]{1,0:T(8,128)}, f32[8,1280]{1,0:T(8,128)}, bf16[3840,1280]{1,0:T(8,128)(2,1)}) custom-call(bf16[256,1280]{1,0:T(8,128)(2,1)} %bitcast.13, bf16[256,1280]{1,0:T(8,128)(2,1)} %bitcast.14, s32[1,1024]{1,0:T(1,128)} %seg.1, f32[1280]{0:T(1024)} %gain_one.1, f32[1280]{0:T(1024)} %gain_two.1, ...), custom_call_target="tpu_custom_call" | custom-call | tf_op jit(solution)/shard_map/pallas_call | solution.py:947
  260.7 12.7 %shard_map.187 = (bf16[256,1280]{1,0:T(8,128)(2,1)}, f32[256,1280]{1,0:T(8,128)}, f32[1280]{0:T(1024)}, f32[1280]{0:T(1024)}, f32[1280,1280]{1,0:T(8,128)}, /*in...) custom-call(bf16[256,1280]{1,0:T(8,128)(2,1)} %get-tuple-element.24., ...), custom_call_target="tpu_custom_call" | custom-call | tf_op jit(solution)/shard_map/pallas_call | solution.py:1015
